TPU v7x, 256 devices: a whole 4x4x8 slice. The times are simulated.
256 devices in a mesh: gx: 16 (over z, x_lo), gy: 16 (over y, x_hi, core).
Axes of the slice: x: 4 (x_hi: 2, x_lo: 2; x = x_hi * 2 + x_lo), y: 4, z: 8, core: 2. Of those that a mesh axis runs over, the one named last changes fastest.
Arguments:
- gradient: float32 [2048, 512], P('gx', 'gy'), may hold values from -6 to 6
- stat_old: float32 [2048, 2048], P('gx', 'gy'), may hold values from -1.001 to 1.001, as said below
Outputs:
- statistic: float32 [2048, 2048], P('gx', 'gy')
- inverse_root: float32 [2048, 2048], P('gx', 'gy')
Inputs may be any that keep to these rules, and one draw needn't show every extreme that they name: stat_old is symmetric positive semidefinite with unit diagonal, the Gram matrix of 2048 unit-length rows of 512 entries.
All inputs are finite; a program needn't handle non-finite values.
Results may differ from a plain program's by a relative error of at most 0.0003.
Values sent between devices are 32-bit elements.
No kernel may reach another device: no remote copies, remote signals or barrier semaphores. Data moves between devices by JAX's collectives and lax.ppermute only.
A program may use at most 64 MiB of HBM per device.

v0:
```python
import jax
import jax.numpy as jnp
from jax import lax
from jax.sharding import Mesh
from jax.sharding import PartitionSpec as P


Z, XL, Y, XH, CORE = "gx_0", "gx_1", "gy_0", "gy_1", "gy_2"
GX = (Z, XL)
GY = (Y, XH, CORE)


def matmul(leading, trailing):
    return jnp.dot(
        leading, trailing, preferred_element_type=jnp.float32, precision=lax.Precision.HIGHEST
    )


def rotate(array, axis, shift):
    size = lax.axis_size(axis)
    return lax.ppermute(array, axis, [(s, (s + shift) % size) for s in range(size)])


def swap(array, axis):
    return lax.ppermute(array, axis, [(0, 1), (1, 0)])


def turn(array):
    return lax.ppermute(array, (XL, CORE), [(0, 0), (1, 2), (2, 1), (3, 3)])


def ordered(mine, other, index):
    first = jnp.where(index == 0, mine, other)
    second = jnp.where(index == 0, other, mine)
    return first, second


def row_panel(block):
    copies = jnp.broadcast_to(block[None], (16,) + block.shape)
    return lax.all_to_all(copies, (Y, XH, XL), 0, 0, tiled=True)


def column_panel(block):
    place = lax.axis_index(Z)
    found = {0: block}
    for shift in (2, -2, 1, -1):
        found[shift] = rotate(block, Z, shift)
    found[3] = rotate(found[2], Z, 1)
    found[-3] = rotate(found[-2], Z, -1)
    found[4] = rotate(found[2], Z, 2)
    mine = jnp.zeros((8,) + block.shape, block.dtype)
    for shift, piece in found.items():
        mine = lax.dynamic_update_slice(mine, piece[None], ((place - shift) % 8, 0, 0))
    first, second = ordered(mine, swap(mine, CORE), lax.axis_index(CORE))
    return jnp.stack((first, second), axis=1).reshape((16,) + block.shape)


def contract(rows, columns):
    side = rows.shape[1]
    return matmul(rows.transpose(1, 0, 2).reshape(side, -1), columns.reshape(-1, side))


def gradient_panels(gradient):
    piece = gradient.T
    copies = jnp.broadcast_to(piece[None], (8,) + piece.shape)
    along_z = lax.all_to_all(copies, Z, 0, 0, tiled=True)
    own = jnp.stack(ordered(piece, swap(piece, XL), lax.axis_index(XL)))
    for_rows = jnp.tile(own, (8, 1, 1))
    for_columns = jnp.repeat(along_z, 2, axis=0)
    parts = lax.all_to_all(jnp.stack((for_rows, for_columns), axis=1), GY, 0, 0, tiled=True)
    width = piece.shape[1]
    return parts[:, 0].reshape(-1, width), parts[:, 1].reshape(-1, width)


def local(gradient, stat_old):
    side = stat_old.shape[0]
    total = side * 16
    row_block = 2 * lax.axis_index(Z) + lax.axis_index(CORE)
    column_block = 4 * lax.axis_index(Y) + 2 * lax.axis_index(XH) + lax.axis_index(XL)
    eye = jnp.eye(side, dtype=jnp.float32)
    numbers = jnp.arange(16)[:, None, None]

    rows_of, columns_of = gradient_panels(gradient)
    outer = matmul(rows_of.T, columns_of) / rows_of.shape[0]
    stat = 0.9 * turn(stat_old) + outer

    stat_row = row_panel(stat)
    stat_column = column_panel(stat)
    statistic = turn(stat)
    square = contract(stat_row, stat_column)
    row_norm = jnp.sum(stat_row * stat_row)

    carried = jnp.concatenate((square, jnp.full((8, side), row_norm)), axis=0)
    square_row = row_panel(square)
    square_column = column_panel(carried)
    squares = jnp.sum(square_column[:, side, 0])
    divisor = 2.0 * jnp.sqrt(squares / total)
    inverse = 1.0 / divisor
    w_row = (square_row * inverse - 4.5 * stat_row) * inverse + jnp.where(
        numbers == row_block, 3.375, 0.0
    ) * eye
    w_column = (square_column[:, :side] * inverse - 4.5 * stat_column) * inverse + jnp.where(
        numbers == column_block, 3.375, 0.0
    ) * eye
    result = 0.0625 * contract(w_row, w_column) - (0.5390625 * inverse) * stat
    result = result + jnp.where(row_block == column_block, 1.5380859375, 0.0) * eye
    return (statistic, turn(result))


def solution(mesh):
    torus = Mesh(mesh.devices.reshape(8, 2, 4, 2, 2), (Z, XL, Y, XH, CORE))
    placed = (P(GX, GY), P(GX, GY))
    return jax.shard_map(
        local, mesh=torus, in_specs=placed, out_specs=(P(GX, GY), P(GX, GY)), check_vma=False
    )
```

profile of v0, /device:TPU:1, one launch (start us, length us, event | category | flops | bytes accessed | tf_op | source)
XLA Modules:
  0.0 124.8 jit_solution(8124947345590745901)
XLA Ops:
  0.6 2.1 %collective-permute-start.1 = (f32[32,128]{1,0:T(8,128)}, f32[32,128]{1,0:T(8,128)S(1)}, u32[]{:S(2)}, u32[]{:S(2)}) collective-permute-start(f32[32,128]{1,0:T(8,128)} %bitcast.103), channel_id=1, source_target_pairs={{0,16},{16,0},{1,17},{17,1},{2,18},{18,2},{3,19},{19,3},{4,20},{20... | collective-permute-start | bytes 49160 | tf_op jit(solution)/shard_map/ppermute | solution.py:25
  2.8 1.4 %broadcast_in_dim.89 = f32[8,32,128]{2,1,0:T(8,128)} broadcast(f32[32,128]{1,0:T(8,128)} %bitcast.104), dimensions={1,2} | broadcast | bytes 147456 | tf_op jit(solution)/shard_map/broadcast_in_dim | solution.py:65
  4.2 8.2 %all-to-all-start = ((f32[8,32,128]{2,1,0:T(8,128)}), f32[8,32,128]{2,1,0:T(8,128)S(1)}, u32[]{:S(2)}, u32[]{:S(2)}) async-start(f32[8,32,128]{2,1,0:T(8,128)} %broadcast_in_dim.89), calls=%async_computation | async-start | bytes 262144 | tf_op jit(solution)/shard_map/all_to_all | solution.py:66
  12.4 0.7 select_bitcast_fusion.5
  13.1 7.2 %all-to-all-done = f32[8,32,128]{2,1,0:T(8,128)S(1)} async-done(((f32[8,32,128]{2,1,0:T(8,128)}), f32[8,32,128]{2,1,0:T(8,128)S(1)}, u32[]{:S(2)}, u32[]{:S(2)}) %all-to-all-start) | async-done | bytes 131104 | tf_op jit(solution)/shard_map/all_to_all | solution.py:66
  20.3 0.8 pad_maximum_fusion.2
  21.2 9.0 %all-to-all-start.1 = ((f32[16,2,32,128]{3,2,1,0:T(8,128)}), f32[16,2,32,128]{3,2,1,0:T(8,128)S(1)}, u32[]{:S(2)}, u32[]{:S(2)}) async-start(f32[16,2,32,128]{3,2,1,0:T(8,128)} %pad_maximum_fusion.2), calls=%async_computation.1 | async-start | bytes 1048576 | tf_op jit(solution)/shard_map/all_to_all | solution.py:70
  30.2 1.9 %collective-permute-start = (f32[128,128]{1,0:T(8,128)S(1)}, f32[128,128]{1,0:T(8,128)S(1)}, u32[]{:S(2)}, u32[]{:S(2)}) collective-permute-start(f32[128,128]{1,0:T(8,128)S(1)} %copy-done), channel_id=1, source_target_pairs={{0,0},{1,16},{16,1},{17,17},{2,2},{3,18},{18,3},{19,19},{4,4},{5,2... | collective-permute-start | bytes 196616 | tf_op jit(solution)/shard_map/ppermute | solution.py:29
  32.2 5.8 %collective-permute-done = f32[128,128]{1,0:T(8,128)S(1)} collective-permute-done((f32[128,128]{1,0:T(8,128)S(1)}, f32[128,128]{1,0:T(8,128)S(1)}, u32[]{:S(2)}, u32[]{:S(2)}) %collective-permute-start) | collective-permute-done | bytes 65568 | tf_op jit(solution)/shard_map/ppermute | solution.py:29
  37.9 3.5 %all-to-all-done.1 = f32[16,2,32,128]{3,2,1,0:T(8,128)S(1)} async-done(((f32[16,2,32,128]{3,2,1,0:T(8,128)}), f32[16,2,32,128]{3,2,1,0:T(8,128)S(1)}, u32[]{:S(2)}, u32[]{:S(2)}) %all-to-all-start.1) | async-done | bytes 524320 | tf_op jit(solution)/shard_map/all_to_all | solution.py:70
  41.4 0.6 bitcast_dynamic-update-slice_fusion.15
  42.1 3.6 %collective-permute-start.4 = (f32[128,128]{1,0:T(8,128)S(1)}, f32[128,128]{1,0:T(8,128)S(1)}, u32[]{:S(2)}, u32[]{:S(2)}) collective-permute-start(f32[128,128]{1,0:T(8,128)S(1)} %get-tuple-element.11), channel_id=1, source_target_pairs={{0,192},{32,224},{64,0},{96,32},{128,64},{160,96},{192,128},{224,1... | collective-permute-start | bytes 196616 | tf_op jit(solution)/shard_map/ppermute | solution.py:21
  45.7 0.3 collective-permute-start.5
  46.0 2.4 %collective-permute-start.6 = (f32[128,128]{1,0:T(8,128)S(1)}, f32[128,128]{1,0:T(8,128)S(1)}, u32[]{:S(2)}, u32[]{:S(2)}) collective-permute-start(f32[128,128]{1,0:T(8,128)S(1)} %get-tuple-element.11), channel_id=1, source_target_pairs={{0,224},{32,0},{64,32},{96,64},{128,96},{160,128},{192,160},{224,1... | collective-permute-start | bytes 196616 | tf_op jit(solution)/shard_map/ppermute | solution.py:21
  48.4 1.1 broadcast_in_dim.91
  49.5 3.7 %all-to-all-start.2 = ((f32[16,128,128]{1,2,0:T(8,128)}), f32[16,128,128]{1,2,0:T(8,128)S(1)}, u32[]{:S(2)}, u32[]{:S(2)}) async-start(f32[16,128,128]{1,2,0:T(8,128)} %broadcast_in_dim.91), calls=%async_computation.2 | async-start | bytes 2097152 | tf_op jit(solution)/shard_map/all_to_all | solution.py:40
  53.4 2.6 %collective-permute-start.8 = (f32[128,128]{1,0:T(8,128)S(1)}, f32[128,128]{1,0:T(8,128)S(1)}, u32[]{:S(2)}, u32[]{:S(2)}) collective-permute-start(f32[128,128]{1,0:T(8,128)S(1)} %collective-permute-done.4), channel_id=1, source_target_pairs={{0,224},{32,0},{64,32},{96,64},{128,96},{160,128},{192,160},{224,1... | collective-permute-start | bytes 196616 | tf_op jit(solution)/shard_map/ppermute | solution.py:21
  56.1 1.6 %collective-permute-done.7 = f32[128,128]{1,0:T(8,128)S(1)} collective-permute-done((f32[128,128]{1,0:T(8,128)S(1)}, f32[128,128]{1,0:T(8,128)S(1)}, u32[]{:S(2)}, u32[]{:S(2)}) %collective-permute-start.7) | collective-permute-done | bytes 65568 | tf_op jit(solution)/shard_map/ppermute | solution.py:21
  57.7 1.1 collective-permute-done.9
  58.7 4.2 %collective-permute-start.10 = (f32[8,128,128]{2,1,0:T(8,128)S(1)}, f32[8,128,128]{2,1,0:T(8,128)S(1)}, u32[]{:S(2)}, u32[]{:S(2)}) collective-permute-start(f32[8,128,128]{2,1,0:T(8,128)S(1)} %bitcast_dynamic-update-slice_fusion.8), channel_id=1, source_target_pairs={{0,1},{1,0},{2,3},{3,2},{4,5},{5,4},{6,7},{7,6},{8,9},{9,8},{10,11... | collective-permute-start | bytes 1572872 | tf_op jit(solution)/shard_map/ppermute | solution.py:25
  62.9 1.5 %collective-permute-done.10 = f32[8,128,128]{2,1,0:T(8,128)S(1)} collective-permute-done((f32[8,128,128]{2,1,0:T(8,128)S(1)}, f32[8,128,128]{2,1,0:T(8,128)S(1)}, u32[]{:S(2)}, u32[]{:S(2)}) %collective-permute-start.10) | collective-permute-done | bytes 524320 | tf_op jit(solution)/shard_map/ppermute | solution.py:25
  64.5 0.1 select_bitcast_fusion.3
  64.6 0.2 pad_maximum_fusion.1
  64.9 2.8 %all-to-all-done.2 = f32[16,128,128]{1,2,0:T(8,128)S(1)} async-done(((f32[16,128,128]{1,2,0:T(8,128)}), f32[16,128,128]{1,2,0:T(8,128)S(1)}, u32[]{:S(2)}, u32[]{:S(2)}) %all-to-all-start.2) | async-done | bytes 1048608 | tf_op jit(solution)/shard_map/all_to_all | solution.py:40
  67.7 1.8 %fusion.31 = f32[128,128]{1,0:T(8,128)S(1)} fusion(f32[128,2048]{0,1:T(8,128)S(1)} %bitcast.96, f32[2048,128]{1,0:T(8,128)S(1)} %bitcast.100), kind=kOutput, calls=%fused_computation.60 | convolution fusion | flops 402653184 | bytes 2162688 | tf_op jit(solution)/shard_map/dot_general | solution.py:14
  69.5 0.9 multiply_reduce_fusion
  70.4 0.7 concatenate.3
  71.1 3.6 %collective-permute-start.12 = (f32[136,128]{1,0:T(8,128)S(1)}, f32[136,128]{1,0:T(8,128)S(1)}, u32[]{:S(2)}, u32[]{:S(2)}) collective-permute-start(f32[136,128]{1,0:T(8,128)S(1)} %concatenate.3), channel_id=1, source_target_pairs={{0,192},{32,224},{64,0},{96,32},{128,64},{160,96},{192,128},{224,1... | collective-permute-start | bytes 208904 | tf_op jit(solution)/shard_map/ppermute | solution.py:21
  74.7 2.7 %collective-permute-start.14 = (f32[136,128]{1,0:T(8,128)S(1)}, f32[136,128]{1,0:T(8,128)S(1)}, u32[]{:S(2)}, u32[]{:S(2)}) collective-permute-start(f32[136,128]{1,0:T(8,128)S(1)} %concatenate.3), channel_id=1, source_target_pairs={{0,224},{32,0},{64,32},{96,64},{128,96},{160,128},{192,160},{224,1... | collective-permute-start | bytes 208904 | tf_op jit(solution)/shard_map/ppermute | solution.py:21
  77.4 0.7 bitcast_dynamic-update-slice_fusion.7
  78.3 2.6 %collective-permute-start.16 = (f32[136,128]{1,0:T(8,128)S(1)}, f32[136,128]{1,0:T(8,128)S(1)}, u32[]{:S(2)}, u32[]{:S(2)}) collective-permute-start(f32[136,128]{1,0:T(8,128)S(1)} %collective-permute-done.12), channel_id=1, source_target_pairs={{0,224},{32,0},{64,32},{96,64},{128,96},{160,128},{192,160},{224,1... | collective-permute-start | bytes 208904 | tf_op jit(solution)/shard_map/ppermute | solution.py:21
  81.0 1.5 %collective-permute-done.15 = f32[136,128]{1,0:T(8,128)S(1)} collective-permute-done((f32[136,128]{1,0:T(8,128)S(1)}, f32[136,128]{1,0:T(8,128)S(1)}, u32[]{:S(2)}, u32[]{:S(2)}) %collective-permute-start.15) | collective-permute-done | bytes 69664 | tf_op jit(solution)/shard_map/ppermute | solution.py:21
  82.5 1.0 collective-permute-done.17
  83.6 6.4 %collective-permute-start.18 = (f32[8,136,128]{2,1,0:T(8,128)S(1)}, f32[8,136,128]{2,1,0:T(8,128)}, u32[]{:S(2)}, u32[]{:S(2)}) collective-permute-start(f32[8,136,128]{2,1,0:T(8,128)S(1)} %bitcast_dynamic-update-slice_fusion), channel_id=1, source_target_pairs={{0,1},{1,0},{2,3},{3,2},{4,5},{5,4},{6,7},{7,6},{8,9},{9,8},{10,11... | collective-permute-start | bytes 1671176 | tf_op jit(solution)/shard_map/ppermute | solution.py:25
  90.1 1.1 broadcast_in_dim.101
  91.2 4.3 %all-to-all-start.3 = ((f32[16,128,128]{1,2,0:T(8,128)}), f32[16,128,128]{1,2,0:T(8,128)}, u32[]{:S(2)}, u32[]{:S(2)}) async-start(f32[16,128,128]{1,2,0:T(8,128)} %broadcast_in_dim.101), calls=%async_computation.3 | async-start | bytes 2097152 | tf_op jit(solution)/shard_map/all_to_all | solution.py:40
  95.7 3.3 %collective-permute-start.2 = (f32[128,128]{1,0:T(8,128)S(1)}, f32[128,128]{1,0:T(8,128)S(1)}, u32[]{:S(2)}, u32[]{:S(2)}) collective-permute-start(f32[128,128]{1,0:T(8,128)S(1)} %get-tuple-element.11), channel_id=1, source_target_pairs={{0,0},{1,16},{16,1},{17,17},{2,2},{3,18},{18,3},{19,19},{4,4},{5,2... | collective-permute-start | bytes 196616 | tf_op jit(solution)/shard_map/ppermute | solution.py:29
  98.9 1.3 %copy.29 = f32[8,2,128,128]{2,3,1,0:T(8,128)} copy(f32[8,2,128,128]{3,2,0,1:T(8,128)S(1)} %get-tuple-element.5) | data formatting | bytes 2097152 | tf_op jit(solution)/shard_map/mul | solution.py:102
  100.3 1.1 select_bitcast_fusion.1
  101.4 1.1 pad_maximum_fusion
  102.5 1.8 %copy.27 = f32[8,2,136,128]{2,3,1,0:T(8,128)S(1)} copy(f32[8,2,136,128]{3,2,0,1:T(8,128)} %pad_maximum_fusion) | data formatting | bytes 2228224 | tf_op jit(solution)/shard_map/stack | solution.py:55
  104.2 0.6 slice_reduce_fusion
  105.6 8.7 %all-to-all-done.3 = f32[16,128,128]{1,2,0:T(8,128)} async-done(((f32[16,128,128]{1,2,0:T(8,128)}), f32[16,128,128]{1,2,0:T(8,128)}, u32[]{:S(2)}, u32[]{:S(2)}) %all-to-all-start.3) | async-done | bytes 1048608 | tf_op jit(solution)/shard_map/all_to_all | solution.py:40
  114.3 3.7 %fusion.20 = f32[128,128]{1,0:T(8,128)S(1)} fusion(f32[16,128,128]{1,2,0:T(8,128)} %bitcast.99, f32[16,136,128]{1,2,0:T(8,128)S(1)} %bitcast.98, f32[16]{0:T(128)S(1)} %get-tuple-element.12, f32[16,128,128]{1,2,0:T(8,128)S(1)} %all-to-all-done.2, f32[16,128,128]{1,2,0:T(8,128)} %all-to-all-done.3, f32[128,128]{0,1:T(8,128)S(1)} %copy.28, ...), kind=kOutput, calls=%fused_computation.24 | convolution fusion | flops 405635072 | bytes 4459520 | tf_op jit(solution)/shard_map/dot_general | solution.py:14
  118.0 1.9 %collective-permute-start.19 = (f32[128,128]{1,0:T(8,128)S(1)}, f32[128,128]{1,0:T(8,128)S(1)}, u32[]{:S(2)}, u32[]{:S(2)}) collective-permute-start(f32[128,128]{1,0:T(8,128)S(1)} %fusion.20), channel_id=1, source_target_pairs={{0,0},{1,16},{16,1},{17,17},{2,2},{3,18},{18,3},{19,19},{4,4},{5,2... | collective-permute-start | bytes 196616 | tf_op jit(solution)/shard_map/ppermute | solution.py:29
  119.9 3.6 %collective-permute-done.19 = f32[128,128]{1,0:T(8,128)S(1)} collective-permute-done((f32[128,128]{1,0:T(8,128)S(1)}, f32[128,128]{1,0:T(8,128)S(1)}, u32[]{:S(2)}, u32[]{:S(2)}) %collective-permute-start.19) | collective-permute-done | bytes 65568 | tf_op jit(solution)/shard_map/ppermute | solution.py:29
  123.6 0.6 copy.54
  124.2 0.6 copy.55
  (47 shorter events, 1.2 us)
Async XLA Ops:
  0.6 29.6 %copy-start = (f32[128,128]{1,0:T(8,128)S(1)}, f32[128,128]{1,0:T(8,128)}, u32[]{:S(2)}) copy-start(f32[128,128]{1,0:T(8,128)} %param.3) | copy-start | bytes 196612
  0.6 11.7 %collective-permute-start.1 = (f32[32,128]{1,0:T(8,128)}, f32[32,128]{1,0:T(8,128)S(1)}, u32[]{:S(2)}, u32[]{:S(2)}) collective-permute-start(f32[32,128]{1,0:T(8,128)} %bitcast.103), channel_id=1, source_target_pairs={{0,16},{16,0},{1,17},{17,1},{2,18},{18,2},{3,19},{19,3},{4,20},{20... | collective-permute-start | bytes 49160 | tf_op jit(solution)/shard_map/ppermute | solution.py:25
  4.2 16.1 %all-to-all-start = ((f32[8,32,128]{2,1,0:T(8,128)}), f32[8,32,128]{2,1,0:T(8,128)S(1)}, u32[]{:S(2)}, u32[]{:S(2)}) async-start(f32[8,32,128]{2,1,0:T(8,128)} %broadcast_in_dim.89), calls=%async_computation | async-start | bytes 262144 | tf_op jit(solution)/shard_map/all_to_all | solution.py:66
  21.2 20.2 %all-to-all-start.1 = ((f32[16,2,32,128]{3,2,1,0:T(8,128)}), f32[16,2,32,128]{3,2,1,0:T(8,128)S(1)}, u32[]{:S(2)}, u32[]{:S(2)}) async-start(f32[16,2,32,128]{3,2,1,0:T(8,128)} %pad_maximum_fusion.2), calls=%async_computation.1 | async-start | bytes 1048576 | tf_op jit(solution)/shard_map/all_to_all | solution.py:70
  30.2 7.7 %collective-permute-start = (f32[128,128]{1,0:T(8,128)S(1)}, f32[128,128]{1,0:T(8,128)S(1)}, u32[]{:S(2)}, u32[]{:S(2)}) collective-permute-start(f32[128,128]{1,0:T(8,128)S(1)} %copy-done), channel_id=1, source_target_pairs={{0,0},{1,16},{16,1},{17,17},{2,2},{3,18},{18,3},{19,19},{4,4},{5,2... | collective-permute-start | bytes 196616 | tf_op jit(solution)/shard_map/ppermute | solution.py:29
  42.0 11.2 %collective-permute-start.3 = (f32[128,128]{1,0:T(8,128)S(1)}, f32[128,128]{1,0:T(8,128)S(1)}, u32[]{:S(2)}, u32[]{:S(2)}) collective-permute-start(f32[128,128]{1,0:T(8,128)S(1)} %get-tuple-element.11), channel_id=1, source_target_pairs={{0,64},{32,96},{64,128},{96,160},{128,192},{160,224},{192,0},{224,... | collective-permute-start | bytes 196616 | tf_op jit(solution)/shard_map/ppermute | solution.py:21
  42.1 11.3 %collective-permute-start.4 = (f32[128,128]{1,0:T(8,128)S(1)}, f32[128,128]{1,0:T(8,128)S(1)}, u32[]{:S(2)}, u32[]{:S(2)}) collective-permute-start(f32[128,128]{1,0:T(8,128)S(1)} %get-tuple-element.11), channel_id=1, source_target_pairs={{0,192},{32,224},{64,0},{96,32},{128,64},{160,96},{192,128},{224,1... | collective-permute-start | bytes 196616 | tf_op jit(solution)/shard_map/ppermute | solution.py:21
  45.7 10.3 %collective-permute-start.5 = (f32[128,128]{1,0:T(8,128)S(1)}, f32[128,128]{1,0:T(8,128)S(1)}, u32[]{:S(2)}, u32[]{:S(2)}) collective-permute-start(f32[128,128]{1,0:T(8,128)S(1)} %get-tuple-element.11), channel_id=1, source_target_pairs={{0,32},{32,64},{64,96},{96,128},{128,160},{160,192},{192,224},{224... | collective-permute-start | bytes 196616 | tf_op jit(solution)/shard_map/ppermute | solution.py:21
  46.0 10.1 %collective-permute-start.6 = (f32[128,128]{1,0:T(8,128)S(1)}, f32[128,128]{1,0:T(8,128)S(1)}, u32[]{:S(2)}, u32[]{:S(2)}) collective-permute-start(f32[128,128]{1,0:T(8,128)S(1)} %get-tuple-element.11), channel_id=1, source_target_pairs={{0,224},{32,0},{64,32},{96,64},{128,96},{160,128},{192,160},{224,1... | collective-permute-start | bytes 196616 | tf_op jit(solution)/shard_map/ppermute | solution.py:21
  49.5 18.1 %all-to-all-start.2 = ((f32[16,128,128]{1,2,0:T(8,128)}), f32[16,128,128]{1,2,0:T(8,128)S(1)}, u32[]{:S(2)}, u32[]{:S(2)}) async-start(f32[16,128,128]{1,2,0:T(8,128)} %broadcast_in_dim.91), calls=%async_computation.2 | async-start | bytes 2097152 | tf_op jit(solution)/shard_map/all_to_all | solution.py:40
  53.2 4.4 %collective-permute-start.7 = (f32[128,128]{1,0:T(8,128)S(1)}, f32[128,128]{1,0:T(8,128)S(1)}, u32[]{:S(2)}, u32[]{:S(2)}) collective-permute-start(f32[128,128]{1,0:T(8,128)S(1)} %collective-permute-done.3), channel_id=1, source_target_pairs={{0,32},{32,64},{64,96},{96,128},{128,160},{160,192},{192,224},{224... | collective-permute-start | bytes 196616 | tf_op jit(solution)/shard_map/ppermute | solution.py:21
  53.3 5.4 %collective-permute-start.9 = (f32[128,128]{1,0:T(8,128)S(1)}, f32[128,128]{1,0:T(8,128)S(1)}, u32[]{:S(2)}, u32[]{:S(2)}) collective-permute-start(f32[128,128]{1,0:T(8,128)S(1)} %collective-permute-done.3), channel_id=1, source_target_pairs={{0,64},{32,96},{64,128},{96,160},{128,192},{160,224},{192,0},{224,... | collective-permute-start | bytes 196616 | tf_op jit(solution)/shard_map/ppermute | solution.py:21
  53.4 4.2 %collective-permute-start.8 = (f32[128,128]{1,0:T(8,128)S(1)}, f32[128,128]{1,0:T(8,128)S(1)}, u32[]{:S(2)}, u32[]{:S(2)}) collective-permute-start(f32[128,128]{1,0:T(8,128)S(1)} %collective-permute-done.4), channel_id=1, source_target_pairs={{0,224},{32,0},{64,32},{96,64},{128,96},{160,128},{192,160},{224,1... | collective-permute-start | bytes 196616 | tf_op jit(solution)/shard_map/ppermute | solution.py:21
  58.7 5.7 %collective-permute-start.10 = (f32[8,128,128]{2,1,0:T(8,128)S(1)}, f32[8,128,128]{2,1,0:T(8,128)S(1)}, u32[]{:S(2)}, u32[]{:S(2)}) collective-permute-start(f32[8,128,128]{2,1,0:T(8,128)S(1)} %bitcast_dynamic-update-slice_fusion.8), channel_id=1, source_target_pairs={{0,1},{1,0},{2,3},{3,2},{4,5},{5,4},{6,7},{7,6},{8,9},{9,8},{10,11... | collective-permute-start | bytes 1572872 | tf_op jit(solution)/shard_map/ppermute | solution.py:25
  71.0 7.0 %collective-permute-start.11 = (f32[136,128]{1,0:T(8,128)S(1)}, f32[136,128]{1,0:T(8,128)S(1)}, u32[]{:S(2)}, u32[]{:S(2)}) collective-permute-start(f32[136,128]{1,0:T(8,128)S(1)} %concatenate.3), channel_id=1, source_target_pairs={{0,64},{32,96},{64,128},{96,160},{128,192},{160,224},{192,0},{224,... | collective-permute-start | bytes 208904 | tf_op jit(solution)/shard_map/ppermute | solution.py:21
  71.1 7.2 %collective-permute-start.12 = (f32[136,128]{1,0:T(8,128)S(1)}, f32[136,128]{1,0:T(8,128)S(1)}, u32[]{:S(2)}, u32[]{:S(2)}) collective-permute-start(f32[136,128]{1,0:T(8,128)S(1)} %concatenate.3), channel_id=1, source_target_pairs={{0,192},{32,224},{64,0},{96,32},{128,64},{160,96},{192,128},{224,1... | collective-permute-start | bytes 208904 | tf_op jit(solution)/shard_map/ppermute | solution.py:21
  74.7 6.3 %collective-permute-start.13 = (f32[136,128]{1,0:T(8,128)S(1)}, f32[136,128]{1,0:T(8,128)S(1)}, u32[]{:S(2)}, u32[]{:S(2)}) collective-permute-start(f32[136,128]{1,0:T(8,128)S(1)} %concatenate.3), channel_id=1, source_target_pairs={{0,32},{32,64},{64,96},{96,128},{128,160},{160,192},{192,224},{224... | collective-permute-start | bytes 208904 | tf_op jit(solution)/shard_map/ppermute | solution.py:21
  74.7 6.3 %collective-permute-start.14 = (f32[136,128]{1,0:T(8,128)S(1)}, f32[136,128]{1,0:T(8,128)S(1)}, u32[]{:S(2)}, u32[]{:S(2)}) collective-permute-start(f32[136,128]{1,0:T(8,128)S(1)} %concatenate.3), channel_id=1, source_target_pairs={{0,224},{32,0},{64,32},{96,64},{128,96},{160,128},{192,160},{224,1... | collective-permute-start | bytes 208904 | tf_op jit(solution)/shard_map/ppermute | solution.py:21
  78.1 4.4 %collective-permute-start.15 = (f32[136,128]{1,0:T(8,128)S(1)}, f32[136,128]{1,0:T(8,128)S(1)}, u32[]{:S(2)}, u32[]{:S(2)}) collective-permute-start(f32[136,128]{1,0:T(8,128)S(1)} %collective-permute-done.11), channel_id=1, source_target_pairs={{0,32},{32,64},{64,96},{96,128},{128,160},{160,192},{192,224},{224... | collective-permute-start | bytes 208904 | tf_op jit(solution)/shard_map/ppermute | solution.py:21
  78.1 5.4 %collective-permute-start.17 = (f32[136,128]{1,0:T(8,128)S(1)}, f32[136,128]{1,0:T(8,128)S(1)}, u32[]{:S(2)}, u32[]{:S(2)}) collective-permute-start(f32[136,128]{1,0:T(8,128)S(1)} %collective-permute-done.11), channel_id=1, source_target_pairs={{0,64},{32,96},{64,128},{96,160},{128,192},{160,224},{192,0},{224,... | collective-permute-start | bytes 208904 | tf_op jit(solution)/shard_map/ppermute | solution.py:21
  78.3 4.2 %collective-permute-start.16 = (f32[136,128]{1,0:T(8,128)S(1)}, f32[136,128]{1,0:T(8,128)S(1)}, u32[]{:S(2)}, u32[]{:S(2)}) collective-permute-start(f32[136,128]{1,0:T(8,128)S(1)} %collective-permute-done.12), channel_id=1, source_target_pairs={{0,224},{32,0},{64,32},{96,64},{128,96},{160,128},{192,160},{224,1... | collective-permute-start | bytes 208904 | tf_op jit(solution)/shard_map/ppermute | solution.py:21
  83.6 16.6 %collective-permute-start.18 = (f32[8,136,128]{2,1,0:T(8,128)S(1)}, f32[8,136,128]{2,1,0:T(8,128)}, u32[]{:S(2)}, u32[]{:S(2)}) collective-permute-start(f32[8,136,128]{2,1,0:T(8,128)S(1)} %bitcast_dynamic-update-slice_fusion), channel_id=1, source_target_pairs={{0,1},{1,0},{2,3},{3,2},{4,5},{5,4},{6,7},{7,6},{8,9},{9,8},{10,11... | collective-permute-start | bytes 1671176 | tf_op jit(solution)/shard_map/ppermute | solution.py:25
  91.2 23.1 %all-to-all-start.3 = ((f32[16,128,128]{1,2,0:T(8,128)}), f32[16,128,128]{1,2,0:T(8,128)}, u32[]{:S(2)}, u32[]{:S(2)}) async-start(f32[16,128,128]{1,2,0:T(8,128)} %broadcast_in_dim.101), calls=%async_computation.3 | async-start | bytes 2097152 | tf_op jit(solution)/shard_map/all_to_all | solution.py:40
  95.7 24.3 %collective-permute-start.2 = (f32[128,128]{1,0:T(8,128)S(1)}, f32[128,128]{1,0:T(8,128)S(1)}, u32[]{:S(2)}, u32[]{:S(2)}) collective-permute-start(f32[128,128]{1,0:T(8,128)S(1)} %get-tuple-element.11), channel_id=1, source_target_pairs={{0,0},{1,16},{16,1},{17,17},{2,2},{3,18},{18,3},{19,19},{4,4},{5,2... | collective-permute-start | bytes 196616 | tf_op jit(solution)/shard_map/ppermute | solution.py:29
  118.0 5.6 %collective-permute-start.19 = (f32[128,128]{1,0:T(8,128)S(1)}, f32[128,128]{1,0:T(8,128)S(1)}, u32[]{:S(2)}, u32[]{:S(2)}) collective-permute-start(f32[128,128]{1,0:T(8,128)S(1)} %fusion.20), channel_id=1, source_target_pairs={{0,0},{1,16},{16,1},{17,17},{2,2},{3,18},{18,3},{19,19},{4,4},{5,2... | collective-permute-start | bytes 196616 | tf_op jit(solution)/shard_map/ppermute | solution.py:29
where the time goes:
time: 126 us; the launch traced here: 125 us
  starting transfers between devices  63.2 us (50%)
  waiting for transfers between devices  38.3 us (30%)
  local copies, waits for them, and re-layouts  9.84 us (8%)
  matrix products  6.07 us (5%)
  other arithmetic  5.61 us (4%)
  between operations  1.82 us (1%)
    ppermute x14, starting transfers between devices, rotate(): lax.ppermute(array, axis, [(s, (s + shift) % size) for s in range(size)])  18.2 us
    ppermute x3, starting transfers between devices, swap(): return lax.ppermute(array, axis, [(0, 1), (1, 0)])  12.7 us
    all_to_all x2, waiting for transfers between devices, row_panel(): return lax.all_to_all(copies, (Y, XH, XL), 0, 0, tiled=True)  11.5 us
    ppermute x3, waiting for transfers between devices, turn(): return lax.ppermute(array, (XL, CORE), [(0, 0), (1, 2), (2, 1), (3, 3)])  9.41 us
    all_to_all x1, starting transfers between devices, gradient_panels(): lax.all_to_all(jnp.stack((for_rows, for_columns), axis=1), GY, 0, 0, tile...  9.02 us
    all_to_all x1, starting transfers between devices, gradient_panels(): along_z = lax.all_to_all(copies, Z, 0, 0, tiled=True)  8.19 us
    all_to_all x2, starting transfers between devices, row_panel(): return lax.all_to_all(copies, (Y, XH, XL), 0, 0, tiled=True)  7.98 us
    all_to_all x1, waiting for transfers between devices, gradient_panels(): along_z = lax.all_to_all(copies, Z, 0, 0, tiled=True)  7.21 us
  transfers between devices with their start and end apart: 24, of which 11 were waited for; matrix products, arithmetic and copies ran while one was open for 12% of the time, Pallas kernels for 0%

commit v1 on v0

v1 whole, which is shorter than its diff:
```python
import jax
import jax.numpy as jnp
from jax import lax
from jax.experimental import pallas as pl
from jax.experimental.pallas import tpu as pltpu
from jax.sharding import Mesh
from jax.sharding import PartitionSpec as P


Z, XL, Y, XH, CORE = "gx_0", "gx_1", "gy_0", "gy_1", "gy_2"
GX = (Z, XL)
GY = (Y, XH, CORE)


def matmul(leading, trailing):
    return jnp.dot(
        leading, trailing, preferred_element_type=jnp.float32, precision=lax.Precision.HIGHEST
    )


def rotate(array, axis, shift):
    size = lax.axis_size(axis)
    return lax.ppermute(array, axis, [(s, (s + shift) % size) for s in range(size)])


def swap(array, axis):
    return lax.ppermute(array, axis, [(0, 1), (1, 0)])


def turn(array):
    return lax.ppermute(array, (XL, CORE), [(0, 0), (1, 2), (2, 1), (3, 3)])


def row_panel(copies):
    return lax.all_to_all(copies, (Y, XH, XL), 0, 0, tiled=True)


def column_pieces(block):
    place = lax.axis_index(Z)
    found = {0: block}
    for shift in (2, -2, 1, -1):
        found[shift] = rotate(block, Z, shift)
    found[3] = rotate(found[2], Z, 1)
    found[-3] = rotate(found[-2], Z, -1)
    found[4] = rotate(found[2], Z, 2)
    mine = jnp.zeros((8,) + block.shape, block.dtype)
    for shift, piece in found.items():
        mine = lax.dynamic_update_slice(mine, piece[None], ((place - shift) % 8, 0, 0))
    return mine, swap(mine, CORE)


def exchange(array):
    places = [(z, x, g, c) for z in range(8) for x in range(2) for g in range(8) for c in range(2)]
    pairs = [
        (((z * 2 + x) * 8 + g) * 2 + c, ((g * 2 + x) * 8 + z) * 2 + c) for z, x, g, c in places
    ]
    return lax.ppermute(array, (Z, XL, Y, XH, CORE), pairs)


def outer_part(gradient):
    piece = gradient.T
    beside = swap(piece, XL)
    moved = exchange(piece)
    at_high = lax.axis_index(XL) == 1
    pair = jnp.stack((jnp.where(at_high, beside, piece), jnp.where(at_high, piece, beside)))
    rows_of = lax.all_to_all(jnp.tile(pair, (8, 1, 1)), GY, 0, 0, tiled=True)
    mine, other = column_pieces(moved)
    core = lax.axis_index(CORE)
    columns_of = jnp.stack(
        (jnp.where(core == 0, mine, other), jnp.where(core == 0, other, mine)), axis=1
    )
    width = piece.shape[1]
    return matmul(rows_of.reshape(-1, width).T, columns_of.reshape(-1, width))


def split(array):
    high = array.astype(jnp.bfloat16)
    return high, (array - high.astype(jnp.float32)).astype(jnp.bfloat16)


def product(left, right):
    left_high, left_low = split(left)
    right_high, right_low = split(right)

    def dot(one, two):
        return jnp.dot(one, two, preferred_element_type=jnp.float32)

    return dot(left_high, right_high) + (dot(left_high, right_low) + dot(left_low, right_high))


def square_kernel(core_ref, row_ref, mine_ref, other_ref, copies_ref, carried_ref):
    core = core_ref[0]
    side = mine_ref.shape[1]
    total = jnp.zeros((side, mine_ref.shape[2]), jnp.float32)
    norms = jnp.zeros((side, side), jnp.float32)
    for place in range(mine_ref.shape[0]):
        first = row_ref[2 * place + core]
        second = row_ref[2 * place + 1 - core]
        total = total + product(
            jnp.concatenate((first, second), axis=1),
            jnp.concatenate((mine_ref[place], other_ref[place]), axis=0),
        )
        norms = norms + first * first + second * second
    for number in range(copies_ref.shape[0]):
        copies_ref[number] = total
    carried_ref[:side] = total
    carried_ref[side:] = jnp.full((carried_ref.shape[0] - side, side), jnp.sum(norms))


def root_kernel(
    index_ref, square_row, stat_row, square_mine, square_other, stat_mine, stat_other, stat, out
):
    core, row_block, column_block = index_ref[0], index_ref[1], index_ref[2]
    places, side = stat_mine.shape[0], stat.shape[0]
    sums = jnp.zeros((8, side), jnp.float32)
    for place in range(places):
        sums = sums + square_mine[place, side : side + 8] + square_other[place, side : side + 8]
    divisor = 2.0 * jnp.sqrt(sums[:1] / (2 * places * side))
    inverse = 1.0 / divisor
    across = lax.broadcasted_iota(jnp.int32, (side, side), 0)
    along = lax.broadcasted_iota(jnp.int32, (side, side), 1)
    eye = jnp.where(across == along, 1.0, 0.0)

    def quadratic(square, plain, on_diagonal):
        scaled = (square * inverse - 4.5 * plain) * inverse
        return scaled + jnp.where(on_diagonal, 3.375, 0.0) * eye

    total = jnp.zeros((side, side), jnp.float32)
    for place in range(places):
        lefts, rights = [], []
        for part, square, plain in ((core, square_mine, stat_mine), (1 - core, square_other, stat_other)):
            number = 2 * place + part
            lefts.append(quadratic(square_row[number], stat_row[number], number == row_block))
            rights.append(quadratic(square[place, :side], plain[place], number == column_block))
        total = total + product(jnp.concatenate(lefts, axis=1), jnp.concatenate(rights, axis=0))
    constant = jnp.where(row_block == column_block, 1.5380859375, 0.0) * eye
    out[...] = 0.0625 * total - (0.5390625 * inverse) * stat[...] + constant


def call(kernel, outs, *operands):
    spaces = [pl.BlockSpec(memory_space=pltpu.SMEM)] + [
        pl.BlockSpec(memory_space=pltpu.VMEM) for _ in operands[1:]
    ]
    return pl.pallas_call(
        kernel,
        out_shape=[jax.ShapeDtypeStruct(shape, jnp.float32) for shape in outs],
        in_specs=spaces,
        out_specs=[pl.BlockSpec(memory_space=pltpu.VMEM) for _ in outs],
    )(*operands)


def local(gradient, stat_old):
    side = stat_old.shape[0]
    core = lax.axis_index(CORE)
    row_block = 2 * lax.axis_index(Z) + core
    column_block = 4 * lax.axis_index(Y) + 2 * lax.axis_index(XH) + lax.axis_index(XL)

    indices = jnp.stack((core, row_block, column_block))

    outer = outer_part(gradient)
    stat_moved = turn(stat_old)
    stat = 0.9 * stat_moved + outer / (gradient.shape[1] * 16)

    stat_row = row_panel(jnp.broadcast_to(stat[None], (16,) + stat.shape))
    stat_mine, stat_other = column_pieces(stat)
    statistic = turn(stat)
    copies, carried = call(
        square_kernel,
        ((16, side, side), (side + 8, side)),
        indices,
        stat_row,
        stat_mine,
        stat_other,
    )
    square_row = row_panel(copies)
    square_mine, square_other = column_pieces(carried)
    (result,) = call(
        root_kernel,
        ((side, side),),
        indices,
        square_row,
        stat_row,
        square_mine,
        square_other,
        stat_mine,
        stat_other,
        stat,
    )
    return (statistic, turn(result))


def solution(mesh):
    torus = Mesh(mesh.devices.reshape(8, 2, 4, 2, 2), (Z, XL, Y, XH, CORE))
    placed = (P(GX, GY), P(GX, GY))
    return jax.shard_map(
        local, mesh=torus, in_specs=placed, out_specs=(P(GX, GY), P(GX, GY)), check_vma=False
    )
```

time: 126 us -> 121 us (0.960)
  starting transfers between devices: 63.2 us -> 79.5 us
  waiting for transfers between devices: 38.3 us -> 24.4 us
  Pallas kernels: 0 us -> 6.9 us
  matrix products: 6.07 us -> 0.6 us
  other arithmetic: 5.61 us -> 0.72 us
  local copies, waits for them, and re-layouts: 9.84 us -> 6.99 us
    ppermute x14 -> x21, starting transfers between devices: 18.2 us -> 36.2 us  [rotate(): lax.ppermute(array, axis, [(s, (s + shift) % size) for s in range(size)])]
    all_to_all x2 -> x1, starting transfers between devices: 17.2 us -> 5.94 us  [outer_part(): rows_of = lax.all_to_all(jnp.tile(pair, (8, 1, 1)), GY, 0, 0, tiled=True)]
    all_to_all x2, waiting for transfers between devices: 11.5 us -> 3.7 us  [row_panel(): return lax.all_to_all(copies, (Y, XH, XL), 0, 0, tiled=True)]
    ppermute x3, waiting for transfers between devices: 9.41 us -> 2.14 us  [turn(): return lax.ppermute(array, (XL, CORE), [(0, 0), (1, 2), (2, 1), (3, 3)])]
    pallas_call x0 -> x2, Pallas kernels: none -> 6.9 us  [call(): pl.pallas_call(kernel, out_shape=[jax.ShapeDtypeStruct(shape, jnp.float32...]
    dot_general x3 -> x1, matrix products: 6.07 us -> 0.6 us  [matmul(): jnp.dot(leading, trailing, preferred_element_type=jnp.float32, precision=...]
    ppermute x3, starting transfers between devices: 7.09 us -> 12.5 us  [turn(): return lax.ppermute(array, (XL, CORE), [(0, 0), (1, 2), (2, 1), (3, 3)])]
    ppermute x14 -> x21, waiting for transfers between devices: 5.19 us -> 9.06 us  [rotate(): lax.ppermute(array, axis, [(s, (s + shift) % size) for s in range(size)])]
  transfers between devices with their start and end apart: 24 -> 32, of which waited for: 11 -> 9; matrix products, arithmetic and copies ran while one was open for 12% -> 2% of each run, Pallas kernels for 0% -> 3%
where the time goes in v1:
time: 121 us; the launch traced here: 120 us
  starting transfers between devices  79.5 us (66%)
  waiting for transfers between devices  24.4 us (20%)
  local copies, waits for them, and re-layouts  6.99 us (6%)
  Pallas kernels  6.9 us (6%)
    ppermute x21, starting transfers between devices, rotate(): lax.ppermute(array, axis, [(s, (s + shift) % size) for s in range(size)])  36.2 us
    ppermute x4, starting transfers between devices, swap(): return lax.ppermute(array, axis, [(0, 1), (1, 0)])  15 us
    ppermute x3, starting transfers between devices, turn(): return lax.ppermute(array, (XL, CORE), [(0, 0), (1, 2), (2, 1), (3, 3)])  12.5 us
    ppermute x21, waiting for transfers between devices, rotate(): lax.ppermute(array, axis, [(s, (s + shift) % size) for s in range(size)])  9.06 us
    all_to_all x1, waiting for transfers between devices, outer_part(): rows_of = lax.all_to_all(jnp.tile(pair, (8, 1, 1)), GY, 0, 0, tiled=True)  8.62 us
    all_to_all x2, starting transfers between devices, row_panel(): return lax.all_to_all(copies, (Y, XH, XL), 0, 0, tiled=True)  8.5 us
    pallas_call x2, Pallas kernels, call(): pl.pallas_call(kernel, out_shape=[jax.ShapeDtypeStruct(shape, jnp.float32...  6.9 us
    all_to_all x1, starting transfers between devices, outer_part(): rows_of = lax.all_to_all(jnp.tile(pair, (8, 1, 1)), GY, 0, 0, tiled=True)  5.94 us
  transfers between devices with their start and end apart: 32, of which 9 were waited for; matrix products, arithmetic and copies ran while one was open for 2% of the time, Pallas kernels for 3%

profile of v1, /device:TPU:1, one launch (start us, length us, event | category | flops | bytes accessed | tf_op | source)
XLA Modules:
  0.0 120.3 jit_solution(11180210619248958978)
XLA Ops:
  0.6 1.4 %collective-permute-start.2 = (f32[32,128]{1,0:T(8,128)}, f32[32,128]{1,0:T(8,128)S(1)}, u32[]{:S(2)}, u32[]{:S(2)}) collective-permute-start(f32[32,128]{1,0:T(8,128)} %bitcast.71), channel_id=1, source_target_pairs={{0,0},{1,1},{2,32},{3,33},{4,64},{5,65},{6,96},{7,97},{8,128},{9,1... | collective-permute-start | bytes 49160 | tf_op jit(solution)/shard_map/ppermute | solution.py:57
  2.0 2.0 %collective-permute-start.1 = (f32[32,128]{1,0:T(8,128)}, f32[32,128]{1,0:T(8,128)S(1)}, u32[]{:S(2)}, u32[]{:S(2)}) collective-permute-start(f32[32,128]{1,0:T(8,128)} %bitcast.72), channel_id=1, source_target_pairs={{0,16},{16,0},{1,17},{17,1},{2,18},{18,2},{3,19},{19,3},{4,20},{20... | collective-permute-start | bytes 49160 | tf_op jit(solution)/shard_map/ppermute | solution.py:27
  4.0 4.7 %collective-permute-start = (f32[128,128]{1,0:T(8,128)}, f32[128,128]{1,0:T(8,128)S(1)}, u32[]{:S(2)}, u32[]{:S(2)}) collective-permute-start(f32[128,128]{1,0:T(8,128)} %param.3), channel_id=1, source_target_pairs={{0,0},{1,16},{16,1},{17,17},{2,2},{3,18},{18,3},{19,19},{4,4},{5,2... | collective-permute-start | bytes 196616 | tf_op jit(solution)/shard_map/ppermute | solution.py:31
  8.9 2.7 %collective-permute-start.3 = (f32[32,128]{1,0:T(8,128)S(1)}, f32[32,128]{1,0:T(8,128)S(1)}, u32[]{:S(2)}, u32[]{:S(2)}) collective-permute-start(f32[32,128]{1,0:T(8,128)S(1)} %collective-permute-done.2), channel_id=1, source_target_pairs={{0,64},{32,96},{64,128},{96,160},{128,192},{160,224},{192,0},{224,... | collective-permute-start | bytes 49160 | tf_op jit(solution)/shard_map/ppermute | solution.py:23
  11.6 4.8 %collective-permute-start.4 = (f32[32,128]{1,0:T(8,128)S(1)}, f32[32,128]{1,0:T(8,128)S(1)}, u32[]{:S(2)}, u32[]{:S(2)}) collective-permute-start(f32[32,128]{1,0:T(8,128)S(1)} %collective-permute-done.2), channel_id=1, source_target_pairs={{0,192},{32,224},{64,0},{96,32},{128,64},{160,96},{192,128},{224,1... | collective-permute-start | bytes 49160 | tf_op jit(solution)/shard_map/ppermute | solution.py:23
  16.4 2.2 %collective-permute-start.5 = (f32[32,128]{1,0:T(8,128)S(1)}, f32[32,128]{1,0:T(8,128)S(1)}, u32[]{:S(2)}, u32[]{:S(2)}) collective-permute-start(f32[32,128]{1,0:T(8,128)S(1)} %collective-permute-done.2), channel_id=1, source_target_pairs={{0,32},{32,64},{64,96},{96,128},{128,160},{160,192},{192,224},{224... | collective-permute-start | bytes 49160 | tf_op jit(solution)/shard_map/ppermute | solution.py:23
  18.7 3.3 %collective-permute-start.6 = (f32[32,128]{1,0:T(8,128)S(1)}, f32[32,128]{1,0:T(8,128)S(1)}, u32[]{:S(2)}, u32[]{:S(2)}) collective-permute-start(f32[32,128]{1,0:T(8,128)S(1)} %collective-permute-done.2), channel_id=1, source_target_pairs={{0,224},{32,0},{64,32},{96,64},{128,96},{160,128},{192,160},{224,1... | collective-permute-start | bytes 49160 | tf_op jit(solution)/shard_map/ppermute | solution.py:23
  22.0 1.2 collective-permute-start.7
  23.2 1.5 %collective-permute-start.8 = (f32[32,128]{1,0:T(8,128)S(1)}, f32[32,128]{1,0:T(8,128)S(1)}, u32[]{:S(2)}, u32[]{:S(2)}) collective-permute-start(f32[32,128]{1,0:T(8,128)S(1)} %collective-permute-done.4), channel_id=1, source_target_pairs={{0,224},{32,0},{64,32},{96,64},{128,96},{160,128},{192,160},{224,1... | collective-permute-start | bytes 49160 | tf_op jit(solution)/shard_map/ppermute | solution.py:23
  24.7 2.2 %collective-permute-start.9 = (f32[32,128]{1,0:T(8,128)S(1)}, f32[32,128]{1,0:T(8,128)S(1)}, u32[]{:S(2)}, u32[]{:S(2)}) collective-permute-start(f32[32,128]{1,0:T(8,128)S(1)} %collective-permute-done.3), channel_id=1, source_target_pairs={{0,64},{32,96},{64,128},{96,160},{128,192},{160,224},{192,0},{224,... | collective-permute-start | bytes 49160 | tf_op jit(solution)/shard_map/ppermute | solution.py:23
  26.9 2.5 %collective-permute-done.9 = f32[32,128]{1,0:T(8,128)S(1)} collective-permute-done((f32[32,128]{1,0:T(8,128)S(1)}, f32[32,128]{1,0:T(8,128)S(1)}, u32[]{:S(2)}, u32[]{:S(2)}) %collective-permute-start.9) | collective-permute-done | bytes 16416 | tf_op jit(solution)/shard_map/ppermute | solution.py:23
  29.4 4.7 %collective-permute-start.10 = (f32[8,32,128]{2,1,0:T(8,128)S(1)}, f32[8,32,128]{2,1,0:T(8,128)S(1)}, u32[]{:S(2)}, u32[]{:S(2)}) collective-permute-start(f32[8,32,128]{2,1,0:T(8,128)S(1)} %bitcast_dynamic-update-slice_fusion.16), channel_id=1, source_target_pairs={{0,1},{1,0},{2,3},{3,2},{4,5},{5,4},{6,7},{7,6},{8,9},{9,8},{10,11... | collective-permute-start | bytes 393224 | tf_op jit(solution)/shard_map/ppermute | solution.py:27
  34.1 0.7 tile.4
  34.8 5.9 %all-to-all-start = ((f32[16,32,128]{2,1,0:T(8,128)}), f32[16,32,128]{2,1,0:T(8,128)S(1)}, u32[]{:S(2)}, u32[]{:S(2)}) async-start(f32[16,32,128]{2,1,0:T(8,128)} %bitcast.3), calls=%async_computation | async-start | bytes 524288 | tf_op jit(solution)/shard_map/all_to_all | solution.py:66
  40.9 8.6 %all-to-all-done = f32[16,32,128]{2,1,0:T(8,128)S(1)} async-done(((f32[16,32,128]{2,1,0:T(8,128)}), f32[16,32,128]{2,1,0:T(8,128)S(1)}, u32[]{:S(2)}, u32[]{:S(2)}) %all-to-all-start) | async-done | bytes 262176 | tf_op jit(solution)/shard_map/all_to_all | solution.py:66
  49.5 0.6 bitcast_dynamic-update-slice_fusion.15
  50.1 0.3 collective-permute-start.12
  50.4 3.4 %collective-permute-start.13 = (f32[128,128]{1,0:T(8,128)S(1)}, f32[128,128]{1,0:T(8,128)S(1)}, u32[]{:S(2)}, u32[]{:S(2)}) collective-permute-start(f32[128,128]{1,0:T(8,128)S(1)} %get-tuple-element.11.stat), channel_id=1, source_target_pairs={{0,192},{32,224},{64,0},{96,32},{128,64},{160,96},{192,128},{224,1... | collective-permute-start | bytes 196616 | tf_op jit(solution)/shard_map/ppermute | solution.py:23
  53.9 2.6 %collective-permute-start.15 = (f32[128,128]{1,0:T(8,128)S(1)}, f32[128,128]{1,0:T(8,128)S(1)}, u32[]{:S(2)}, u32[]{:S(2)}) collective-permute-start(f32[128,128]{1,0:T(8,128)S(1)} %get-tuple-element.11.stat), channel_id=1, source_target_pairs={{0,224},{32,0},{64,32},{96,64},{128,96},{160,128},{192,160},{224,1... | collective-permute-start | bytes 196616 | tf_op jit(solution)/shard_map/ppermute | solution.py:23
  56.5 1.1 broadcast_in_dim.96
  57.6 3.7 %all-to-all-start.1 = ((f32[16,128,128]{2,1,0:T(8,128)}), f32[16,128,128]{2,1,0:T(8,128)S(1)}, u32[]{:S(2)}, u32[]{:S(2)}) async-start(f32[16,128,128]{2,1,0:T(8,128)} %broadcast_in_dim.96), calls=%async_computation.1 | async-start | bytes 2097152 | tf_op jit(solution)/shard_map/all_to_all | solution.py:35
  61.3 1.7 %collective-permute-start.18 = (f32[128,128]{1,0:T(8,128)S(1)}, f32[128,128]{1,0:T(8,128)S(1)}, u32[]{:S(2)}, u32[]{:S(2)}) collective-permute-start(f32[128,128]{1,0:T(8,128)S(1)} %collective-permute-done.12), channel_id=1, source_target_pairs={{0,64},{32,96},{64,128},{96,160},{128,192},{160,224},{192,0},{224,... | collective-permute-start | bytes 196616 | tf_op jit(solution)/shard_map/ppermute | solution.py:23
  63.0 1.1 collective-permute-start.17
  64.2 1.5 %collective-permute-done.16 = f32[128,128]{1,0:T(8,128)S(1)} collective-permute-done((f32[128,128]{1,0:T(8,128)S(1)}, f32[128,128]{1,0:T(8,128)S(1)}, u32[]{:S(2)}, u32[]{:S(2)}) %collective-permute-start.16) | collective-permute-done | bytes 65568 | tf_op jit(solution)/shard_map/ppermute | solution.py:23
  65.7 1.8 %collective-permute-done.17 = f32[128,128]{1,0:T(8,128)S(1)} collective-permute-done((f32[128,128]{1,0:T(8,128)S(1)}, f32[128,128]{1,0:T(8,128)S(1)}, u32[]{:S(2)}, u32[]{:S(2)}) %collective-permute-start.17) | collective-permute-done | bytes 65568 | tf_op jit(solution)/shard_map/ppermute | solution.py:23
  67.5 3.6 %collective-permute-start.19 = (f32[8,128,128]{2,1,0:T(8,128)S(1)}, f32[8,128,128]{2,1,0:T(8,128)S(1)}, u32[]{:S(2)}, u32[]{:S(2)}) collective-permute-start(f32[8,128,128]{2,1,0:T(8,128)S(1)} %bitcast_dynamic-update-slice_fusion.8.mine_ref.stat_mine), channel_id=1, source_target_pairs={{0,1},{1,0},{2,3},{3,2},{4,5},{5,4},{6,7},{7,6},{8,9},{9,8},{10,11... | collective-permute-start | bytes 1572872 | tf_op jit(solution)/shard_map/ppermute | solution.py:27
  71.1 0.7 pad_add_fusion.core_ref.index_ref
  71.7 0.9 collective-permute-done.19.other_ref.stat_other
  72.6 3.7 %all-to-all-done.1.row_ref.stat_row = f32[16,128,128]{2,1,0:T(8,128)S(1)} async-done(((f32[16,128,128]{2,1,0:T(8,128)}), f32[16,128,128]{2,1,0:T(8,128)S(1)}, u32[]{:S(2)}, u32[]{:S(2)}) %all-to-all-start.1) | async-done | bytes 1048608 | tf_op jit(solution)/shard_map/all_to_all | solution.py:35
  76.3 1.0 copy-done
  77.3 3.2 %shard_map.41 = (f32[16,128,128]{2,1,0:T(8,128)}, f32[136,128]{1,0:T(8,128)}) custom-call(s32[3]{0:T(128)} %pad_add_fusion.core_ref.index_ref, f32[16,128,128]{2,1,0:T(8,128)} %copy-done, f32[8,128,128]{2,1,0:T(8,128)} %copy-done.1, f32[8,128,128]{2,1,0:T(8,128)} %copy-done.4), custom_call_target="tpu_custom_call" | custom-call | tf_op jit(solution)/shard_map/pallas_call | solution.py:144
  80.5 3.6 %collective-permute-start.21 = (f32[136,128]{1,0:T(8,128)}, f32[136,128]{1,0:T(8,128)S(1)}, u32[]{:S(2)}, u32[]{:S(2)}) collective-permute-start(f32[136,128]{1,0:T(8,128)} %get-tuple-element.5), channel_id=1, source_target_pairs={{0,192},{32,224},{64,0},{96,32},{128,64},{160,96},{192,128},{224,1... | collective-permute-start | bytes 208904 | tf_op jit(solution)/shard_map/ppermute | solution.py:23
  84.1 2.7 %collective-permute-start.23 = (f32[136,128]{1,0:T(8,128)}, f32[136,128]{1,0:T(8,128)S(1)}, u32[]{:S(2)}, u32[]{:S(2)}) collective-permute-start(f32[136,128]{1,0:T(8,128)} %get-tuple-element.5), channel_id=1, source_target_pairs={{0,224},{32,0},{64,32},{96,64},{128,96},{160,128},{192,160},{224,1... | collective-permute-start | bytes 208904 | tf_op jit(solution)/shard_map/ppermute | solution.py:23
  86.8 4.9 %all-to-all-start.2 = ((f32[16,128,128]{2,1,0:T(8,128)}), f32[16,128,128]{2,1,0:T(8,128)S(1)}, u32[]{:S(2)}, u32[]{:S(2)}) async-start(f32[16,128,128]{2,1,0:T(8,128)} %get-tuple-element.4), calls=%async_computation.2 | async-start | bytes 2097152 | tf_op jit(solution)/shard_map/all_to_all | solution.py:35
  91.7 0.8 copy-done.7
  92.6 1.7 %collective-permute-start.26 = (f32[136,128]{1,0:T(8,128)S(1)}, f32[136,128]{1,0:T(8,128)S(1)}, u32[]{:S(2)}, u32[]{:S(2)}) collective-permute-start(f32[136,128]{1,0:T(8,128)S(1)} %collective-permute-done.20), channel_id=1, source_target_pairs={{0,64},{32,96},{64,128},{96,160},{128,192},{160,224},{192,0},{224,... | collective-permute-start | bytes 208904 | tf_op jit(solution)/shard_map/ppermute | solution.py:23
  94.3 1.1 collective-permute-start.25
  95.4 1.5 %collective-permute-done.24 = f32[136,128]{1,0:T(8,128)S(1)} collective-permute-done((f32[136,128]{1,0:T(8,128)S(1)}, f32[136,128]{1,0:T(8,128)S(1)}, u32[]{:S(2)}, u32[]{:S(2)}) %collective-permute-start.24) | collective-permute-done | bytes 69664 | tf_op jit(solution)/shard_map/ppermute | solution.py:23
  97.0 1.8 %collective-permute-done.25 = f32[136,128]{1,0:T(8,128)S(1)} collective-permute-done((f32[136,128]{1,0:T(8,128)S(1)}, f32[136,128]{1,0:T(8,128)S(1)}, u32[]{:S(2)}, u32[]{:S(2)}) %collective-permute-start.25) | collective-permute-done | bytes 69664 | tf_op jit(solution)/shard_map/ppermute | solution.py:23
  98.8 4.7 %collective-permute-start.27 = (f32[8,136,128]{2,1,0:T(8,128)S(1)}, f32[8,136,128]{2,1,0:T(8,128)S(1)}, u32[]{:S(2)}, u32[]{:S(2)}) collective-permute-start(f32[8,136,128]{2,1,0:T(8,128)S(1)} %bitcast_dynamic-update-slice_fusion.square_mine), channel_id=1, source_target_pairs={{0,1},{1,0},{2,3},{3,2},{4,5},{5,4},{6,7},{7,6},{8,9},{9,8},{10,11... | collective-permute-start | bytes 1671176 | tf_op jit(solution)/shard_map/ppermute | solution.py:27
  103.5 3.3 %collective-permute-start.11 = (f32[128,128]{1,0:T(8,128)S(1)}, f32[128,128]{1,0:T(8,128)S(1)}, u32[]{:S(2)}, u32[]{:S(2)}) collective-permute-start(f32[128,128]{1,0:T(8,128)S(1)} %get-tuple-element.11.stat), channel_id=1, source_target_pairs={{0,0},{1,16},{16,1},{17,17},{2,2},{3,18},{18,3},{19,19},{4,4},{5,2... | collective-permute-start | bytes 196616 | tf_op jit(solution)/shard_map/ppermute | solution.py:31
  106.9 0.8 copy-done.6
  107.7 1.0 copy-done.2
  108.7 3.7 %shard_map.42 = f32[128,128]{1,0:T(8,128)} custom-call(s32[3]{0:T(128)} %pad_add_fusion.core_ref.index_ref, f32[16,128,128]{2,1,0:T(8,128)} %copy-done.2, f32[16,128,128]{2,1,0:T(8,128)} %copy-done, f32[8,136,128]{2,1,0:T(8,128)} %copy-done.3, f32[8,136,128]{2,1,0:T(8,128)} %copy-done.6, f32[8,128,128]{2,1,0:T(8,128)} %copy-done.1, ...), custom_call_target="tpu_custom_call" | custom-call | tf_op jit(solution)/shard_map/pallas_call | solution.py:144
  112.4 4.5 %collective-permute-start.28 = (f32[128,128]{1,0:T(8,128)}, f32[128,128]{1,0:T(8,128)S(1)}, u32[]{:S(2)}, u32[]{:S(2)}) collective-permute-start(f32[128,128]{1,0:T(8,128)} %shard_map.42), channel_id=1, source_target_pairs={{0,0},{1,16},{16,1},{17,17},{2,2},{3,18},{18,3},{19,19},{4,4},{5,2... | collective-permute-start | bytes 196616 | tf_op jit(solution)/shard_map/ppermute | solution.py:31
  116.9 2.1 %collective-permute-done.28 = f32[128,128]{1,0:T(8,128)S(1)} collective-permute-done((f32[128,128]{1,0:T(8,128)}, f32[128,128]{1,0:T(8,128)S(1)}, u32[]{:S(2)}, u32[]{:S(2)}) %collective-permute-start.28) | collective-permute-done | bytes 65568 | tf_op jit(solution)/shard_map/ppermute | solution.py:31
  119.1 0.6 copy.31
  119.7 0.6 copy.32
  (72 shorter events, 0.7 us)
Async XLA Ops:
  0.6 8.3 %collective-permute-start.2 = (f32[32,128]{1,0:T(8,128)}, f32[32,128]{1,0:T(8,128)S(1)}, u32[]{:S(2)}, u32[]{:S(2)}) collective-permute-start(f32[32,128]{1,0:T(8,128)} %bitcast.71), channel_id=1, source_target_pairs={{0,0},{1,1},{2,32},{3,33},{4,64},{5,65},{6,96},{7,97},{8,128},{9,1... | collective-permute-start | bytes 49160 | tf_op jit(solution)/shard_map/ppermute | solution.py:57
  2.0 32.1 %collective-permute-start.1 = (f32[32,128]{1,0:T(8,128)}, f32[32,128]{1,0:T(8,128)S(1)}, u32[]{:S(2)}, u32[]{:S(2)}) collective-permute-start(f32[32,128]{1,0:T(8,128)} %bitcast.72), channel_id=1, source_target_pairs={{0,16},{16,0},{1,17},{17,1},{2,18},{18,2},{3,19},{19,3},{4,20},{20... | collective-permute-start | bytes 49160 | tf_op jit(solution)/shard_map/ppermute | solution.py:27
  4.0 36.8 %collective-permute-start = (f32[128,128]{1,0:T(8,128)}, f32[128,128]{1,0:T(8,128)S(1)}, u32[]{:S(2)}, u32[]{:S(2)}) collective-permute-start(f32[128,128]{1,0:T(8,128)} %param.3), channel_id=1, source_target_pairs={{0,0},{1,16},{16,1},{17,17},{2,2},{3,18},{18,3},{19,19},{4,4},{5,2... | collective-permute-start | bytes 196616 | tf_op jit(solution)/shard_map/ppermute | solution.py:31
  8.9 9.8 %collective-permute-start.3 = (f32[32,128]{1,0:T(8,128)S(1)}, f32[32,128]{1,0:T(8,128)S(1)}, u32[]{:S(2)}, u32[]{:S(2)}) collective-permute-start(f32[32,128]{1,0:T(8,128)S(1)} %collective-permute-done.2), channel_id=1, source_target_pairs={{0,64},{32,96},{64,128},{96,160},{128,192},{160,224},{192,0},{224,... | collective-permute-start | bytes 49160 | tf_op jit(solution)/shard_map/ppermute | solution.py:23
  11.6 10.5 %collective-permute-start.4 = (f32[32,128]{1,0:T(8,128)S(1)}, f32[32,128]{1,0:T(8,128)S(1)}, u32[]{:S(2)}, u32[]{:S(2)}) collective-permute-start(f32[32,128]{1,0:T(8,128)S(1)} %collective-permute-done.2), channel_id=1, source_target_pairs={{0,192},{32,224},{64,0},{96,32},{128,64},{160,96},{192,128},{224,1... | collective-permute-start | bytes 49160 | tf_op jit(solution)/shard_map/ppermute | solution.py:23
  16.4 6.8 %collective-permute-start.5 = (f32[32,128]{1,0:T(8,128)S(1)}, f32[32,128]{1,0:T(8,128)S(1)}, u32[]{:S(2)}, u32[]{:S(2)}) collective-permute-start(f32[32,128]{1,0:T(8,128)S(1)} %collective-permute-done.2), channel_id=1, source_target_pairs={{0,32},{32,64},{64,96},{96,128},{128,160},{160,192},{192,224},{224... | collective-permute-start | bytes 49160 | tf_op jit(solution)/shard_map/ppermute | solution.py:23
  18.7 6.0 %collective-permute-start.6 = (f32[32,128]{1,0:T(8,128)S(1)}, f32[32,128]{1,0:T(8,128)S(1)}, u32[]{:S(2)}, u32[]{:S(2)}) collective-permute-start(f32[32,128]{1,0:T(8,128)S(1)} %collective-permute-done.2), channel_id=1, source_target_pairs={{0,224},{32,0},{64,32},{96,64},{128,96},{160,128},{192,160},{224,1... | collective-permute-start | bytes 49160 | tf_op jit(solution)/shard_map/ppermute | solution.py:23
  22.0 4.9 %collective-permute-start.7 = (f32[32,128]{1,0:T(8,128)S(1)}, f32[32,128]{1,0:T(8,128)S(1)}, u32[]{:S(2)}, u32[]{:S(2)}) collective-permute-start(f32[32,128]{1,0:T(8,128)S(1)} %collective-permute-done.3), channel_id=1, source_target_pairs={{0,32},{32,64},{64,96},{96,128},{128,160},{160,192},{192,224},{224... | collective-permute-start | bytes 49160 | tf_op jit(solution)/shard_map/ppermute | solution.py:23
  23.2 3.7 %collective-permute-start.8 = (f32[32,128]{1,0:T(8,128)S(1)}, f32[32,128]{1,0:T(8,128)S(1)}, u32[]{:S(2)}, u32[]{:S(2)}) collective-permute-start(f32[32,128]{1,0:T(8,128)S(1)} %collective-permute-done.4), channel_id=1, source_target_pairs={{0,224},{32,0},{64,32},{96,64},{128,96},{160,128},{192,160},{224,1... | collective-permute-start | bytes 49160 | tf_op jit(solution)/shard_map/ppermute | solution.py:23
  24.7 4.7 %collective-permute-start.9 = (f32[32,128]{1,0:T(8,128)S(1)}, f32[32,128]{1,0:T(8,128)S(1)}, u32[]{:S(2)}, u32[]{:S(2)}) collective-permute-start(f32[32,128]{1,0:T(8,128)S(1)} %collective-permute-done.3), channel_id=1, source_target_pairs={{0,64},{32,96},{64,128},{96,160},{128,192},{160,224},{192,0},{224,... | collective-permute-start | bytes 49160 | tf_op jit(solution)/shard_map/ppermute | solution.py:23
  26.9 7.2 %copy-start.8 = (f32[128,32]{0,1:T(8,128)S(1)}, f32[128,32]{0,1:T(8,128)}, u32[]{:S(2)}) copy-start(f32[128,32]{0,1:T(8,128)} %param.2) | copy-start | bytes 49156
  29.4 11.4 %collective-permute-start.10 = (f32[8,32,128]{2,1,0:T(8,128)S(1)}, f32[8,32,128]{2,1,0:T(8,128)S(1)}, u32[]{:S(2)}, u32[]{:S(2)}) collective-permute-start(f32[8,32,128]{2,1,0:T(8,128)S(1)} %bitcast_dynamic-update-slice_fusion.16), channel_id=1, source_target_pairs={{0,1},{1,0},{2,3},{3,2},{4,5},{5,4},{6,7},{7,6},{8,9},{9,8},{10,11... | collective-permute-start | bytes 393224 | tf_op jit(solution)/shard_map/ppermute | solution.py:27
  34.8 14.6 %all-to-all-start = ((f32[16,32,128]{2,1,0:T(8,128)}), f32[16,32,128]{2,1,0:T(8,128)S(1)}, u32[]{:S(2)}, u32[]{:S(2)}) async-start(f32[16,32,128]{2,1,0:T(8,128)} %bitcast.3), calls=%async_computation | async-start | bytes 524288 | tf_op jit(solution)/shard_map/all_to_all | solution.py:66
  50.1 53.4 %copy-start.5 = (f32[128,128]{1,0:T(8,128)}, f32[128,128]{1,0:T(8,128)S(1)}, u32[]{:S(2)}) copy-start(f32[128,128]{1,0:T(8,128)S(1)} %get-tuple-element.11.stat) | copy-start | bytes 196612
  50.1 11.1 %collective-permute-start.12 = (f32[128,128]{1,0:T(8,128)S(1)}, f32[128,128]{1,0:T(8,128)S(1)}, u32[]{:S(2)}, u32[]{:S(2)}) collective-permute-start(f32[128,128]{1,0:T(8,128)S(1)} %get-tuple-element.11.stat), channel_id=1, source_target_pairs={{0,64},{32,96},{64,128},{96,160},{128,192},{160,224},{192,0},{224,... | collective-permute-start | bytes 196616 | tf_op jit(solution)/shard_map/ppermute | solution.py:23
  50.4 12.6 %collective-permute-start.13 = (f32[128,128]{1,0:T(8,128)S(1)}, f32[128,128]{1,0:T(8,128)S(1)}, u32[]{:S(2)}, u32[]{:S(2)}) collective-permute-start(f32[128,128]{1,0:T(8,128)S(1)} %get-tuple-element.11.stat), channel_id=1, source_target_pairs={{0,192},{32,224},{64,0},{96,32},{128,64},{160,96},{192,128},{224,1... | collective-permute-start | bytes 196616 | tf_op jit(solution)/shard_map/ppermute | solution.py:23
  53.8 10.3 %collective-permute-start.14 = (f32[128,128]{1,0:T(8,128)S(1)}, f32[128,128]{1,0:T(8,128)S(1)}, u32[]{:S(2)}, u32[]{:S(2)}) collective-permute-start(f32[128,128]{1,0:T(8,128)S(1)} %get-tuple-element.11.stat), channel_id=1, source_target_pairs={{0,32},{32,64},{64,96},{96,128},{128,160},{160,192},{192,224},{224... | collective-permute-start | bytes 196616 | tf_op jit(solution)/shard_map/ppermute | solution.py:23
  53.9 10.2 %collective-permute-start.15 = (f32[128,128]{1,0:T(8,128)S(1)}, f32[128,128]{1,0:T(8,128)S(1)}, u32[]{:S(2)}, u32[]{:S(2)}) collective-permute-start(f32[128,128]{1,0:T(8,128)S(1)} %get-tuple-element.11.stat), channel_id=1, source_target_pairs={{0,224},{32,0},{64,32},{96,64},{128,96},{160,128},{192,160},{224,1... | collective-permute-start | bytes 196616 | tf_op jit(solution)/shard_map/ppermute | solution.py:23
  57.6 18.7 %all-to-all-start.1 = ((f32[16,128,128]{2,1,0:T(8,128)}), f32[16,128,128]{2,1,0:T(8,128)S(1)}, u32[]{:S(2)}, u32[]{:S(2)}) async-start(f32[16,128,128]{2,1,0:T(8,128)} %broadcast_in_dim.96), calls=%async_computation.1 | async-start | bytes 2097152 | tf_op jit(solution)/shard_map/all_to_all | solution.py:35
  61.2 4.4 %collective-permute-start.16 = (f32[128,128]{1,0:T(8,128)S(1)}, f32[128,128]{1,0:T(8,128)S(1)}, u32[]{:S(2)}, u32[]{:S(2)}) collective-permute-start(f32[128,128]{1,0:T(8,128)S(1)} %collective-permute-done.12), channel_id=1, source_target_pairs={{0,32},{32,64},{64,96},{96,128},{128,160},{160,192},{192,224},{224... | collective-permute-start | bytes 196616 | tf_op jit(solution)/shard_map/ppermute | solution.py:23
  61.3 6.1 %collective-permute-start.18 = (f32[128,128]{1,0:T(8,128)S(1)}, f32[128,128]{1,0:T(8,128)S(1)}, u32[]{:S(2)}, u32[]{:S(2)}) collective-permute-start(f32[128,128]{1,0:T(8,128)S(1)} %collective-permute-done.12), channel_id=1, source_target_pairs={{0,64},{32,96},{64,128},{96,160},{128,192},{160,224},{192,0},{224,... | collective-permute-start | bytes 196616 | tf_op jit(solution)/shard_map/ppermute | solution.py:23
  63.0 4.4 %collective-permute-start.17 = (f32[128,128]{1,0:T(8,128)S(1)}, f32[128,128]{1,0:T(8,128)S(1)}, u32[]{:S(2)}, u32[]{:S(2)}) collective-permute-start(f32[128,128]{1,0:T(8,128)S(1)} %collective-permute-done.13), channel_id=1, source_target_pairs={{0,224},{32,0},{64,32},{96,64},{128,96},{160,128},{192,160},{224,1... | collective-permute-start | bytes 196616 | tf_op jit(solution)/shard_map/ppermute | solution.py:23
  67.5 8.8 %copy-start.1 = (f32[8,128,128]{2,1,0:T(8,128)}, f32[8,128,128]{2,1,0:T(8,128)S(1)}, u32[]{:S(2)}) copy-start(f32[8,128,128]{2,1,0:T(8,128)S(1)} %bitcast_dynamic-update-slice_fusion.8.mine_ref.stat_mine) | copy-start | bytes 1572868
  67.5 5.1 %collective-permute-start.19 = (f32[8,128,128]{2,1,0:T(8,128)S(1)}, f32[8,128,128]{2,1,0:T(8,128)S(1)}, u32[]{:S(2)}, u32[]{:S(2)}) collective-permute-start(f32[8,128,128]{2,1,0:T(8,128)S(1)} %bitcast_dynamic-update-slice_fusion.8.mine_ref.stat_mine), channel_id=1, source_target_pairs={{0,1},{1,0},{2,3},{3,2},{4,5},{5,4},{6,7},{7,6},{8,9},{9,8},{10,11... | collective-permute-start | bytes 1572872 | tf_op jit(solution)/shard_map/ppermute | solution.py:27
  72.6 3.7 %copy-start.4 = (f32[8,128,128]{2,1,0:T(8,128)}, f32[8,128,128]{2,1,0:T(8,128)S(1)}, u32[]{:S(2)}) copy-start(f32[8,128,128]{2,1,0:T(8,128)S(1)} %collective-permute-done.19.other_ref.stat_other) | copy-start | bytes 1572868
  76.3 1.0 copy-start
  80.5 12.0 %collective-permute-start.20 = (f32[136,128]{1,0:T(8,128)}, f32[136,128]{1,0:T(8,128)S(1)}, u32[]{:S(2)}, u32[]{:S(2)}) collective-permute-start(f32[136,128]{1,0:T(8,128)} %get-tuple-element.5), channel_id=1, source_target_pairs={{0,64},{32,96},{64,128},{96,160},{128,192},{160,224},{192,0},{224,... | collective-permute-start | bytes 208904 | tf_op jit(solution)/shard_map/ppermute | solution.py:23
  80.5 13.8 %collective-permute-start.21 = (f32[136,128]{1,0:T(8,128)}, f32[136,128]{1,0:T(8,128)S(1)}, u32[]{:S(2)}, u32[]{:S(2)}) collective-permute-start(f32[136,128]{1,0:T(8,128)} %get-tuple-element.5), channel_id=1, source_target_pairs={{0,192},{32,224},{64,0},{96,32},{128,64},{160,96},{192,128},{224,1... | collective-permute-start | bytes 208904 | tf_op jit(solution)/shard_map/ppermute | solution.py:23
  84.1 11.3 %collective-permute-start.22 = (f32[136,128]{1,0:T(8,128)}, f32[136,128]{1,0:T(8,128)S(1)}, u32[]{:S(2)}, u32[]{:S(2)}) collective-permute-start(f32[136,128]{1,0:T(8,128)} %get-tuple-element.5), channel_id=1, source_target_pairs={{0,32},{32,64},{64,96},{96,128},{128,160},{160,192},{192,224},{224... | collective-permute-start | bytes 208904 | tf_op jit(solution)/shard_map/ppermute | solution.py:23
  84.1 11.3 %collective-permute-start.23 = (f32[136,128]{1,0:T(8,128)}, f32[136,128]{1,0:T(8,128)S(1)}, u32[]{:S(2)}, u32[]{:S(2)}) collective-permute-start(f32[136,128]{1,0:T(8,128)} %get-tuple-element.5), channel_id=1, source_target_pairs={{0,224},{32,0},{64,32},{96,64},{128,96},{160,128},{192,160},{224,1... | collective-permute-start | bytes 208904 | tf_op jit(solution)/shard_map/ppermute | solution.py:23
  86.8 20.2 %all-to-all-start.2 = ((f32[16,128,128]{2,1,0:T(8,128)}), f32[16,128,128]{2,1,0:T(8,128)S(1)}, u32[]{:S(2)}, u32[]{:S(2)}) async-start(f32[16,128,128]{2,1,0:T(8,128)} %get-tuple-element.4), calls=%async_computation.2 | async-start | bytes 2097152 | tf_op jit(solution)/shard_map/all_to_all | solution.py:35
  91.6 0.9 copy-start.7
  92.5 4.4 %collective-permute-start.24 = (f32[136,128]{1,0:T(8,128)S(1)}, f32[136,128]{1,0:T(8,128)S(1)}, u32[]{:S(2)}, u32[]{:S(2)}) collective-permute-start(f32[136,128]{1,0:T(8,128)S(1)} %collective-permute-done.20), channel_id=1, source_target_pairs={{0,32},{32,64},{64,96},{96,128},{128,160},{160,192},{192,224},{224... | collective-permute-start | bytes 208904 | tf_op jit(solution)/shard_map/ppermute | solution.py:23
  92.6 6.2 %collective-permute-start.26 = (f32[136,128]{1,0:T(8,128)S(1)}, f32[136,128]{1,0:T(8,128)S(1)}, u32[]{:S(2)}, u32[]{:S(2)}) collective-permute-start(f32[136,128]{1,0:T(8,128)S(1)} %collective-permute-done.20), channel_id=1, source_target_pairs={{0,64},{32,96},{64,128},{96,160},{128,192},{160,224},{192,0},{224,... | collective-permute-start | bytes 208904 | tf_op jit(solution)/shard_map/ppermute | solution.py:23
  94.3 4.5 %collective-permute-start.25 = (f32[136,128]{1,0:T(8,128)S(1)}, f32[136,128]{1,0:T(8,128)S(1)}, u32[]{:S(2)}, u32[]{:S(2)}) collective-permute-start(f32[136,128]{1,0:T(8,128)S(1)} %collective-permute-done.21), channel_id=1, source_target_pairs={{0,224},{32,0},{64,32},{96,64},{128,96},{160,128},{192,160},{224,1... | collective-permute-start | bytes 208904 | tf_op jit(solution)/shard_map/ppermute | solution.py:23
  98.8 8.1 %copy-start.3 = (f32[8,136,128]{2,1,0:T(8,128)}, f32[8,136,128]{2,1,0:T(8,128)S(1)}, u32[]{:S(2)}) copy-start(f32[8,136,128]{2,1,0:T(8,128)S(1)} %bitcast_dynamic-update-slice_fusion.square_mine) | copy-start | bytes 1671172
  98.8 8.1 %collective-permute-start.27 = (f32[8,136,128]{2,1,0:T(8,128)S(1)}, f32[8,136,128]{2,1,0:T(8,128)S(1)}, u32[]{:S(2)}, u32[]{:S(2)}) collective-permute-start(f32[8,136,128]{2,1,0:T(8,128)S(1)} %bitcast_dynamic-update-slice_fusion.square_mine), channel_id=1, source_target_pairs={{0,1},{1,0},{2,3},{3,2},{4,5},{5,4},{6,7},{7,6},{8,9},{9,8},{10,11... | collective-permute-start | bytes 1671176 | tf_op jit(solution)/shard_map/ppermute | solution.py:27
  103.5 13.4 %collective-permute-start.11 = (f32[128,128]{1,0:T(8,128)S(1)}, f32[128,128]{1,0:T(8,128)S(1)}, u32[]{:S(2)}, u32[]{:S(2)}) collective-permute-start(f32[128,128]{1,0:T(8,128)S(1)} %get-tuple-element.11.stat), channel_id=1, source_target_pairs={{0,0},{1,16},{16,1},{17,17},{2,2},{3,18},{18,3},{19,19},{4,4},{5,2... | collective-permute-start | bytes 196616 | tf_op jit(solution)/shard_map/ppermute | solution.py:31
  106.9 0.8 copy-start.6
  107.7 1.0 copy-start.2
  112.4 6.7 %collective-permute-start.28 = (f32[128,128]{1,0:T(8,128)}, f32[128,128]{1,0:T(8,128)S(1)}, u32[]{:S(2)}, u32[]{:S(2)}) collective-permute-start(f32[128,128]{1,0:T(8,128)} %shard_map.42), channel_id=1, source_target_pairs={{0,0},{1,16},{16,1},{17,17},{2,2},{3,18},{18,3},{19,19},{4,4},{5,2... | collective-permute-start | bytes 196616 | tf_op jit(solution)/shard_map/ppermute | solution.py:31

commit v2 on v1

--- a/solution.py
+++ b/solution.py
@@ -10,6 +10,7 @@
 Z, XL, Y, XH, CORE = "gx_0", "gx_1", "gy_0", "gy_1", "gy_2"
 GX = (Z, XL)
 GY = (Y, XH, CORE)
+VMEM_BYTES = 20 * 1024 * 1024
 
 
 def matmul(leading, trailing):
@@ -46,7 +47,8 @@
     mine = jnp.zeros((8,) + block.shape, block.dtype)
     for shift, piece in found.items():
         mine = lax.dynamic_update_slice(mine, piece[None], ((place - shift) % 8, 0, 0))
-    return mine, swap(mine, CORE)
+    other = swap(mine, CORE)
+    return jnp.concatenate((mine, other), axis=0)
 
 
 def exchange(array):
@@ -64,7 +66,8 @@
     at_high = lax.axis_index(XL) == 1
     pair = jnp.stack((jnp.where(at_high, beside, piece), jnp.where(at_high, piece, beside)))
     rows_of = lax.all_to_all(jnp.tile(pair, (8, 1, 1)), GY, 0, 0, tiled=True)
-    mine, other = column_pieces(moved)
+    pieces = column_pieces(moved)
+    mine, other = pieces[:8], pieces[8:]
     core = lax.axis_index(CORE)
     columns_of = jnp.stack(
         (jnp.where(core == 0, mine, other), jnp.where(core == 0, other, mine)), axis=1
@@ -88,17 +91,17 @@
     return dot(left_high, right_high) + (dot(left_high, right_low) + dot(left_low, right_high))
 
 
-def square_kernel(core_ref, row_ref, mine_ref, other_ref, copies_ref, carried_ref):
-    core = core_ref[0]
-    side = mine_ref.shape[1]
-    total = jnp.zeros((side, mine_ref.shape[2]), jnp.float32)
+def square_kernel(row_ref, column_ref, copies_ref, carried_ref):
+    core = lax.axis_index(CORE)
+    places, side = column_ref.shape[0] // 2, column_ref.shape[1]
+    total = jnp.zeros((side, side), jnp.float32)
     norms = jnp.zeros((side, side), jnp.float32)
-    for place in range(mine_ref.shape[0]):
+    for place in range(places):
         first = row_ref[2 * place + core]
         second = row_ref[2 * place + 1 - core]
         total = total + product(
             jnp.concatenate((first, second), axis=1),
-            jnp.concatenate((mine_ref[place], other_ref[place]), axis=0),
+            jnp.concatenate((column_ref[place], column_ref[places + place]), axis=0),
         )
         norms = norms + first * first + second * second
     for number in range(copies_ref.shape[0]):
@@ -108,13 +111,16 @@
 
 
 def root_kernel(
-    index_ref, square_row, stat_row, square_mine, square_other, stat_mine, stat_other, stat, out
+    square_row, stat_row, square_column, stat_column, stat, home, out, kept
 ):
-    core, row_block, column_block = index_ref[0], index_ref[1], index_ref[2]
-    places, side = stat_mine.shape[0], stat.shape[0]
+    core = lax.axis_index(CORE)
+    row_block = 2 * lax.axis_index(Z) + core
+    column_block = 4 * lax.axis_index(Y) + 2 * lax.axis_index(XH) + lax.axis_index(XL)
+    kept[...] = home[...]
+    places, side = stat_column.shape[0] // 2, stat.shape[0]
     sums = jnp.zeros((8, side), jnp.float32)
-    for place in range(places):
-        sums = sums + square_mine[place, side : side + 8] + square_other[place, side : side + 8]
+    for place in range(2 * places):
+        sums = sums + square_column[place, side : side + 8]
     divisor = 2.0 * jnp.sqrt(sums[:1] / (2 * places * side))
     inverse = 1.0 / divisor
     across = lax.broadcasted_iota(jnp.int32, (side, side), 0)
@@ -128,63 +134,51 @@
     total = jnp.zeros((side, side), jnp.float32)
     for place in range(places):
         lefts, rights = [], []
-        for part, square, plain in ((core, square_mine, stat_mine), (1 - core, square_other, stat_other)):
+        for part, piece in ((core, place), (1 - core, places + place)):
             number = 2 * place + part
             lefts.append(quadratic(square_row[number], stat_row[number], number == row_block))
-            rights.append(quadratic(square[place, :side], plain[place], number == column_block))
+            rights.append(quadratic(square_column[piece, :side], stat_column[piece], number == column_block))
         total = total + product(jnp.concatenate(lefts, axis=1), jnp.concatenate(rights, axis=0))
     constant = jnp.where(row_block == column_block, 1.5380859375, 0.0) * eye
     out[...] = 0.0625 * total - (0.5390625 * inverse) * stat[...] + constant
 
 
 def call(kernel, outs, *operands):
-    spaces = [pl.BlockSpec(memory_space=pltpu.SMEM)] + [
-        pl.BlockSpec(memory_space=pltpu.VMEM) for _ in operands[1:]
-    ]
     return pl.pallas_call(
         kernel,
         out_shape=[jax.ShapeDtypeStruct(shape, jnp.float32) for shape in outs],
-        in_specs=spaces,
+        in_specs=[pl.BlockSpec(memory_space=pltpu.VMEM) for _ in operands],
         out_specs=[pl.BlockSpec(memory_space=pltpu.VMEM) for _ in outs],
+        compiler_params=pltpu.CompilerParams(vmem_limit_bytes=VMEM_BYTES),
     )(*operands)
 
 
 def local(gradient, stat_old):
     side = stat_old.shape[0]
-    core = lax.axis_index(CORE)
-    row_block = 2 * lax.axis_index(Z) + core
-    column_block = 4 * lax.axis_index(Y) + 2 * lax.axis_index(XH) + lax.axis_index(XL)
-
-    indices = jnp.stack((core, row_block, column_block))
-
     outer = outer_part(gradient)
     stat_moved = turn(stat_old)
     stat = 0.9 * stat_moved + outer / (gradient.shape[1] * 16)
 
     stat_row = row_panel(jnp.broadcast_to(stat[None], (16,) + stat.shape))
-    stat_mine, stat_other = column_pieces(stat)
-    statistic = turn(stat)
+    stat_column = column_pieces(stat)
+    home = turn(stat)
     copies, carried = call(
         square_kernel,
         ((16, side, side), (side + 8, side)),
-        indices,
         stat_row,
-        stat_mine,
-        stat_other,
+        stat_column,
     )
     square_row = row_panel(copies)
-    square_mine, square_other = column_pieces(carried)
-    (result,) = call(
+    square_column = column_pieces(carried)
+    result, statistic = call(
         root_kernel,
-        ((side, side),),
-        indices,
+        ((side, side), (side, side)),
         square_row,
         stat_row,
-        square_mine,
-        square_other,
-        stat_mine,
-        stat_other,
+        square_column,
+        stat_column,
         stat,
+        home,
     )
     return (statistic, turn(result))
 

time: 121 us -> 117 us (0.967)
  local copies, waits for them, and re-layouts: 6.99 us -> 2.7 us
  waiting for transfers between devices: 24.4 us -> 27.9 us
  Pallas kernels: 6.9 us -> 4.33 us
    unnamed x20 -> x1, local copies, waits for them, and re-layouts: 4.89 us -> 0.63 us
    ppermute x3, waiting for transfers between devices: 2.14 us -> 5.03 us  [turn(): return lax.ppermute(array, (XL, CORE), [(0, 0), (1, 2), (2, 1), (3, 3)])]
    pallas_call x2, Pallas kernels: 6.9 us -> 4.33 us  [call(): pl.pallas_call(kernel, out_shape=[jax.ShapeDtypeStruct(shape, jnp.float32...]
    ppermute x3, starting transfers between devices: 12.5 us -> 11.1 us  [turn(): return lax.ppermute(array, (XL, CORE), [(0, 0), (1, 2), (2, 1), (3, 3)])]
  transfers between devices with their start and end apart: 32 -> 32, of which waited for: 9 -> 10; matrix products, arithmetic and copies ran while one was open for 2% -> 3% of each run, Pallas kernels for 3% -> 0%
where the time goes in v2:
time: 117 us; the launch traced here: 116 us
  starting transfers between devices  78.8 us (67%)
  waiting for transfers between devices  27.9 us (24%)
  Pallas kernels  4.33 us (4%)
  local copies, waits for them, and re-layouts  2.7 us (2%)
    ppermute x21, starting transfers between devices, rotate(): lax.ppermute(array, axis, [(s, (s + shift) % size) for s in range(size)])  36.2 us
    ppermute x4, starting transfers between devices, swap(): return lax.ppermute(array, axis, [(0, 1), (1, 0)])  15.6 us
    ppermute x3, starting transfers between devices, turn(): return lax.ppermute(array, (XL, CORE), [(0, 0), (1, 2), (2, 1), (3, 3)])  11.1 us
    ppermute x21, waiting for transfers between devices, rotate(): lax.ppermute(array, axis, [(s, (s + shift) % size) for s in range(size)])  9.07 us
    all_to_all x1, waiting for transfers between devices, outer_part(): rows_of = lax.all_to_all(jnp.tile(pair, (8, 1, 1)), GY, 0, 0, tiled=True)  8.62 us
    all_to_all x2, starting transfers between devices, row_panel(): return lax.all_to_all(copies, (Y, XH, XL), 0, 0, tiled=True)  8.55 us
    all_to_all x1, starting transfers between devices, outer_part(): rows_of = lax.all_to_all(jnp.tile(pair, (8, 1, 1)), GY, 0, 0, tiled=True)  5.94 us
    ppermute x3, waiting for transfers between devices, turn(): return lax.ppermute(array, (XL, CORE), [(0, 0), (1, 2), (2, 1), (3, 3)])  5.03 us
  transfers between devices with their start and end apart: 32, of which 10 were waited for; matrix products, arithmetic and copies ran while one was open for 3% of the time, Pallas kernels for 0%

profile of v2, /device:TPU:1, one launch (start us, length us, event | category | flops | bytes accessed | tf_op | source)
XLA Modules:
  0.0 116.3 jit_solution(14390548607910274090)
XLA Ops:
  0.6 1.4 %collective-permute-start.2 = (f32[32,128]{1,0:T(8,128)}, f32[32,128]{1,0:T(8,128)S(1)}, u32[]{:S(2)}, u32[]{:S(2)}) collective-permute-start(f32[32,128]{1,0:T(8,128)} %bitcast.68), channel_id=1, source_target_pairs={{0,0},{1,1},{2,32},{3,33},{4,64},{5,65},{6,96},{7,97},{8,128},{9,1... | collective-permute-start | bytes 49160 | tf_op jit(solution)/shard_map/ppermute | solution.py:59
  2.0 2.0 %collective-permute-start.1 = (f32[32,128]{1,0:T(8,128)}, f32[32,128]{1,0:T(8,128)S(1)}, u32[]{:S(2)}, u32[]{:S(2)}) collective-permute-start(f32[32,128]{1,0:T(8,128)} %bitcast.69), channel_id=1, source_target_pairs={{0,16},{16,0},{1,17},{17,1},{2,18},{18,2},{3,19},{19,3},{4,20},{20... | collective-permute-start | bytes 49160 | tf_op jit(solution)/shard_map/ppermute | solution.py:28
  4.0 4.7 %collective-permute-start = (f32[128,128]{1,0:T(8,128)}, f32[128,128]{1,0:T(8,128)S(1)}, u32[]{:S(2)}, u32[]{:S(2)}) collective-permute-start(f32[128,128]{1,0:T(8,128)} %param.3), channel_id=1, source_target_pairs={{0,0},{1,16},{16,1},{17,17},{2,2},{3,18},{18,3},{19,19},{4,4},{5,2... | collective-permute-start | bytes 196616 | tf_op jit(solution)/shard_map/ppermute | solution.py:32
  8.9 2.7 %collective-permute-start.3 = (f32[32,128]{1,0:T(8,128)S(1)}, f32[32,128]{1,0:T(8,128)S(1)}, u32[]{:S(2)}, u32[]{:S(2)}) collective-permute-start(f32[32,128]{1,0:T(8,128)S(1)} %collective-permute-done.2), channel_id=1, source_target_pairs={{0,64},{32,96},{64,128},{96,160},{128,192},{160,224},{192,0},{224,... | collective-permute-start | bytes 49160 | tf_op jit(solution)/shard_map/ppermute | solution.py:24
  11.5 4.8 %collective-permute-start.4 = (f32[32,128]{1,0:T(8,128)S(1)}, f32[32,128]{1,0:T(8,128)S(1)}, u32[]{:S(2)}, u32[]{:S(2)}) collective-permute-start(f32[32,128]{1,0:T(8,128)S(1)} %collective-permute-done.2), channel_id=1, source_target_pairs={{0,192},{32,224},{64,0},{96,32},{128,64},{160,96},{192,128},{224,1... | collective-permute-start | bytes 49160 | tf_op jit(solution)/shard_map/ppermute | solution.py:24
  16.4 2.2 %collective-permute-start.5 = (f32[32,128]{1,0:T(8,128)S(1)}, f32[32,128]{1,0:T(8,128)S(1)}, u32[]{:S(2)}, u32[]{:S(2)}) collective-permute-start(f32[32,128]{1,0:T(8,128)S(1)} %collective-permute-done.2), channel_id=1, source_target_pairs={{0,32},{32,64},{64,96},{96,128},{128,160},{160,192},{192,224},{224... | collective-permute-start | bytes 49160 | tf_op jit(solution)/shard_map/ppermute | solution.py:24
  18.7 3.3 %collective-permute-start.6 = (f32[32,128]{1,0:T(8,128)S(1)}, f32[32,128]{1,0:T(8,128)S(1)}, u32[]{:S(2)}, u32[]{:S(2)}) collective-permute-start(f32[32,128]{1,0:T(8,128)S(1)} %collective-permute-done.2), channel_id=1, source_target_pairs={{0,224},{32,0},{64,32},{96,64},{128,96},{160,128},{192,160},{224,1... | collective-permute-start | bytes 49160 | tf_op jit(solution)/shard_map/ppermute | solution.py:24
  22.0 1.2 %collective-permute-start.7 = (f32[32,128]{1,0:T(8,128)S(1)}, f32[32,128]{1,0:T(8,128)S(1)}, u32[]{:S(2)}, u32[]{:S(2)}) collective-permute-start(f32[32,128]{1,0:T(8,128)S(1)} %collective-permute-done.3), channel_id=1, source_target_pairs={{0,32},{32,64},{64,96},{96,128},{128,160},{160,192},{192,224},{224... | collective-permute-start | bytes 49160 | tf_op jit(solution)/shard_map/ppermute | solution.py:24
  23.2 1.5 %collective-permute-start.8 = (f32[32,128]{1,0:T(8,128)S(1)}, f32[32,128]{1,0:T(8,128)S(1)}, u32[]{:S(2)}, u32[]{:S(2)}) collective-permute-start(f32[32,128]{1,0:T(8,128)S(1)} %collective-permute-done.4), channel_id=1, source_target_pairs={{0,224},{32,0},{64,32},{96,64},{128,96},{160,128},{192,160},{224,1... | collective-permute-start | bytes 49160 | tf_op jit(solution)/shard_map/ppermute | solution.py:24
  24.7 2.2 %collective-permute-start.9 = (f32[32,128]{1,0:T(8,128)S(1)}, f32[32,128]{1,0:T(8,128)S(1)}, u32[]{:S(2)}, u32[]{:S(2)}) collective-permute-start(f32[32,128]{1,0:T(8,128)S(1)} %collective-permute-done.3), channel_id=1, source_target_pairs={{0,64},{32,96},{64,128},{96,160},{128,192},{160,224},{192,0},{224,... | collective-permute-start | bytes 49160 | tf_op jit(solution)/shard_map/ppermute | solution.py:24
  26.9 2.5 %collective-permute-done.9 = f32[32,128]{1,0:T(8,128)S(1)} collective-permute-done((f32[32,128]{1,0:T(8,128)S(1)}, f32[32,128]{1,0:T(8,128)S(1)}, u32[]{:S(2)}, u32[]{:S(2)}) %collective-permute-start.9) | collective-permute-done | bytes 16416 | tf_op jit(solution)/shard_map/ppermute | solution.py:24
  29.4 4.7 %collective-permute-start.10 = (f32[8,32,128]{2,1,0:T(8,128)S(1)}, f32[8,32,128]{2,1,0:T(8,128)S(1)}, u32[]{:S(2)}, u32[]{:S(2)}) collective-permute-start(f32[8,32,128]{2,1,0:T(8,128)S(1)} %bitcast_dynamic-update-slice_fusion.16), channel_id=1, source_target_pairs={{0,1},{1,0},{2,3},{3,2},{4,5},{5,4},{6,7},{7,6},{8,9},{9,8},{10,11... | collective-permute-start | bytes 393224 | tf_op jit(solution)/shard_map/ppermute | solution.py:28
  34.1 0.7 select_bitcast_fusion.3
  34.8 0.7 tile.4
  35.5 5.9 %all-to-all-start = ((f32[16,32,128]{2,1,0:T(8,128)}), f32[16,32,128]{2,1,0:T(8,128)S(1)}, u32[]{:S(2)}, u32[]{:S(2)}) async-start(f32[16,32,128]{2,1,0:T(8,128)} %bitcast.3), calls=%async_computation | async-start | bytes 524288 | tf_op jit(solution)/shard_map/all_to_all | solution.py:68
  41.5 8.6 %all-to-all-done = f32[16,32,128]{2,1,0:T(8,128)S(1)} async-done(((f32[16,32,128]{2,1,0:T(8,128)}), f32[16,32,128]{2,1,0:T(8,128)S(1)}, u32[]{:S(2)}, u32[]{:S(2)}) %all-to-all-start) | async-done | bytes 262176 | tf_op jit(solution)/shard_map/all_to_all | solution.py:68
  50.2 0.6 bitcast_dynamic-update-slice_fusion.15
  50.8 0.3 collective-permute-start.11
  51.1 3.4 %collective-permute-start.12 = (f32[128,128]{1,0:T(8,128)S(1)}, f32[128,128]{1,0:T(8,128)S(1)}, u32[]{:S(2)}, u32[]{:S(2)}) collective-permute-start(f32[128,128]{1,0:T(8,128)S(1)} %get-tuple-element.15.stat), channel_id=1, source_target_pairs={{0,192},{32,224},{64,0},{96,32},{128,64},{160,96},{192,128},{224,1... | collective-permute-start | bytes 196616 | tf_op jit(solution)/shard_map/ppermute | solution.py:24
  54.5 0.1 collective-permute-start.13
  54.6 2.6 %collective-permute-start.14 = (f32[128,128]{1,0:T(8,128)S(1)}, f32[128,128]{1,0:T(8,128)S(1)}, u32[]{:S(2)}, u32[]{:S(2)}) collective-permute-start(f32[128,128]{1,0:T(8,128)S(1)} %get-tuple-element.15.stat), channel_id=1, source_target_pairs={{0,224},{32,0},{64,32},{96,64},{128,96},{160,128},{192,160},{224,1... | collective-permute-start | bytes 196616 | tf_op jit(solution)/shard_map/ppermute | solution.py:24
  57.1 1.1 broadcast_in_dim.96
  58.2 3.7 %all-to-all-start.1 = ((f32[16,128,128]{2,1,0:T(8,128)}), f32[16,128,128]{2,1,0:T(8,128)S(1)}, u32[]{:S(2)}, u32[]{:S(2)}) async-start(f32[16,128,128]{2,1,0:T(8,128)} %broadcast_in_dim.96), calls=%async_computation.1 | async-start | bytes 2097152 | tf_op jit(solution)/shard_map/all_to_all | solution.py:36
  61.9 0.1 collective-permute-start.15
  62.0 1.7 %collective-permute-start.17 = (f32[128,128]{1,0:T(8,128)S(1)}, f32[128,128]{1,0:T(8,128)S(1)}, u32[]{:S(2)}, u32[]{:S(2)}) collective-permute-start(f32[128,128]{1,0:T(8,128)S(1)} %collective-permute-done.11), channel_id=1, source_target_pairs={{0,64},{32,96},{64,128},{96,160},{128,192},{160,224},{192,0},{224,... | collective-permute-start | bytes 196616 | tf_op jit(solution)/shard_map/ppermute | solution.py:24
  63.7 1.1 collective-permute-start.16
  64.8 1.5 %collective-permute-done.15 = f32[128,128]{1,0:T(8,128)S(1)} collective-permute-done((f32[128,128]{1,0:T(8,128)S(1)}, f32[128,128]{1,0:T(8,128)S(1)}, u32[]{:S(2)}, u32[]{:S(2)}) %collective-permute-start.15) | collective-permute-done | bytes 65568 | tf_op jit(solution)/shard_map/ppermute | solution.py:24
  66.3 1.8 %collective-permute-done.16 = f32[128,128]{1,0:T(8,128)S(1)} collective-permute-done((f32[128,128]{1,0:T(8,128)S(1)}, f32[128,128]{1,0:T(8,128)S(1)}, u32[]{:S(2)}, u32[]{:S(2)}) %collective-permute-start.16) | collective-permute-done | bytes 65568 | tf_op jit(solution)/shard_map/ppermute | solution.py:24
  68.1 3.6 %collective-permute-start.18 = (f32[8,128,128]{2,1,0:T(8,128)S(1)}, f32[8,128,128]{2,1,0:T(8,128)S(1)}, u32[]{:S(2)}, u32[]{:S(2)}) collective-permute-start(f32[8,128,128]{2,1,0:T(8,128)S(1)} %bitcast_dynamic-update-slice_fusion.8), channel_id=1, source_target_pairs={{0,1},{1,0},{2,3},{3,2},{4,5},{5,4},{6,7},{7,6},{8,9},{9,8},{10,11... | collective-permute-start | bytes 1572872 | tf_op jit(solution)/shard_map/ppermute | solution.py:28
  71.7 1.5 %collective-permute-done.18 = f32[8,128,128]{2,1,0:T(8,128)S(1)} collective-permute-done((f32[8,128,128]{2,1,0:T(8,128)S(1)}, f32[8,128,128]{2,1,0:T(8,128)S(1)}, u32[]{:S(2)}, u32[]{:S(2)}) %collective-permute-start.18) | collective-permute-done | bytes 524320 | tf_op jit(solution)/shard_map/ppermute | solution.py:28
  73.2 0.1 pad_maximum_fusion.1.column_ref.stat_column
  73.3 3.6 %all-to-all-done.1.row_ref.stat_row = f32[16,128,128]{2,1,0:T(8,128)S(1)} async-done(((f32[16,128,128]{2,1,0:T(8,128)}), f32[16,128,128]{2,1,0:T(8,128)S(1)}, u32[]{:S(2)}, u32[]{:S(2)}) %all-to-all-start.1) | async-done | bytes 1048608 | tf_op jit(solution)/shard_map/all_to_all | solution.py:36
  76.9 1.6 %shard_map.41 = (f32[16,128,128]{2,1,0:T(8,128)}, f32[136,128]{1,0:T(8,128)S(1)}) custom-call(f32[16,128,128]{2,1,0:T(8,128)S(1)} %all-to-all-done.1.row_ref.stat_row, f32[16,128,128]{2,1,0:T(8,128)S(1)} %pad_maximum_fusion.1.column_ref.stat_column), custom_call_target="tpu_custom_call" | custom-call | tf_op jit(solution)/shard_map/pallas_call | solution.py:147
  78.6 3.6 %collective-permute-start.20 = (f32[136,128]{1,0:T(8,128)S(1)}, f32[136,128]{1,0:T(8,128)S(1)}, u32[]{:S(2)}, u32[]{:S(2)}) collective-permute-start(f32[136,128]{1,0:T(8,128)S(1)} %get-tuple-element.7), channel_id=1, source_target_pairs={{0,192},{32,224},{64,0},{96,32},{128,64},{160,96},{192,128},{224,1... | collective-permute-start | bytes 208904 | tf_op jit(solution)/shard_map/ppermute | solution.py:24
  82.2 2.7 %collective-permute-start.22 = (f32[136,128]{1,0:T(8,128)S(1)}, f32[136,128]{1,0:T(8,128)S(1)}, u32[]{:S(2)}, u32[]{:S(2)}) collective-permute-start(f32[136,128]{1,0:T(8,128)S(1)} %get-tuple-element.7), channel_id=1, source_target_pairs={{0,224},{32,0},{64,32},{96,64},{128,96},{160,128},{192,160},{224,1... | collective-permute-start | bytes 208904 | tf_op jit(solution)/shard_map/ppermute | solution.py:24
  84.8 4.9 %all-to-all-start.2 = ((f32[16,128,128]{2,1,0:T(8,128)}), f32[16,128,128]{2,1,0:T(8,128)}, u32[]{:S(2)}, u32[]{:S(2)}) async-start(f32[16,128,128]{2,1,0:T(8,128)} %get-tuple-element.6), calls=%async_computation.2 | async-start | bytes 2097152 | tf_op jit(solution)/shard_map/all_to_all | solution.py:36
  89.8 0.1 collective-permute-start.23
  89.9 1.7 %collective-permute-start.25 = (f32[136,128]{1,0:T(8,128)S(1)}, f32[136,128]{1,0:T(8,128)S(1)}, u32[]{:S(2)}, u32[]{:S(2)}) collective-permute-start(f32[136,128]{1,0:T(8,128)S(1)} %collective-permute-done.19), channel_id=1, source_target_pairs={{0,64},{32,96},{64,128},{96,160},{128,192},{160,224},{192,0},{224,... | collective-permute-start | bytes 208904 | tf_op jit(solution)/shard_map/ppermute | solution.py:24
  91.6 1.1 collective-permute-start.24
  92.8 1.5 %collective-permute-done.23 = f32[136,128]{1,0:T(8,128)S(1)} collective-permute-done((f32[136,128]{1,0:T(8,128)S(1)}, f32[136,128]{1,0:T(8,128)S(1)}, u32[]{:S(2)}, u32[]{:S(2)}) %collective-permute-start.23) | collective-permute-done | bytes 69664 | tf_op jit(solution)/shard_map/ppermute | solution.py:24
  94.3 1.8 %collective-permute-done.24 = f32[136,128]{1,0:T(8,128)S(1)} collective-permute-done((f32[136,128]{1,0:T(8,128)S(1)}, f32[136,128]{1,0:T(8,128)S(1)}, u32[]{:S(2)}, u32[]{:S(2)}) %collective-permute-start.24) | collective-permute-done | bytes 69664 | tf_op jit(solution)/shard_map/ppermute | solution.py:24
  96.1 5.4 %collective-permute-start.26 = (f32[8,136,128]{2,1,0:T(8,128)S(1)}, f32[8,136,128]{2,1,0:T(8,128)S(1)}, u32[]{:S(2)}, u32[]{:S(2)}) collective-permute-start(f32[8,136,128]{2,1,0:T(8,128)S(1)} %bitcast_dynamic-update-slice_fusion), channel_id=1, source_target_pairs={{0,1},{1,0},{2,3},{3,2},{4,5},{5,4},{6,7},{7,6},{8,9},{9,8},{10,11... | collective-permute-start | bytes 1671176 | tf_op jit(solution)/shard_map/ppermute | solution.py:28
  101.5 3.3 %collective-permute-start.27 = (f32[128,128]{1,0:T(8,128)S(1)}, f32[128,128]{1,0:T(8,128)S(1)}, u32[]{:S(2)}, u32[]{:S(2)}) collective-permute-start(f32[128,128]{1,0:T(8,128)S(1)} %get-tuple-element.15.stat), channel_id=1, source_target_pairs={{0,0},{1,16},{16,1},{17,17},{2,2},{3,18},{18,3},{19,19},{4,4},{5,2... | collective-permute-start | bytes 196616 | tf_op jit(solution)/shard_map/ppermute | solution.py:32
  104.8 2.6 %collective-permute-done.27.home = f32[128,128]{1,0:T(8,128)S(1)} collective-permute-done((f32[128,128]{1,0:T(8,128)S(1)}, f32[128,128]{1,0:T(8,128)S(1)}, u32[]{:S(2)}, u32[]{:S(2)}) %collective-permute-start.27) | collective-permute-done | bytes 65568 | tf_op jit(solution)/shard_map/ppermute | solution.py:32
  107.4 2.7 %shard_map.42 = (f32[128,128]{1,0:T(8,128)S(1)}, f32[128,128]{1,0:T(8,128)}) custom-call(f32[16,128,128]{2,1,0:T(8,128)} %all-to-all-done.2.square_row, f32[16,128,128]{2,1,0:T(8,128)S(1)} %all-to-all-done.1.row_ref.stat_row, f32[16,136,128]{2,1,0:T(8,128)S(1)} %pad_maximum_fusion.square_column, ...), custom_call_target="tpu_custom_call" | custom-call | tf_op jit(solution)/shard_map/pallas_call | solution.py:147
  110.1 3.1 %collective-permute-start.28 = (f32[128,128]{1,0:T(8,128)S(1)}, f32[128,128]{1,0:T(8,128)S(1)}, u32[]{:S(2)}, u32[]{:S(2)}) collective-permute-start(f32[128,128]{1,0:T(8,128)S(1)} %get-tuple-element.9), channel_id=1, source_target_pairs={{0,0},{1,16},{16,1},{17,17},{2,2},{3,18},{18,3},{19,19},{4,4},{5,2... | collective-permute-start | bytes 196616 | tf_op jit(solution)/shard_map/ppermute | solution.py:32
  113.3 2.4 %collective-permute-done.28 = f32[128,128]{1,0:T(8,128)S(1)} collective-permute-done((f32[128,128]{1,0:T(8,128)S(1)}, f32[128,128]{1,0:T(8,128)S(1)}, u32[]{:S(2)}, u32[]{:S(2)}) %collective-permute-start.28) | collective-permute-done | bytes 65568 | tf_op jit(solution)/shard_map/ppermute | solution.py:32
  115.7 0.6 copy.30
  (54 shorter events, 0.4 us)
Async XLA Ops:
  0.6 8.3 %collective-permute-start.2 = (f32[32,128]{1,0:T(8,128)}, f32[32,128]{1,0:T(8,128)S(1)}, u32[]{:S(2)}, u32[]{:S(2)}) collective-permute-start(f32[32,128]{1,0:T(8,128)} %bitcast.68), channel_id=1, source_target_pairs={{0,0},{1,1},{2,32},{3,33},{4,64},{5,65},{6,96},{7,97},{8,128},{9,1... | collective-permute-start | bytes 49160 | tf_op jit(solution)/shard_map/ppermute | solution.py:59
  2.0 32.1 %collective-permute-start.1 = (f32[32,128]{1,0:T(8,128)}, f32[32,128]{1,0:T(8,128)S(1)}, u32[]{:S(2)}, u32[]{:S(2)}) collective-permute-start(f32[32,128]{1,0:T(8,128)} %bitcast.69), channel_id=1, source_target_pairs={{0,16},{16,0},{1,17},{17,1},{2,18},{18,2},{3,19},{19,3},{4,20},{20... | collective-permute-start | bytes 49160 | tf_op jit(solution)/shard_map/ppermute | solution.py:28
  4.0 37.5 %collective-permute-start = (f32[128,128]{1,0:T(8,128)}, f32[128,128]{1,0:T(8,128)S(1)}, u32[]{:S(2)}, u32[]{:S(2)}) collective-permute-start(f32[128,128]{1,0:T(8,128)} %param.3), channel_id=1, source_target_pairs={{0,0},{1,16},{16,1},{17,17},{2,2},{3,18},{18,3},{19,19},{4,4},{5,2... | collective-permute-start | bytes 196616 | tf_op jit(solution)/shard_map/ppermute | solution.py:32
  8.9 9.8 %collective-permute-start.3 = (f32[32,128]{1,0:T(8,128)S(1)}, f32[32,128]{1,0:T(8,128)S(1)}, u32[]{:S(2)}, u32[]{:S(2)}) collective-permute-start(f32[32,128]{1,0:T(8,128)S(1)} %collective-permute-done.2), channel_id=1, source_target_pairs={{0,64},{32,96},{64,128},{96,160},{128,192},{160,224},{192,0},{224,... | collective-permute-start | bytes 49160 | tf_op jit(solution)/shard_map/ppermute | solution.py:24
  11.5 10.5 %collective-permute-start.4 = (f32[32,128]{1,0:T(8,128)S(1)}, f32[32,128]{1,0:T(8,128)S(1)}, u32[]{:S(2)}, u32[]{:S(2)}) collective-permute-start(f32[32,128]{1,0:T(8,128)S(1)} %collective-permute-done.2), channel_id=1, source_target_pairs={{0,192},{32,224},{64,0},{96,32},{128,64},{160,96},{192,128},{224,1... | collective-permute-start | bytes 49160 | tf_op jit(solution)/shard_map/ppermute | solution.py:24
  16.4 6.8 %collective-permute-start.5 = (f32[32,128]{1,0:T(8,128)S(1)}, f32[32,128]{1,0:T(8,128)S(1)}, u32[]{:S(2)}, u32[]{:S(2)}) collective-permute-start(f32[32,128]{1,0:T(8,128)S(1)} %collective-permute-done.2), channel_id=1, source_target_pairs={{0,32},{32,64},{64,96},{96,128},{128,160},{160,192},{192,224},{224... | collective-permute-start | bytes 49160 | tf_op jit(solution)/shard_map/ppermute | solution.py:24
  18.7 6.0 %collective-permute-start.6 = (f32[32,128]{1,0:T(8,128)S(1)}, f32[32,128]{1,0:T(8,128)S(1)}, u32[]{:S(2)}, u32[]{:S(2)}) collective-permute-start(f32[32,128]{1,0:T(8,128)S(1)} %collective-permute-done.2), channel_id=1, source_target_pairs={{0,224},{32,0},{64,32},{96,64},{128,96},{160,128},{192,160},{224,1... | collective-permute-start | bytes 49160 | tf_op jit(solution)/shard_map/ppermute | solution.py:24
  22.0 4.9 %collective-permute-start.7 = (f32[32,128]{1,0:T(8,128)S(1)}, f32[32,128]{1,0:T(8,128)S(1)}, u32[]{:S(2)}, u32[]{:S(2)}) collective-permute-start(f32[32,128]{1,0:T(8,128)S(1)} %collective-permute-done.3), channel_id=1, source_target_pairs={{0,32},{32,64},{64,96},{96,128},{128,160},{160,192},{192,224},{224... | collective-permute-start | bytes 49160 | tf_op jit(solution)/shard_map/ppermute | solution.py:24
  23.2 3.7 %collective-permute-start.8 = (f32[32,128]{1,0:T(8,128)S(1)}, f32[32,128]{1,0:T(8,128)S(1)}, u32[]{:S(2)}, u32[]{:S(2)}) collective-permute-start(f32[32,128]{1,0:T(8,128)S(1)} %collective-permute-done.4), channel_id=1, source_target_pairs={{0,224},{32,0},{64,32},{96,64},{128,96},{160,128},{192,160},{224,1... | collective-permute-start | bytes 49160 | tf_op jit(solution)/shard_map/ppermute | solution.py:24
  24.7 4.7 %collective-permute-start.9 = (f32[32,128]{1,0:T(8,128)S(1)}, f32[32,128]{1,0:T(8,128)S(1)}, u32[]{:S(2)}, u32[]{:S(2)}) collective-permute-start(f32[32,128]{1,0:T(8,128)S(1)} %collective-permute-done.3), channel_id=1, source_target_pairs={{0,64},{32,96},{64,128},{96,160},{128,192},{160,224},{192,0},{224,... | collective-permute-start | bytes 49160 | tf_op jit(solution)/shard_map/ppermute | solution.py:24
  29.4 12.1 %collective-permute-start.10 = (f32[8,32,128]{2,1,0:T(8,128)S(1)}, f32[8,32,128]{2,1,0:T(8,128)S(1)}, u32[]{:S(2)}, u32[]{:S(2)}) collective-permute-start(f32[8,32,128]{2,1,0:T(8,128)S(1)} %bitcast_dynamic-update-slice_fusion.16), channel_id=1, source_target_pairs={{0,1},{1,0},{2,3},{3,2},{4,5},{5,4},{6,7},{7,6},{8,9},{9,8},{10,11... | collective-permute-start | bytes 393224 | tf_op jit(solution)/shard_map/ppermute | solution.py:28
  35.5 14.6 %all-to-all-start = ((f32[16,32,128]{2,1,0:T(8,128)}), f32[16,32,128]{2,1,0:T(8,128)S(1)}, u32[]{:S(2)}, u32[]{:S(2)}) async-start(f32[16,32,128]{2,1,0:T(8,128)} %bitcast.3), calls=%async_computation | async-start | bytes 524288 | tf_op jit(solution)/shard_map/all_to_all | solution.py:68
  50.8 11.1 %collective-permute-start.11 = (f32[128,128]{1,0:T(8,128)S(1)}, f32[128,128]{1,0:T(8,128)S(1)}, u32[]{:S(2)}, u32[]{:S(2)}) collective-permute-start(f32[128,128]{1,0:T(8,128)S(1)} %get-tuple-element.15.stat), channel_id=1, source_target_pairs={{0,64},{32,96},{64,128},{96,160},{128,192},{160,224},{192,0},{224,... | collective-permute-start | bytes 196616 | tf_op jit(solution)/shard_map/ppermute | solution.py:24
  51.1 12.6 %collective-permute-start.12 = (f32[128,128]{1,0:T(8,128)S(1)}, f32[128,128]{1,0:T(8,128)S(1)}, u32[]{:S(2)}, u32[]{:S(2)}) collective-permute-start(f32[128,128]{1,0:T(8,128)S(1)} %get-tuple-element.15.stat), channel_id=1, source_target_pairs={{0,192},{32,224},{64,0},{96,32},{128,64},{160,96},{192,128},{224,1... | collective-permute-start | bytes 196616 | tf_op jit(solution)/shard_map/ppermute | solution.py:24
  54.5 10.3 %collective-permute-start.13 = (f32[128,128]{1,0:T(8,128)S(1)}, f32[128,128]{1,0:T(8,128)S(1)}, u32[]{:S(2)}, u32[]{:S(2)}) collective-permute-start(f32[128,128]{1,0:T(8,128)S(1)} %get-tuple-element.15.stat), channel_id=1, source_target_pairs={{0,32},{32,64},{64,96},{96,128},{128,160},{160,192},{192,224},{224... | collective-permute-start | bytes 196616 | tf_op jit(solution)/shard_map/ppermute | solution.py:24
  54.6 10.2 %collective-permute-start.14 = (f32[128,128]{1,0:T(8,128)S(1)}, f32[128,128]{1,0:T(8,128)S(1)}, u32[]{:S(2)}, u32[]{:S(2)}) collective-permute-start(f32[128,128]{1,0:T(8,128)S(1)} %get-tuple-element.15.stat), channel_id=1, source_target_pairs={{0,224},{32,0},{64,32},{96,64},{128,96},{160,128},{192,160},{224,1... | collective-permute-start | bytes 196616 | tf_op jit(solution)/shard_map/ppermute | solution.py:24
  58.2 18.7 %all-to-all-start.1 = ((f32[16,128,128]{2,1,0:T(8,128)}), f32[16,128,128]{2,1,0:T(8,128)S(1)}, u32[]{:S(2)}, u32[]{:S(2)}) async-start(f32[16,128,128]{2,1,0:T(8,128)} %broadcast_in_dim.96), calls=%async_computation.1 | async-start | bytes 2097152 | tf_op jit(solution)/shard_map/all_to_all | solution.py:36
  61.9 4.4 %collective-permute-start.15 = (f32[128,128]{1,0:T(8,128)S(1)}, f32[128,128]{1,0:T(8,128)S(1)}, u32[]{:S(2)}, u32[]{:S(2)}) collective-permute-start(f32[128,128]{1,0:T(8,128)S(1)} %collective-permute-done.11), channel_id=1, source_target_pairs={{0,32},{32,64},{64,96},{96,128},{128,160},{160,192},{192,224},{224... | collective-permute-start | bytes 196616 | tf_op jit(solution)/shard_map/ppermute | solution.py:24
  62.0 6.1 %collective-permute-start.17 = (f32[128,128]{1,0:T(8,128)S(1)}, f32[128,128]{1,0:T(8,128)S(1)}, u32[]{:S(2)}, u32[]{:S(2)}) collective-permute-start(f32[128,128]{1,0:T(8,128)S(1)} %collective-permute-done.11), channel_id=1, source_target_pairs={{0,64},{32,96},{64,128},{96,160},{128,192},{160,224},{192,0},{224,... | collective-permute-start | bytes 196616 | tf_op jit(solution)/shard_map/ppermute | solution.py:24
  63.7 4.4 %collective-permute-start.16 = (f32[128,128]{1,0:T(8,128)S(1)}, f32[128,128]{1,0:T(8,128)S(1)}, u32[]{:S(2)}, u32[]{:S(2)}) collective-permute-start(f32[128,128]{1,0:T(8,128)S(1)} %collective-permute-done.12), channel_id=1, source_target_pairs={{0,224},{32,0},{64,32},{96,64},{128,96},{160,128},{192,160},{224,1... | collective-permute-start | bytes 196616 | tf_op jit(solution)/shard_map/ppermute | solution.py:24
  68.1 5.1 %collective-permute-start.18 = (f32[8,128,128]{2,1,0:T(8,128)S(1)}, f32[8,128,128]{2,1,0:T(8,128)S(1)}, u32[]{:S(2)}, u32[]{:S(2)}) collective-permute-start(f32[8,128,128]{2,1,0:T(8,128)S(1)} %bitcast_dynamic-update-slice_fusion.8), channel_id=1, source_target_pairs={{0,1},{1,0},{2,3},{3,2},{4,5},{5,4},{6,7},{7,6},{8,9},{9,8},{10,11... | collective-permute-start | bytes 1572872 | tf_op jit(solution)/shard_map/ppermute | solution.py:28
  78.6 11.2 %collective-permute-start.19 = (f32[136,128]{1,0:T(8,128)S(1)}, f32[136,128]{1,0:T(8,128)S(1)}, u32[]{:S(2)}, u32[]{:S(2)}) collective-permute-start(f32[136,128]{1,0:T(8,128)S(1)} %get-tuple-element.7), channel_id=1, source_target_pairs={{0,64},{32,96},{64,128},{96,160},{128,192},{160,224},{192,0},{224,... | collective-permute-start | bytes 208904 | tf_op jit(solution)/shard_map/ppermute | solution.py:24
  78.6 13.0 %collective-permute-start.20 = (f32[136,128]{1,0:T(8,128)S(1)}, f32[136,128]{1,0:T(8,128)S(1)}, u32[]{:S(2)}, u32[]{:S(2)}) collective-permute-start(f32[136,128]{1,0:T(8,128)S(1)} %get-tuple-element.7), channel_id=1, source_target_pairs={{0,192},{32,224},{64,0},{96,32},{128,64},{160,96},{192,128},{224,1... | collective-permute-start | bytes 208904 | tf_op jit(solution)/shard_map/ppermute | solution.py:24
  82.2 10.5 %collective-permute-start.21 = (f32[136,128]{1,0:T(8,128)S(1)}, f32[136,128]{1,0:T(8,128)S(1)}, u32[]{:S(2)}, u32[]{:S(2)}) collective-permute-start(f32[136,128]{1,0:T(8,128)S(1)} %get-tuple-element.7), channel_id=1, source_target_pairs={{0,32},{32,64},{64,96},{96,128},{128,160},{160,192},{192,224},{224... | collective-permute-start | bytes 208904 | tf_op jit(solution)/shard_map/ppermute | solution.py:24
  82.2 10.6 %collective-permute-start.22 = (f32[136,128]{1,0:T(8,128)S(1)}, f32[136,128]{1,0:T(8,128)S(1)}, u32[]{:S(2)}, u32[]{:S(2)}) collective-permute-start(f32[136,128]{1,0:T(8,128)S(1)} %get-tuple-element.7), channel_id=1, source_target_pairs={{0,224},{32,0},{64,32},{96,64},{128,96},{160,128},{192,160},{224,1... | collective-permute-start | bytes 208904 | tf_op jit(solution)/shard_map/ppermute | solution.py:24
  84.8 22.6 %all-to-all-start.2 = ((f32[16,128,128]{2,1,0:T(8,128)}), f32[16,128,128]{2,1,0:T(8,128)}, u32[]{:S(2)}, u32[]{:S(2)}) async-start(f32[16,128,128]{2,1,0:T(8,128)} %get-tuple-element.6), calls=%async_computation.2 | async-start | bytes 2097152 | tf_op jit(solution)/shard_map/all_to_all | solution.py:36
  89.8 4.4 %collective-permute-start.23 = (f32[136,128]{1,0:T(8,128)S(1)}, f32[136,128]{1,0:T(8,128)S(1)}, u32[]{:S(2)}, u32[]{:S(2)}) collective-permute-start(f32[136,128]{1,0:T(8,128)S(1)} %collective-permute-done.19), channel_id=1, source_target_pairs={{0,32},{32,64},{64,96},{96,128},{128,160},{160,192},{192,224},{224... | collective-permute-start | bytes 208904 | tf_op jit(solution)/shard_map/ppermute | solution.py:24
  89.9 6.2 %collective-permute-start.25 = (f32[136,128]{1,0:T(8,128)S(1)}, f32[136,128]{1,0:T(8,128)S(1)}, u32[]{:S(2)}, u32[]{:S(2)}) collective-permute-start(f32[136,128]{1,0:T(8,128)S(1)} %collective-permute-done.19), channel_id=1, source_target_pairs={{0,64},{32,96},{64,128},{96,160},{128,192},{160,224},{192,0},{224,... | collective-permute-start | bytes 208904 | tf_op jit(solution)/shard_map/ppermute | solution.py:24
  91.6 4.5 %collective-permute-start.24 = (f32[136,128]{1,0:T(8,128)S(1)}, f32[136,128]{1,0:T(8,128)S(1)}, u32[]{:S(2)}, u32[]{:S(2)}) collective-permute-start(f32[136,128]{1,0:T(8,128)S(1)} %collective-permute-done.20), channel_id=1, source_target_pairs={{0,224},{32,0},{64,32},{96,64},{128,96},{160,128},{192,160},{224,1... | collective-permute-start | bytes 208904 | tf_op jit(solution)/shard_map/ppermute | solution.py:24
  96.1 8.6 %collective-permute-start.26 = (f32[8,136,128]{2,1,0:T(8,128)S(1)}, f32[8,136,128]{2,1,0:T(8,128)S(1)}, u32[]{:S(2)}, u32[]{:S(2)}) collective-permute-start(f32[8,136,128]{2,1,0:T(8,128)S(1)} %bitcast_dynamic-update-slice_fusion), channel_id=1, source_target_pairs={{0,1},{1,0},{2,3},{3,2},{4,5},{5,4},{6,7},{7,6},{8,9},{9,8},{10,11... | collective-permute-start | bytes 1671176 | tf_op jit(solution)/shard_map/ppermute | solution.py:28
  101.5 6.0 %collective-permute-start.27 = (f32[128,128]{1,0:T(8,128)S(1)}, f32[128,128]{1,0:T(8,128)S(1)}, u32[]{:S(2)}, u32[]{:S(2)}) collective-permute-start(f32[128,128]{1,0:T(8,128)S(1)} %get-tuple-element.15.stat), channel_id=1, source_target_pairs={{0,0},{1,16},{16,1},{17,17},{2,2},{3,18},{18,3},{19,19},{4,4},{5,2... | collective-permute-start | bytes 196616 | tf_op jit(solution)/shard_map/ppermute | solution.py:32
  110.1 5.6 %collective-permute-start.28 = (f32[128,128]{1,0:T(8,128)S(1)}, f32[128,128]{1,0:T(8,128)S(1)}, u32[]{:S(2)}, u32[]{:S(2)}) collective-permute-start(f32[128,128]{1,0:T(8,128)S(1)} %get-tuple-element.9), channel_id=1, source_target_pairs={{0,0},{1,16},{16,1},{17,17},{2,2},{3,18},{18,3},{19,19},{4,4},{5,2... | collective-permute-start | bytes 196616 | tf_op jit(solution)/shard_map/ppermute | solution.py:32

commit v3 on v2

--- a/solution.py
+++ b/solution.py
@@ -36,7 +36,11 @@
     return lax.all_to_all(copies, (Y, XH, XL), 0, 0, tiled=True)
 
 
-def column_pieces(block):
+def plain_slot(place):
+    return place
+
+
+def column_pieces(block, slot=plain_slot):
     place = lax.axis_index(Z)
     found = {0: block}
     for shift in (2, -2, 1, -1):
@@ -46,15 +50,25 @@
     found[4] = rotate(found[2], Z, 2)
     mine = jnp.zeros((8,) + block.shape, block.dtype)
     for shift, piece in found.items():
-        mine = lax.dynamic_update_slice(mine, piece[None], ((place - shift) % 8, 0, 0))
+        mine = lax.dynamic_update_slice(mine, piece[None], (slot((place - shift) % 8), 0, 0))
     other = swap(mine, CORE)
     return jnp.concatenate((mine, other), axis=0)
+
+
+OFFSETS = (5, 3, 1, 2, 0, 6, 4, 7)
+
+
+def origin(away, group):
+    packed = sum(offset << (3 * number) for number, offset in enumerate(OFFSETS))
+    offset = (packed >> (3 * away)) & 7
+    return ((group & 6) + (offset & 6)) & 6 | ((group ^ offset) & 1)
 
 
 def exchange(array):
     places = [(z, x, g, c) for z in range(8) for x in range(2) for g in range(8) for c in range(2)]
     pairs = [
-        (((z * 2 + x) * 8 + g) * 2 + c, ((g * 2 + x) * 8 + z) * 2 + c) for z, x, g, c in places
+        (((g * 2 + x) * 8 + origin((z - g) % 8, g)) * 2 + c, ((z * 2 + x) * 8 + g) * 2 + c)
+        for z, x, g, c in places
     ]
     return lax.ppermute(array, (Z, XL, Y, XH, CORE), pairs)
 
@@ -66,7 +80,8 @@
     at_high = lax.axis_index(XL) == 1
     pair = jnp.stack((jnp.where(at_high, beside, piece), jnp.where(at_high, piece, beside)))
     rows_of = lax.all_to_all(jnp.tile(pair, (8, 1, 1)), GY, 0, 0, tiled=True)
-    pieces = column_pieces(moved)
+    group = 2 * lax.axis_index(Y) + lax.axis_index(XH)
+    pieces = column_pieces(moved, lambda place: origin((place - group) % 8, group))
     mine, other = pieces[:8], pieces[8:]
     core = lax.axis_index(CORE)
     columns_of = jnp.stack(

time: 117 us -> 113 us (0.966)
  starting transfers between devices: 78.8 us -> 74.1 us
    ppermute x21, starting transfers between devices: 36.2 us -> 28.3 us  [rotate(): lax.ppermute(array, axis, [(s, (s + shift) % size) for s in range(size)])]
    ppermute x1, starting transfers between devices: 1.38 us -> 7.8 us  [exchange(): return lax.ppermute(array, (Z, XL, Y, XH, CORE), pairs)]
    ppermute x3, starting transfers between devices: 11.1 us -> 9.92 us  [turn(): return lax.ppermute(array, (XL, CORE), [(0, 0), (1, 2), (2, 1), (3, 3)])]
  transfers between devices with their start and end apart: 32 -> 32, of which waited for: 10 -> 11; matrix products, arithmetic and copies ran while one was open for 3% -> 3% of each run, Pallas kernels for 0% -> 0%
where the time goes in v3:
time: 113 us
  starting transfers between devices  74.1 us (66%)
  waiting for transfers between devices  28.6 us (25%)
  Pallas kernels  4.33 us (4%)
  local copies, waits for them, and re-layouts  2.7 us (2%)
  between operations  1.3 us (1%)
    ppermute x21, starting transfers between devices, rotate(): lax.ppermute(array, axis, [(s, (s + shift) % size) for s in range(size)])  28.3 us
    ppermute x4, starting transfers between devices, swap(): return lax.ppermute(array, axis, [(0, 1), (1, 0)])  14.6 us
    ppermute x3, starting transfers between devices, turn(): return lax.ppermute(array, (XL, CORE), [(0, 0), (1, 2), (2, 1), (3, 3)])  9.92 us
    ppermute x21, waiting for transfers between devices, rotate(): lax.ppermute(array, axis, [(s, (s + shift) % size) for s in range(size)])  9.91 us
    all_to_all x1, waiting for transfers between devices, outer_part(): rows_of = lax.all_to_all(jnp.tile(pair, (8, 1, 1)), GY, 0, 0, tiled=True)  8.62 us
    all_to_all x2, starting transfers between devices, row_panel(): return lax.all_to_all(copies, (Y, XH, XL), 0, 0, tiled=True)  8.55 us
    ppermute x1, starting transfers between devices, exchange(): return lax.ppermute(array, (Z, XL, Y, XH, CORE), pairs)  7.8 us
    all_to_all x1, starting transfers between devices, outer_part(): rows_of = lax.all_to_all(jnp.tile(pair, (8, 1, 1)), GY, 0, 0, tiled=True)  4.97 us
  transfers between devices with their start and end apart: 32, of which 11 were waited for; matrix products, arithmetic and copies ran while one was open for 3% of the time, Pallas kernels for 0%

profile of v3, /device:TPU:1, one launch (start us, length us, event | category | flops | bytes accessed | tf_op | source)
XLA Modules:
  0.0 112.6 jit_solution(14276302456840289366)
XLA Ops:
  0.6 7.8 %collective-permute-start.2 = (f32[32,128]{1,0:T(8,128)}, f32[32,128]{1,0:T(8,128)S(1)}, u32[]{:S(2)}, u32[]{:S(2)}) collective-permute-start(f32[32,128]{1,0:T(8,128)} %bitcast.68), channel_id=1, source_target_pairs={{10,0},{11,1},{44,2},{45,3},{76,4},{77,5},{98,6},{99,7},{136,8},{1... | collective-permute-start | bytes 49160 | tf_op jit(solution)/shard_map/ppermute | solution.py:73
  8.4 1.2 %collective-permute-start.1 = (f32[32,128]{1,0:T(8,128)}, f32[32,128]{1,0:T(8,128)S(1)}, u32[]{:S(2)}, u32[]{:S(2)}) collective-permute-start(f32[32,128]{1,0:T(8,128)} %bitcast.69), channel_id=1, source_target_pairs={{0,16},{16,0},{1,17},{17,1},{2,18},{18,2},{3,19},{19,3},{4,20},{20... | collective-permute-start | bytes 49160 | tf_op jit(solution)/shard_map/ppermute | solution.py:28
  9.6 3.3 %collective-permute-start = (f32[128,128]{1,0:T(8,128)}, f32[128,128]{1,0:T(8,128)S(1)}, u32[]{:S(2)}, u32[]{:S(2)}) collective-permute-start(f32[128,128]{1,0:T(8,128)} %param.3), channel_id=1, source_target_pairs={{0,0},{1,16},{16,1},{17,17},{2,2},{3,18},{18,3},{19,19},{4,4},{5,2... | collective-permute-start | bytes 196616 | tf_op jit(solution)/shard_map/ppermute | solution.py:32
  13.3 1.8 %collective-permute-start.3 = (f32[32,128]{1,0:T(8,128)S(1)}, f32[32,128]{1,0:T(8,128)S(1)}, u32[]{:S(2)}, u32[]{:S(2)}) collective-permute-start(f32[32,128]{1,0:T(8,128)S(1)} %collective-permute-done.2), channel_id=1, source_target_pairs={{0,64},{32,96},{64,128},{96,160},{128,192},{160,224},{192,0},{224,... | collective-permute-start | bytes 49160 | tf_op jit(solution)/shard_map/ppermute | solution.py:24
  15.1 1.8 %collective-permute-start.4 = (f32[32,128]{1,0:T(8,128)S(1)}, f32[32,128]{1,0:T(8,128)S(1)}, u32[]{:S(2)}, u32[]{:S(2)}) collective-permute-start(f32[32,128]{1,0:T(8,128)S(1)} %collective-permute-done.2), channel_id=1, source_target_pairs={{0,192},{32,224},{64,0},{96,32},{128,64},{160,96},{192,128},{224,1... | collective-permute-start | bytes 49160 | tf_op jit(solution)/shard_map/ppermute | solution.py:24
  16.9 0.2 collective-permute-start.5
  17.1 1.3 %collective-permute-done.3 = f32[32,128]{1,0:T(8,128)S(1)} collective-permute-done((f32[32,128]{1,0:T(8,128)S(1)}, f32[32,128]{1,0:T(8,128)S(1)}, u32[]{:S(2)}, u32[]{:S(2)}) %collective-permute-start.3) | collective-permute-done | bytes 16416 | tf_op jit(solution)/shard_map/ppermute | solution.py:24
  18.4 1.3 %collective-permute-start.6 = (f32[32,128]{1,0:T(8,128)S(1)}, f32[32,128]{1,0:T(8,128)S(1)}, u32[]{:S(2)}, u32[]{:S(2)}) collective-permute-start(f32[32,128]{1,0:T(8,128)S(1)} %collective-permute-done.2), channel_id=1, source_target_pairs={{0,224},{32,0},{64,32},{96,64},{128,96},{160,128},{192,160},{224,1... | collective-permute-start | bytes 49160 | tf_op jit(solution)/shard_map/ppermute | solution.py:24
  19.7 1.5 %collective-permute-start.7 = (f32[32,128]{1,0:T(8,128)S(1)}, f32[32,128]{1,0:T(8,128)S(1)}, u32[]{:S(2)}, u32[]{:S(2)}) collective-permute-start(f32[32,128]{1,0:T(8,128)S(1)} %collective-permute-done.3), channel_id=1, source_target_pairs={{0,32},{32,64},{64,96},{96,128},{128,160},{160,192},{192,224},{224... | collective-permute-start | bytes 49160 | tf_op jit(solution)/shard_map/ppermute | solution.py:24
  21.2 1.2 %collective-permute-start.8 = (f32[32,128]{1,0:T(8,128)S(1)}, f32[32,128]{1,0:T(8,128)S(1)}, u32[]{:S(2)}, u32[]{:S(2)}) collective-permute-start(f32[32,128]{1,0:T(8,128)S(1)} %collective-permute-done.4), channel_id=1, source_target_pairs={{0,224},{32,0},{64,32},{96,64},{128,96},{160,128},{192,160},{224,1... | collective-permute-start | bytes 49160 | tf_op jit(solution)/shard_map/ppermute | solution.py:24
  22.4 2.1 %collective-permute-start.9 = (f32[32,128]{1,0:T(8,128)S(1)}, f32[32,128]{1,0:T(8,128)S(1)}, u32[]{:S(2)}, u32[]{:S(2)}) collective-permute-start(f32[32,128]{1,0:T(8,128)S(1)} %collective-permute-done.3), channel_id=1, source_target_pairs={{0,64},{32,96},{64,128},{96,160},{128,192},{160,224},{192,0},{224,... | collective-permute-start | bytes 49160 | tf_op jit(solution)/shard_map/ppermute | solution.py:24
  24.6 2.5 %collective-permute-done.9 = f32[32,128]{1,0:T(8,128)S(1)} collective-permute-done((f32[32,128]{1,0:T(8,128)S(1)}, f32[32,128]{1,0:T(8,128)S(1)}, u32[]{:S(2)}, u32[]{:S(2)}) %collective-permute-start.9) | collective-permute-done | bytes 16416 | tf_op jit(solution)/shard_map/ppermute | solution.py:24
  27.1 4.5 %collective-permute-start.10 = (f32[8,32,128]{2,1,0:T(8,128)S(1)}, f32[8,32,128]{2,1,0:T(8,128)S(1)}, u32[]{:S(2)}, u32[]{:S(2)}) collective-permute-start(f32[8,32,128]{2,1,0:T(8,128)S(1)} %bitcast_dynamic-update-slice_fusion.16), channel_id=1, source_target_pairs={{0,1},{1,0},{2,3},{3,2},{4,5},{5,4},{6,7},{7,6},{8,9},{9,8},{10,11... | collective-permute-start | bytes 393224 | tf_op jit(solution)/shard_map/ppermute | solution.py:28
  31.6 0.7 select_bitcast_fusion.3
  32.3 0.7 tile.4
  33.0 5.0 %all-to-all-start = ((f32[16,32,128]{2,1,0:T(8,128)}), f32[16,32,128]{2,1,0:T(8,128)S(1)}, u32[]{:S(2)}, u32[]{:S(2)}) async-start(f32[16,32,128]{2,1,0:T(8,128)} %bitcast.3), calls=%async_computation | async-start | bytes 524288 | tf_op jit(solution)/shard_map/all_to_all | solution.py:82
  38.1 8.6 %all-to-all-done = f32[16,32,128]{2,1,0:T(8,128)S(1)} async-done(((f32[16,32,128]{2,1,0:T(8,128)}), f32[16,32,128]{2,1,0:T(8,128)S(1)}, u32[]{:S(2)}, u32[]{:S(2)}) %all-to-all-start) | async-done | bytes 262176 | tf_op jit(solution)/shard_map/all_to_all | solution.py:82
  46.8 0.6 bitcast_dynamic-update-slice_fusion.15
  47.4 0.1 collective-permute-start.11
  47.5 3.6 %collective-permute-start.12 = (f32[128,128]{1,0:T(8,128)S(1)}, f32[128,128]{1,0:T(8,128)S(1)}, u32[]{:S(2)}, u32[]{:S(2)}) collective-permute-start(f32[128,128]{1,0:T(8,128)S(1)} %get-tuple-element.15.stat), channel_id=1, source_target_pairs={{0,192},{32,224},{64,0},{96,32},{128,64},{160,96},{192,128},{224,1... | collective-permute-start | bytes 196616 | tf_op jit(solution)/shard_map/ppermute | solution.py:24
  51.0 2.7 %collective-permute-start.14 = (f32[128,128]{1,0:T(8,128)S(1)}, f32[128,128]{1,0:T(8,128)S(1)}, u32[]{:S(2)}, u32[]{:S(2)}) collective-permute-start(f32[128,128]{1,0:T(8,128)S(1)} %get-tuple-element.15.stat), channel_id=1, source_target_pairs={{0,224},{32,0},{64,32},{96,64},{128,96},{160,128},{192,160},{224,1... | collective-permute-start | bytes 196616 | tf_op jit(solution)/shard_map/ppermute | solution.py:24
  53.7 1.1 broadcast_in_dim.96
  54.8 3.7 %all-to-all-start.1 = ((f32[16,128,128]{2,1,0:T(8,128)}), f32[16,128,128]{2,1,0:T(8,128)S(1)}, u32[]{:S(2)}, u32[]{:S(2)}) async-start(f32[16,128,128]{2,1,0:T(8,128)} %broadcast_in_dim.96), calls=%async_computation.1 | async-start | bytes 2097152 | tf_op jit(solution)/shard_map/all_to_all | solution.py:36
  58.4 0.3 collective-permute-start.15
  58.7 1.4 %collective-permute-start.17 = (f32[128,128]{1,0:T(8,128)S(1)}, f32[128,128]{1,0:T(8,128)S(1)}, u32[]{:S(2)}, u32[]{:S(2)}) collective-permute-start(f32[128,128]{1,0:T(8,128)S(1)} %collective-permute-done.11), channel_id=1, source_target_pairs={{0,64},{32,96},{64,128},{96,160},{128,192},{160,224},{192,0},{224,... | collective-permute-start | bytes 196616 | tf_op jit(solution)/shard_map/ppermute | solution.py:24
  60.1 1.2 %collective-permute-start.16 = (f32[128,128]{1,0:T(8,128)S(1)}, f32[128,128]{1,0:T(8,128)S(1)}, u32[]{:S(2)}, u32[]{:S(2)}) collective-permute-start(f32[128,128]{1,0:T(8,128)S(1)} %collective-permute-done.12), channel_id=1, source_target_pairs={{0,224},{32,0},{64,32},{96,64},{128,96},{160,128},{192,160},{224,1... | collective-permute-start | bytes 196616 | tf_op jit(solution)/shard_map/ppermute | solution.py:24
  61.5 1.6 %collective-permute-done.15 = f32[128,128]{1,0:T(8,128)S(1)} collective-permute-done((f32[128,128]{1,0:T(8,128)S(1)}, f32[128,128]{1,0:T(8,128)S(1)}, u32[]{:S(2)}, u32[]{:S(2)}) %collective-permute-start.15) | collective-permute-done | bytes 65568 | tf_op jit(solution)/shard_map/ppermute | solution.py:24
  63.0 1.4 %collective-permute-done.16 = f32[128,128]{1,0:T(8,128)S(1)} collective-permute-done((f32[128,128]{1,0:T(8,128)S(1)}, f32[128,128]{1,0:T(8,128)S(1)}, u32[]{:S(2)}, u32[]{:S(2)}) %collective-permute-start.16) | collective-permute-done | bytes 65568 | tf_op jit(solution)/shard_map/ppermute | solution.py:24
  64.5 3.6 %collective-permute-start.18 = (f32[8,128,128]{2,1,0:T(8,128)S(1)}, f32[8,128,128]{2,1,0:T(8,128)S(1)}, u32[]{:S(2)}, u32[]{:S(2)}) collective-permute-start(f32[8,128,128]{2,1,0:T(8,128)S(1)} %bitcast_dynamic-update-slice_fusion.8), channel_id=1, source_target_pairs={{0,1},{1,0},{2,3},{3,2},{4,5},{5,4},{6,7},{7,6},{8,9},{9,8},{10,11... | collective-permute-start | bytes 1572872 | tf_op jit(solution)/shard_map/ppermute | solution.py:28
  68.1 1.5 %collective-permute-done.18 = f32[8,128,128]{2,1,0:T(8,128)S(1)} collective-permute-done((f32[8,128,128]{2,1,0:T(8,128)S(1)}, f32[8,128,128]{2,1,0:T(8,128)S(1)}, u32[]{:S(2)}, u32[]{:S(2)}) %collective-permute-start.18) | collective-permute-done | bytes 524320 | tf_op jit(solution)/shard_map/ppermute | solution.py:28
  69.6 0.1 pad_maximum_fusion.1.column_ref.stat_column
  69.7 3.8 %all-to-all-done.1.row_ref.stat_row = f32[16,128,128]{2,1,0:T(8,128)S(1)} async-done(((f32[16,128,128]{2,1,0:T(8,128)}), f32[16,128,128]{2,1,0:T(8,128)S(1)}, u32[]{:S(2)}, u32[]{:S(2)}) %all-to-all-start.1) | async-done | bytes 1048608 | tf_op jit(solution)/shard_map/all_to_all | solution.py:36
  73.5 1.6 %shard_map.41 = (f32[16,128,128]{2,1,0:T(8,128)}, f32[136,128]{1,0:T(8,128)S(1)}) custom-call(f32[16,128,128]{2,1,0:T(8,128)S(1)} %all-to-all-done.1.row_ref.stat_row, f32[16,128,128]{2,1,0:T(8,128)S(1)} %pad_maximum_fusion.1.column_ref.stat_column), custom_call_target="tpu_custom_call" | custom-call | tf_op jit(solution)/shard_map/pallas_call | solution.py:162
  75.1 3.6 %collective-permute-start.20 = (f32[136,128]{1,0:T(8,128)S(1)}, f32[136,128]{1,0:T(8,128)S(1)}, u32[]{:S(2)}, u32[]{:S(2)}) collective-permute-start(f32[136,128]{1,0:T(8,128)S(1)} %get-tuple-element.7), channel_id=1, source_target_pairs={{0,192},{32,224},{64,0},{96,32},{128,64},{160,96},{192,128},{224,1... | collective-permute-start | bytes 208904 | tf_op jit(solution)/shard_map/ppermute | solution.py:24
  78.7 2.7 %collective-permute-start.22 = (f32[136,128]{1,0:T(8,128)S(1)}, f32[136,128]{1,0:T(8,128)S(1)}, u32[]{:S(2)}, u32[]{:S(2)}) collective-permute-start(f32[136,128]{1,0:T(8,128)S(1)} %get-tuple-element.7), channel_id=1, source_target_pairs={{0,224},{32,0},{64,32},{96,64},{128,96},{160,128},{192,160},{224,1... | collective-permute-start | bytes 208904 | tf_op jit(solution)/shard_map/ppermute | solution.py:24
  81.4 4.9 %all-to-all-start.2 = ((f32[16,128,128]{2,1,0:T(8,128)}), f32[16,128,128]{2,1,0:T(8,128)}, u32[]{:S(2)}, u32[]{:S(2)}) async-start(f32[16,128,128]{2,1,0:T(8,128)} %get-tuple-element.6), calls=%async_computation.2 | async-start | bytes 2097152 | tf_op jit(solution)/shard_map/all_to_all | solution.py:36
  86.4 0.1 collective-permute-start.23
  86.5 1.4 %collective-permute-start.25 = (f32[136,128]{1,0:T(8,128)S(1)}, f32[136,128]{1,0:T(8,128)S(1)}, u32[]{:S(2)}, u32[]{:S(2)}) collective-permute-start(f32[136,128]{1,0:T(8,128)S(1)} %collective-permute-done.19), channel_id=1, source_target_pairs={{0,64},{32,96},{64,128},{96,160},{128,192},{160,224},{192,0},{224,... | collective-permute-start | bytes 208904 | tf_op jit(solution)/shard_map/ppermute | solution.py:24
  87.9 1.3 %collective-permute-start.24 = (f32[136,128]{1,0:T(8,128)S(1)}, f32[136,128]{1,0:T(8,128)S(1)}, u32[]{:S(2)}, u32[]{:S(2)}) collective-permute-start(f32[136,128]{1,0:T(8,128)S(1)} %collective-permute-done.20), channel_id=1, source_target_pairs={{0,224},{32,0},{64,32},{96,64},{128,96},{160,128},{192,160},{224,1... | collective-permute-start | bytes 208904 | tf_op jit(solution)/shard_map/ppermute | solution.py:24
  89.3 1.5 %collective-permute-done.23 = f32[136,128]{1,0:T(8,128)S(1)} collective-permute-done((f32[136,128]{1,0:T(8,128)S(1)}, f32[136,128]{1,0:T(8,128)S(1)}, u32[]{:S(2)}, u32[]{:S(2)}) %collective-permute-start.23) | collective-permute-done | bytes 69664 | tf_op jit(solution)/shard_map/ppermute | solution.py:24
  90.8 1.5 %collective-permute-done.24 = f32[136,128]{1,0:T(8,128)S(1)} collective-permute-done((f32[136,128]{1,0:T(8,128)S(1)}, f32[136,128]{1,0:T(8,128)S(1)}, u32[]{:S(2)}, u32[]{:S(2)}) %collective-permute-start.24) | collective-permute-done | bytes 69664 | tf_op jit(solution)/shard_map/ppermute | solution.py:24
  92.4 5.4 %collective-permute-start.26 = (f32[8,136,128]{2,1,0:T(8,128)S(1)}, f32[8,136,128]{2,1,0:T(8,128)S(1)}, u32[]{:S(2)}, u32[]{:S(2)}) collective-permute-start(f32[8,136,128]{2,1,0:T(8,128)S(1)} %bitcast_dynamic-update-slice_fusion), channel_id=1, source_target_pairs={{0,1},{1,0},{2,3},{3,2},{4,5},{5,4},{6,7},{7,6},{8,9},{9,8},{10,11... | collective-permute-start | bytes 1671176 | tf_op jit(solution)/shard_map/ppermute | solution.py:28
  97.8 3.3 %collective-permute-start.27 = (f32[128,128]{1,0:T(8,128)S(1)}, f32[128,128]{1,0:T(8,128)S(1)}, u32[]{:S(2)}, u32[]{:S(2)}) collective-permute-start(f32[128,128]{1,0:T(8,128)S(1)} %get-tuple-element.15.stat), channel_id=1, source_target_pairs={{0,0},{1,16},{16,1},{17,17},{2,2},{3,18},{18,3},{19,19},{4,4},{5,2... | collective-permute-start | bytes 196616 | tf_op jit(solution)/shard_map/ppermute | solution.py:32
  101.1 2.6 %collective-permute-done.27.home = f32[128,128]{1,0:T(8,128)S(1)} collective-permute-done((f32[128,128]{1,0:T(8,128)S(1)}, f32[128,128]{1,0:T(8,128)S(1)}, u32[]{:S(2)}, u32[]{:S(2)}) %collective-permute-start.27) | collective-permute-done | bytes 65568 | tf_op jit(solution)/shard_map/ppermute | solution.py:32
  103.7 2.7 %shard_map.42 = (f32[128,128]{1,0:T(8,128)S(1)}, f32[128,128]{1,0:T(8,128)}) custom-call(f32[16,128,128]{2,1,0:T(8,128)} %all-to-all-done.2.square_row, f32[16,128,128]{2,1,0:T(8,128)S(1)} %all-to-all-done.1.row_ref.stat_row, f32[16,136,128]{2,1,0:T(8,128)S(1)} %pad_maximum_fusion.square_column, ...), custom_call_target="tpu_custom_call" | custom-call | tf_op jit(solution)/shard_map/pallas_call | solution.py:162
  106.4 3.4 %collective-permute-start.28 = (f32[128,128]{1,0:T(8,128)S(1)}, f32[128,128]{1,0:T(8,128)S(1)}, u32[]{:S(2)}, u32[]{:S(2)}) collective-permute-start(f32[128,128]{1,0:T(8,128)S(1)} %get-tuple-element.9), channel_id=1, source_target_pairs={{0,0},{1,16},{16,1},{17,17},{2,2},{3,18},{18,3},{19,19},{4,4},{5,2... | collective-permute-start | bytes 196616 | tf_op jit(solution)/shard_map/ppermute | solution.py:32
  109.8 2.2 %collective-permute-done.28 = f32[128,128]{1,0:T(8,128)S(1)} collective-permute-done((f32[128,128]{1,0:T(8,128)S(1)}, f32[128,128]{1,0:T(8,128)S(1)}, u32[]{:S(2)}, u32[]{:S(2)}) %collective-permute-start.28) | collective-permute-done | bytes 65568 | tf_op jit(solution)/shard_map/ppermute | solution.py:32
  112.0 0.6 copy.30
  (54 shorter events, 0.5 us)
Async XLA Ops:
  0.6 12.6 %collective-permute-start.2 = (f32[32,128]{1,0:T(8,128)}, f32[32,128]{1,0:T(8,128)S(1)}, u32[]{:S(2)}, u32[]{:S(2)}) collective-permute-start(f32[32,128]{1,0:T(8,128)} %bitcast.68), channel_id=1, source_target_pairs={{10,0},{11,1},{44,2},{45,3},{76,4},{77,5},{98,6},{99,7},{136,8},{1... | collective-permute-start | bytes 49160 | tf_op jit(solution)/shard_map/ppermute | solution.py:73
  8.4 23.2 %collective-permute-start.1 = (f32[32,128]{1,0:T(8,128)}, f32[32,128]{1,0:T(8,128)S(1)}, u32[]{:S(2)}, u32[]{:S(2)}) collective-permute-start(f32[32,128]{1,0:T(8,128)} %bitcast.69), channel_id=1, source_target_pairs={{0,16},{16,0},{1,17},{17,1},{2,18},{18,2},{3,19},{19,3},{4,20},{20... | collective-permute-start | bytes 49160 | tf_op jit(solution)/shard_map/ppermute | solution.py:28
  9.6 28.4 %collective-permute-start = (f32[128,128]{1,0:T(8,128)}, f32[128,128]{1,0:T(8,128)S(1)}, u32[]{:S(2)}, u32[]{:S(2)}) collective-permute-start(f32[128,128]{1,0:T(8,128)} %param.3), channel_id=1, source_target_pairs={{0,0},{1,16},{16,1},{17,17},{2,2},{3,18},{18,3},{19,19},{4,4},{5,2... | collective-permute-start | bytes 196616 | tf_op jit(solution)/shard_map/ppermute | solution.py:32
  13.3 5.2 %collective-permute-start.3 = (f32[32,128]{1,0:T(8,128)S(1)}, f32[32,128]{1,0:T(8,128)S(1)}, u32[]{:S(2)}, u32[]{:S(2)}) collective-permute-start(f32[32,128]{1,0:T(8,128)S(1)} %collective-permute-done.2), channel_id=1, source_target_pairs={{0,64},{32,96},{64,128},{96,160},{128,192},{160,224},{192,0},{224,... | collective-permute-start | bytes 49160 | tf_op jit(solution)/shard_map/ppermute | solution.py:24
  15.1 4.6 %collective-permute-start.4 = (f32[32,128]{1,0:T(8,128)S(1)}, f32[32,128]{1,0:T(8,128)S(1)}, u32[]{:S(2)}, u32[]{:S(2)}) collective-permute-start(f32[32,128]{1,0:T(8,128)S(1)} %collective-permute-done.2), channel_id=1, source_target_pairs={{0,192},{32,224},{64,0},{96,32},{128,64},{160,96},{192,128},{224,1... | collective-permute-start | bytes 49160 | tf_op jit(solution)/shard_map/ppermute | solution.py:24
  16.9 4.3 %collective-permute-start.5 = (f32[32,128]{1,0:T(8,128)S(1)}, f32[32,128]{1,0:T(8,128)S(1)}, u32[]{:S(2)}, u32[]{:S(2)}) collective-permute-start(f32[32,128]{1,0:T(8,128)S(1)} %collective-permute-done.2), channel_id=1, source_target_pairs={{0,32},{32,64},{64,96},{96,128},{128,160},{160,192},{192,224},{224... | collective-permute-start | bytes 49160 | tf_op jit(solution)/shard_map/ppermute | solution.py:24
  18.4 4.0 %collective-permute-start.6 = (f32[32,128]{1,0:T(8,128)S(1)}, f32[32,128]{1,0:T(8,128)S(1)}, u32[]{:S(2)}, u32[]{:S(2)}) collective-permute-start(f32[32,128]{1,0:T(8,128)S(1)} %collective-permute-done.2), channel_id=1, source_target_pairs={{0,224},{32,0},{64,32},{96,64},{128,96},{160,128},{192,160},{224,1... | collective-permute-start | bytes 49160 | tf_op jit(solution)/shard_map/ppermute | solution.py:24
  19.7 4.8 %collective-permute-start.7 = (f32[32,128]{1,0:T(8,128)S(1)}, f32[32,128]{1,0:T(8,128)S(1)}, u32[]{:S(2)}, u32[]{:S(2)}) collective-permute-start(f32[32,128]{1,0:T(8,128)S(1)} %collective-permute-done.3), channel_id=1, source_target_pairs={{0,32},{32,64},{64,96},{96,128},{128,160},{160,192},{192,224},{224... | collective-permute-start | bytes 49160 | tf_op jit(solution)/shard_map/ppermute | solution.py:24
  21.2 3.4 %collective-permute-start.8 = (f32[32,128]{1,0:T(8,128)S(1)}, f32[32,128]{1,0:T(8,128)S(1)}, u32[]{:S(2)}, u32[]{:S(2)}) collective-permute-start(f32[32,128]{1,0:T(8,128)S(1)} %collective-permute-done.4), channel_id=1, source_target_pairs={{0,224},{32,0},{64,32},{96,64},{128,96},{160,128},{192,160},{224,1... | collective-permute-start | bytes 49160 | tf_op jit(solution)/shard_map/ppermute | solution.py:24
  22.4 4.7 %collective-permute-start.9 = (f32[32,128]{1,0:T(8,128)S(1)}, f32[32,128]{1,0:T(8,128)S(1)}, u32[]{:S(2)}, u32[]{:S(2)}) collective-permute-start(f32[32,128]{1,0:T(8,128)S(1)} %collective-permute-done.3), channel_id=1, source_target_pairs={{0,64},{32,96},{64,128},{96,160},{128,192},{160,224},{192,0},{224,... | collective-permute-start | bytes 49160 | tf_op jit(solution)/shard_map/ppermute | solution.py:24
  27.1 10.9 %collective-permute-start.10 = (f32[8,32,128]{2,1,0:T(8,128)S(1)}, f32[8,32,128]{2,1,0:T(8,128)S(1)}, u32[]{:S(2)}, u32[]{:S(2)}) collective-permute-start(f32[8,32,128]{2,1,0:T(8,128)S(1)} %bitcast_dynamic-update-slice_fusion.16), channel_id=1, source_target_pairs={{0,1},{1,0},{2,3},{3,2},{4,5},{5,4},{6,7},{7,6},{8,9},{9,8},{10,11... | collective-permute-start | bytes 393224 | tf_op jit(solution)/shard_map/ppermute | solution.py:28
  33.0 13.7 %all-to-all-start = ((f32[16,32,128]{2,1,0:T(8,128)}), f32[16,32,128]{2,1,0:T(8,128)S(1)}, u32[]{:S(2)}, u32[]{:S(2)}) async-start(f32[16,32,128]{2,1,0:T(8,128)} %bitcast.3), calls=%async_computation | async-start | bytes 524288 | tf_op jit(solution)/shard_map/all_to_all | solution.py:82
  47.4 11.1 %collective-permute-start.11 = (f32[128,128]{1,0:T(8,128)S(1)}, f32[128,128]{1,0:T(8,128)S(1)}, u32[]{:S(2)}, u32[]{:S(2)}) collective-permute-start(f32[128,128]{1,0:T(8,128)S(1)} %get-tuple-element.15.stat), channel_id=1, source_target_pairs={{0,64},{32,96},{64,128},{96,160},{128,192},{160,224},{192,0},{224,... | collective-permute-start | bytes 196616 | tf_op jit(solution)/shard_map/ppermute | solution.py:24
  47.5 12.7 %collective-permute-start.12 = (f32[128,128]{1,0:T(8,128)S(1)}, f32[128,128]{1,0:T(8,128)S(1)}, u32[]{:S(2)}, u32[]{:S(2)}) collective-permute-start(f32[128,128]{1,0:T(8,128)S(1)} %get-tuple-element.15.stat), channel_id=1, source_target_pairs={{0,192},{32,224},{64,0},{96,32},{128,64},{160,96},{192,128},{224,1... | collective-permute-start | bytes 196616 | tf_op jit(solution)/shard_map/ppermute | solution.py:24
  51.0 10.4 %collective-permute-start.13 = (f32[128,128]{1,0:T(8,128)S(1)}, f32[128,128]{1,0:T(8,128)S(1)}, u32[]{:S(2)}, u32[]{:S(2)}) collective-permute-start(f32[128,128]{1,0:T(8,128)S(1)} %get-tuple-element.15.stat), channel_id=1, source_target_pairs={{0,32},{32,64},{64,96},{96,128},{128,160},{160,192},{192,224},{224... | collective-permute-start | bytes 196616 | tf_op jit(solution)/shard_map/ppermute | solution.py:24
  51.0 10.4 %collective-permute-start.14 = (f32[128,128]{1,0:T(8,128)S(1)}, f32[128,128]{1,0:T(8,128)S(1)}, u32[]{:S(2)}, u32[]{:S(2)}) collective-permute-start(f32[128,128]{1,0:T(8,128)S(1)} %get-tuple-element.15.stat), channel_id=1, source_target_pairs={{0,224},{32,0},{64,32},{96,64},{128,96},{160,128},{192,160},{224,1... | collective-permute-start | bytes 196616 | tf_op jit(solution)/shard_map/ppermute | solution.py:24
  54.8 18.7 %all-to-all-start.1 = ((f32[16,128,128]{2,1,0:T(8,128)}), f32[16,128,128]{2,1,0:T(8,128)S(1)}, u32[]{:S(2)}, u32[]{:S(2)}) async-start(f32[16,128,128]{2,1,0:T(8,128)} %broadcast_in_dim.96), calls=%async_computation.1 | async-start | bytes 2097152 | tf_op jit(solution)/shard_map/all_to_all | solution.py:36
  58.4 4.6 %collective-permute-start.15 = (f32[128,128]{1,0:T(8,128)S(1)}, f32[128,128]{1,0:T(8,128)S(1)}, u32[]{:S(2)}, u32[]{:S(2)}) collective-permute-start(f32[128,128]{1,0:T(8,128)S(1)} %collective-permute-done.11), channel_id=1, source_target_pairs={{0,32},{32,64},{64,96},{96,128},{128,160},{160,192},{192,224},{224... | collective-permute-start | bytes 196616 | tf_op jit(solution)/shard_map/ppermute | solution.py:24
  58.7 5.8 %collective-permute-start.17 = (f32[128,128]{1,0:T(8,128)S(1)}, f32[128,128]{1,0:T(8,128)S(1)}, u32[]{:S(2)}, u32[]{:S(2)}) collective-permute-start(f32[128,128]{1,0:T(8,128)S(1)} %collective-permute-done.11), channel_id=1, source_target_pairs={{0,64},{32,96},{64,128},{96,160},{128,192},{160,224},{192,0},{224,... | collective-permute-start | bytes 196616 | tf_op jit(solution)/shard_map/ppermute | solution.py:24
  60.1 4.3 %collective-permute-start.16 = (f32[128,128]{1,0:T(8,128)S(1)}, f32[128,128]{1,0:T(8,128)S(1)}, u32[]{:S(2)}, u32[]{:S(2)}) collective-permute-start(f32[128,128]{1,0:T(8,128)S(1)} %collective-permute-done.12), channel_id=1, source_target_pairs={{0,224},{32,0},{64,32},{96,64},{128,96},{160,128},{192,160},{224,1... | collective-permute-start | bytes 196616 | tf_op jit(solution)/shard_map/ppermute | solution.py:24
  64.5 5.1 %collective-permute-start.18 = (f32[8,128,128]{2,1,0:T(8,128)S(1)}, f32[8,128,128]{2,1,0:T(8,128)S(1)}, u32[]{:S(2)}, u32[]{:S(2)}) collective-permute-start(f32[8,128,128]{2,1,0:T(8,128)S(1)} %bitcast_dynamic-update-slice_fusion.8), channel_id=1, source_target_pairs={{0,1},{1,0},{2,3},{3,2},{4,5},{5,4},{6,7},{7,6},{8,9},{9,8},{10,11... | collective-permute-start | bytes 1572872 | tf_op jit(solution)/shard_map/ppermute | solution.py:28
  75.1 11.2 %collective-permute-start.19 = (f32[136,128]{1,0:T(8,128)S(1)}, f32[136,128]{1,0:T(8,128)S(1)}, u32[]{:S(2)}, u32[]{:S(2)}) collective-permute-start(f32[136,128]{1,0:T(8,128)S(1)} %get-tuple-element.7), channel_id=1, source_target_pairs={{0,64},{32,96},{64,128},{96,160},{128,192},{160,224},{192,0},{224,... | collective-permute-start | bytes 208904 | tf_op jit(solution)/shard_map/ppermute | solution.py:24
  75.1 12.8 %collective-permute-start.20 = (f32[136,128]{1,0:T(8,128)S(1)}, f32[136,128]{1,0:T(8,128)S(1)}, u32[]{:S(2)}, u32[]{:S(2)}) collective-permute-start(f32[136,128]{1,0:T(8,128)S(1)} %get-tuple-element.7), channel_id=1, source_target_pairs={{0,192},{32,224},{64,0},{96,32},{128,64},{160,96},{192,128},{224,1... | collective-permute-start | bytes 208904 | tf_op jit(solution)/shard_map/ppermute | solution.py:24
  78.7 10.5 %collective-permute-start.21 = (f32[136,128]{1,0:T(8,128)S(1)}, f32[136,128]{1,0:T(8,128)S(1)}, u32[]{:S(2)}, u32[]{:S(2)}) collective-permute-start(f32[136,128]{1,0:T(8,128)S(1)} %get-tuple-element.7), channel_id=1, source_target_pairs={{0,32},{32,64},{64,96},{96,128},{128,160},{160,192},{192,224},{224... | collective-permute-start | bytes 208904 | tf_op jit(solution)/shard_map/ppermute | solution.py:24
  78.7 10.6 %collective-permute-start.22 = (f32[136,128]{1,0:T(8,128)S(1)}, f32[136,128]{1,0:T(8,128)S(1)}, u32[]{:S(2)}, u32[]{:S(2)}) collective-permute-start(f32[136,128]{1,0:T(8,128)S(1)} %get-tuple-element.7), channel_id=1, source_target_pairs={{0,224},{32,0},{64,32},{96,64},{128,96},{160,128},{192,160},{224,1... | collective-permute-start | bytes 208904 | tf_op jit(solution)/shard_map/ppermute | solution.py:24
  81.4 22.4 %all-to-all-start.2 = ((f32[16,128,128]{2,1,0:T(8,128)}), f32[16,128,128]{2,1,0:T(8,128)}, u32[]{:S(2)}, u32[]{:S(2)}) async-start(f32[16,128,128]{2,1,0:T(8,128)} %get-tuple-element.6), calls=%async_computation.2 | async-start | bytes 2097152 | tf_op jit(solution)/shard_map/all_to_all | solution.py:36
  86.4 4.4 %collective-permute-start.23 = (f32[136,128]{1,0:T(8,128)S(1)}, f32[136,128]{1,0:T(8,128)S(1)}, u32[]{:S(2)}, u32[]{:S(2)}) collective-permute-start(f32[136,128]{1,0:T(8,128)S(1)} %collective-permute-done.19), channel_id=1, source_target_pairs={{0,32},{32,64},{64,96},{96,128},{128,160},{160,192},{192,224},{224... | collective-permute-start | bytes 208904 | tf_op jit(solution)/shard_map/ppermute | solution.py:24
  86.5 5.9 %collective-permute-start.25 = (f32[136,128]{1,0:T(8,128)S(1)}, f32[136,128]{1,0:T(8,128)S(1)}, u32[]{:S(2)}, u32[]{:S(2)}) collective-permute-start(f32[136,128]{1,0:T(8,128)S(1)} %collective-permute-done.19), channel_id=1, source_target_pairs={{0,64},{32,96},{64,128},{96,160},{128,192},{160,224},{192,0},{224,... | collective-permute-start | bytes 208904 | tf_op jit(solution)/shard_map/ppermute | solution.py:24
  87.9 4.5 %collective-permute-start.24 = (f32[136,128]{1,0:T(8,128)S(1)}, f32[136,128]{1,0:T(8,128)S(1)}, u32[]{:S(2)}, u32[]{:S(2)}) collective-permute-start(f32[136,128]{1,0:T(8,128)S(1)} %collective-permute-done.20), channel_id=1, source_target_pairs={{0,224},{32,0},{64,32},{96,64},{128,96},{160,128},{192,160},{224,1... | collective-permute-start | bytes 208904 | tf_op jit(solution)/shard_map/ppermute | solution.py:24
  92.4 8.6 %collective-permute-start.26 = (f32[8,136,128]{2,1,0:T(8,128)S(1)}, f32[8,136,128]{2,1,0:T(8,128)S(1)}, u32[]{:S(2)}, u32[]{:S(2)}) collective-permute-start(f32[8,136,128]{2,1,0:T(8,128)S(1)} %bitcast_dynamic-update-slice_fusion), channel_id=1, source_target_pairs={{0,1},{1,0},{2,3},{3,2},{4,5},{5,4},{6,7},{7,6},{8,9},{9,8},{10,11... | collective-permute-start | bytes 1671176 | tf_op jit(solution)/shard_map/ppermute | solution.py:28
  97.8 6.0 %collective-permute-start.27 = (f32[128,128]{1,0:T(8,128)S(1)}, f32[128,128]{1,0:T(8,128)S(1)}, u32[]{:S(2)}, u32[]{:S(2)}) collective-permute-start(f32[128,128]{1,0:T(8,128)S(1)} %get-tuple-element.15.stat), channel_id=1, source_target_pairs={{0,0},{1,16},{16,1},{17,17},{2,2},{3,18},{18,3},{19,19},{4,4},{5,2... | collective-permute-start | bytes 196616 | tf_op jit(solution)/shard_map/ppermute | solution.py:32
  106.4 5.6 %collective-permute-start.28 = (f32[128,128]{1,0:T(8,128)S(1)}, f32[128,128]{1,0:T(8,128)S(1)}, u32[]{:S(2)}, u32[]{:S(2)}) collective-permute-start(f32[128,128]{1,0:T(8,128)S(1)} %get-tuple-element.9), channel_id=1, source_target_pairs={{0,0},{1,16},{16,1},{17,17},{2,2},{3,18},{18,3},{19,19},{4,4},{5,2... | collective-permute-start | bytes 196616 | tf_op jit(solution)/shard_map/ppermute | solution.py:32

commit v4 on v3

--- a/solution.py
+++ b/solution.py
@@ -88,7 +88,7 @@
         (jnp.where(core == 0, mine, other), jnp.where(core == 0, other, mine)), axis=1
     )
     width = piece.shape[1]
-    return matmul(rows_of.reshape(-1, width).T, columns_of.reshape(-1, width))
+    return rows_of.reshape(-1, width), columns_of.reshape(-1, width)
 
 
 def split(array):
@@ -104,6 +104,14 @@
         return jnp.dot(one, two, preferred_element_type=jnp.float32)
 
     return dot(left_high, right_high) + (dot(left_high, right_low) + dot(left_low, right_high))
+
+
+def stat_kernel(rows_ref, columns_ref, old_ref, copies_ref, stat_ref):
+    outer = matmul(rows_ref[...].T, columns_ref[...])
+    total = 0.9 * old_ref[...] + outer / rows_ref.shape[0]
+    for number in range(copies_ref.shape[0]):
+        copies_ref[number] = total
+    stat_ref[...] = total
 
 
 def square_kernel(row_ref, column_ref, copies_ref, carried_ref):
@@ -170,11 +178,13 @@
 
 def local(gradient, stat_old):
     side = stat_old.shape[0]
-    outer = outer_part(gradient)
+    rows_of, columns_of = outer_part(gradient)
     stat_moved = turn(stat_old)
-    stat = 0.9 * stat_moved + outer / (gradient.shape[1] * 16)
-
-    stat_row = row_panel(jnp.broadcast_to(stat[None], (16,) + stat.shape))
+    copies, stat = call(
+        stat_kernel, ((16, side, side), (side, side)), rows_of, columns_of, stat_moved
+    )
+
+    stat_row = row_panel(copies)
     stat_column = column_pieces(stat)
     home = turn(stat)
     copies, carried = call(

time: 113 us -> 114 us (level)
  Pallas kernels: 4.33 us -> 5.81 us
    ppermute x4, starting transfers between devices: 14.6 us -> 16.1 us  [swap(): return lax.ppermute(array, axis, [(0, 1), (1, 0)])]
    pallas_call x2 -> x3, Pallas kernels: 4.33 us -> 5.81 us  [call(): pl.pallas_call(kernel, out_shape=[jax.ShapeDtypeStruct(shape, jnp.float32...]
  transfers between devices with their start and end apart: 32 -> 32, of which waited for: 11 -> 14; matrix products, arithmetic and copies ran while one was open for 3% -> 2% of each run, Pallas kernels for 0% -> 0%
where the time goes in v4:
time: 114 us
  starting transfers between devices  74.8 us (66%)
  waiting for transfers between devices  29 us (25%)
  Pallas kernels  5.81 us (5%)
  local copies, waits for them, and re-layouts  1.63 us (1%)
  between operations  1.33 us (1%)
    ppermute x21, starting transfers between devices, rotate(): lax.ppermute(array, axis, [(s, (s + shift) % size) for s in range(size)])  28.4 us
    ppermute x4, starting transfers between devices, swap(): return lax.ppermute(array, axis, [(0, 1), (1, 0)])  16.1 us
    ppermute x21, waiting for transfers between devices, rotate(): lax.ppermute(array, axis, [(s, (s + shift) % size) for s in range(size)])  10.4 us
    ppermute x3, starting transfers between devices, turn(): return lax.ppermute(array, (XL, CORE), [(0, 0), (1, 2), (2, 1), (3, 3)])  10 us
    all_to_all x1, waiting for transfers between devices, outer_part(): rows_of = lax.all_to_all(jnp.tile(pair, (8, 1, 1)), GY, 0, 0, tiled=True)  8.62 us
    all_to_all x2, starting transfers between devices, row_panel(): return lax.all_to_all(copies, (Y, XH, XL), 0, 0, tiled=True)  8.56 us
    ppermute x1, starting transfers between devices, exchange(): return lax.ppermute(array, (Z, XL, Y, XH, CORE), pairs)  6.91 us
    pallas_call x3, Pallas kernels, call(): pl.pallas_call(kernel, out_shape=[jax.ShapeDtypeStruct(shape, jnp.float32...  5.81 us
  transfers between devices with their start and end apart: 32, of which 14 were waited for; matrix products, arithmetic and copies ran while one was open for 2% of the time, Pallas kernels for 0%

profile of v4, /device:TPU:1, one launch (start us, length us, event | category | flops | bytes accessed | tf_op | source)
XLA Modules:
  0.0 113.5 jit_solution(2893852962709269131)
XLA Ops:
  0.6 2.1 %collective-permute-start = (f32[32,128]{1,0:T(8,128)}, f32[32,128]{1,0:T(8,128)S(1)}, u32[]{:S(2)}, u32[]{:S(2)}) collective-permute-start(f32[32,128]{1,0:T(8,128)} %bitcast.66), channel_id=1, source_target_pairs={{0,16},{16,0},{1,17},{17,1},{2,18},{18,2},{3,19},{19,3},{4,20},{20... | collective-permute-start | bytes 49160 | tf_op jit(solution)/shard_map/ppermute | solution.py:28
  2.7 6.9 %collective-permute-start.1 = (f32[32,128]{1,0:T(8,128)}, f32[32,128]{1,0:T(8,128)S(1)}, u32[]{:S(2)}, u32[]{:S(2)}) collective-permute-start(f32[32,128]{1,0:T(8,128)} %bitcast.67), channel_id=1, source_target_pairs={{10,0},{11,1},{44,2},{45,3},{76,4},{77,5},{98,6},{99,7},{136,8},{1... | collective-permute-start | bytes 49160 | tf_op jit(solution)/shard_map/ppermute | solution.py:73
  9.7 3.3 %collective-permute-start.10 = (f32[128,128]{1,0:T(8,128)}, f32[128,128]{1,0:T(8,128)S(1)}, u32[]{:S(2)}, u32[]{:S(2)}) collective-permute-start(f32[128,128]{1,0:T(8,128)} %param.3), channel_id=1, source_target_pairs={{0,0},{1,16},{16,1},{17,17},{2,2},{3,18},{18,3},{19,19},{4,4},{5,2... | collective-permute-start | bytes 196616 | tf_op jit(solution)/shard_map/ppermute | solution.py:32
  13.3 1.8 %collective-permute-start.2 = (f32[32,128]{1,0:T(8,128)S(1)}, f32[32,128]{1,0:T(8,128)S(1)}, u32[]{:S(2)}, u32[]{:S(2)}) collective-permute-start(f32[32,128]{1,0:T(8,128)S(1)} %collective-permute-done.1), channel_id=1, source_target_pairs={{0,64},{32,96},{64,128},{96,160},{128,192},{160,224},{192,0},{224,... | collective-permute-start | bytes 49160 | tf_op jit(solution)/shard_map/ppermute | solution.py:24
  15.1 1.8 %collective-permute-start.3 = (f32[32,128]{1,0:T(8,128)S(1)}, f32[32,128]{1,0:T(8,128)S(1)}, u32[]{:S(2)}, u32[]{:S(2)}) collective-permute-start(f32[32,128]{1,0:T(8,128)S(1)} %collective-permute-done.1), channel_id=1, source_target_pairs={{0,192},{32,224},{64,0},{96,32},{128,64},{160,96},{192,128},{224,1... | collective-permute-start | bytes 49160 | tf_op jit(solution)/shard_map/ppermute | solution.py:24
  17.0 1.1 collective-permute-start.4
  18.1 0.1 collective-permute-done.2
  18.1 2.2 %collective-permute-start.5 = (f32[32,128]{1,0:T(8,128)S(1)}, f32[32,128]{1,0:T(8,128)S(1)}, u32[]{:S(2)}, u32[]{:S(2)}) collective-permute-start(f32[32,128]{1,0:T(8,128)S(1)} %collective-permute-done.1), channel_id=1, source_target_pairs={{0,224},{32,0},{64,32},{96,64},{128,96},{160,128},{192,160},{224,1... | collective-permute-start | bytes 49160 | tf_op jit(solution)/shard_map/ppermute | solution.py:24
  20.4 0.4 collective-permute-done.4
  20.8 2.3 %collective-permute-start.7 = (f32[32,128]{1,0:T(8,128)S(1)}, f32[32,128]{1,0:T(8,128)S(1)}, u32[]{:S(2)}, u32[]{:S(2)}) collective-permute-start(f32[32,128]{1,0:T(8,128)S(1)} %collective-permute-done.3), channel_id=1, source_target_pairs={{0,224},{32,0},{64,32},{96,64},{128,96},{160,128},{192,160},{224,1... | collective-permute-start | bytes 49160 | tf_op jit(solution)/shard_map/ppermute | solution.py:24
  23.0 1.0 collective-permute-start.8
  24.0 0.1 collective-permute-done.6
  24.2 3.8 %collective-permute-done.8 = f32[32,128]{1,0:T(8,128)S(1)} collective-permute-done((f32[32,128]{1,0:T(8,128)S(1)}, f32[32,128]{1,0:T(8,128)S(1)}, u32[]{:S(2)}, u32[]{:S(2)}) %collective-permute-start.8) | collective-permute-done | bytes 16416 | tf_op jit(solution)/shard_map/ppermute | solution.py:24
  27.9 5.1 %collective-permute-start.9 = (f32[8,32,128]{2,1,0:T(8,128)S(1)}, f32[8,32,128]{2,1,0:T(8,128)S(1)}, u32[]{:S(2)}, u32[]{:S(2)}) collective-permute-start(f32[8,32,128]{2,1,0:T(8,128)S(1)} %bitcast_dynamic-update-slice_fusion.16), channel_id=1, source_target_pairs={{0,1},{1,0},{2,3},{3,2},{4,5},{5,4},{6,7},{7,6},{8,9},{9,8},{10,11... | collective-permute-start | bytes 393224 | tf_op jit(solution)/shard_map/ppermute | solution.py:28
  33.1 0.7 select_bitcast_fusion.3
  33.8 0.7 tile.4
  34.5 4.8 %all-to-all-start = ((f32[16,32,128]{2,1,0:T(8,128)}), f32[16,32,128]{2,1,0:T(8,128)S(1)}, u32[]{:S(2)}, u32[]{:S(2)}) async-start(f32[16,32,128]{2,1,0:T(8,128)} %bitcast.3), calls=%async_computation | async-start | bytes 524288 | tf_op jit(solution)/shard_map/all_to_all | solution.py:82
  39.4 8.6 %all-to-all-done = f32[16,32,128]{2,1,0:T(8,128)S(1)} async-done(((f32[16,32,128]{2,1,0:T(8,128)}), f32[16,32,128]{2,1,0:T(8,128)S(1)}, u32[]{:S(2)}, u32[]{:S(2)}) %all-to-all-start) | async-done | bytes 262176 | tf_op jit(solution)/shard_map/all_to_all | solution.py:82
  48.0 1.5 %shard_map.41 = (f32[16,128,128]{2,1,0:T(8,128)}, f32[128,128]{1,0:T(8,128)S(1)}) custom-call(f32[512,128]{1,0:T(8,128)S(1)} %bitcast.64, f32[512,128]{1,0:T(8,128)S(1)} %bitcast.65, f32[128,128]{1,0:T(8,128)S(1)} %collective-permute-done.10.old_ref), custom_call_target="tpu_custom_call" | custom-call | tf_op jit(solution)/shard_map/pallas_call | solution.py:170
  49.5 3.6 %collective-permute-start.12 = (f32[128,128]{1,0:T(8,128)S(1)}, f32[128,128]{1,0:T(8,128)S(1)}, u32[]{:S(2)}, u32[]{:S(2)}) collective-permute-start(f32[128,128]{1,0:T(8,128)S(1)} %get-tuple-element.9.stat), channel_id=1, source_target_pairs={{0,192},{32,224},{64,0},{96,32},{128,64},{160,96},{192,128},{224,1... | collective-permute-start | bytes 196616 | tf_op jit(solution)/shard_map/ppermute | solution.py:24
  53.1 2.7 %collective-permute-start.14 = (f32[128,128]{1,0:T(8,128)S(1)}, f32[128,128]{1,0:T(8,128)S(1)}, u32[]{:S(2)}, u32[]{:S(2)}) collective-permute-start(f32[128,128]{1,0:T(8,128)S(1)} %get-tuple-element.9.stat), channel_id=1, source_target_pairs={{0,224},{32,0},{64,32},{96,64},{128,96},{160,128},{192,160},{224,1... | collective-permute-start | bytes 196616 | tf_op jit(solution)/shard_map/ppermute | solution.py:24
  55.7 3.7 %all-to-all-start.1 = ((f32[16,128,128]{2,1,0:T(8,128)}), f32[16,128,128]{2,1,0:T(8,128)S(1)}, u32[]{:S(2)}, u32[]{:S(2)}) async-start(f32[16,128,128]{2,1,0:T(8,128)} %get-tuple-element.8), calls=%async_computation.1 | async-start | bytes 2097152 | tf_op jit(solution)/shard_map/all_to_all | solution.py:36
  59.5 0.3 collective-permute-start.15
  59.8 1.3 %collective-permute-start.17 = (f32[128,128]{1,0:T(8,128)S(1)}, f32[128,128]{1,0:T(8,128)S(1)}, u32[]{:S(2)}, u32[]{:S(2)}) collective-permute-start(f32[128,128]{1,0:T(8,128)S(1)} %collective-permute-done.11), channel_id=1, source_target_pairs={{0,64},{32,96},{64,128},{96,160},{128,192},{160,224},{192,0},{224,... | collective-permute-start | bytes 196616 | tf_op jit(solution)/shard_map/ppermute | solution.py:24
  61.1 1.3 %collective-permute-start.16 = (f32[128,128]{1,0:T(8,128)S(1)}, f32[128,128]{1,0:T(8,128)S(1)}, u32[]{:S(2)}, u32[]{:S(2)}) collective-permute-start(f32[128,128]{1,0:T(8,128)S(1)} %collective-permute-done.12), channel_id=1, source_target_pairs={{0,224},{32,0},{64,32},{96,64},{128,96},{160,128},{192,160},{224,1... | collective-permute-start | bytes 196616 | tf_op jit(solution)/shard_map/ppermute | solution.py:24
  62.5 1.6 %collective-permute-done.15 = f32[128,128]{1,0:T(8,128)S(1)} collective-permute-done((f32[128,128]{1,0:T(8,128)S(1)}, f32[128,128]{1,0:T(8,128)S(1)}, u32[]{:S(2)}, u32[]{:S(2)}) %collective-permute-start.15) | collective-permute-done | bytes 65568 | tf_op jit(solution)/shard_map/ppermute | solution.py:24
  64.1 1.4 %collective-permute-done.16 = f32[128,128]{1,0:T(8,128)S(1)} collective-permute-done((f32[128,128]{1,0:T(8,128)S(1)}, f32[128,128]{1,0:T(8,128)S(1)}, u32[]{:S(2)}, u32[]{:S(2)}) %collective-permute-start.16) | collective-permute-done | bytes 65568 | tf_op jit(solution)/shard_map/ppermute | solution.py:24
  65.5 3.5 %collective-permute-start.18 = (f32[8,128,128]{2,1,0:T(8,128)S(1)}, f32[8,128,128]{2,1,0:T(8,128)S(1)}, u32[]{:S(2)}, u32[]{:S(2)}) collective-permute-start(f32[8,128,128]{2,1,0:T(8,128)S(1)} %bitcast_dynamic-update-slice_fusion.8), channel_id=1, source_target_pairs={{0,1},{1,0},{2,3},{3,2},{4,5},{5,4},{6,7},{7,6},{8,9},{9,8},{10,11... | collective-permute-start | bytes 1572872 | tf_op jit(solution)/shard_map/ppermute | solution.py:28
  69.0 1.5 %collective-permute-done.18 = f32[8,128,128]{2,1,0:T(8,128)S(1)} collective-permute-done((f32[8,128,128]{2,1,0:T(8,128)S(1)}, f32[8,128,128]{2,1,0:T(8,128)S(1)}, u32[]{:S(2)}, u32[]{:S(2)}) %collective-permute-start.18) | collective-permute-done | bytes 524320 | tf_op jit(solution)/shard_map/ppermute | solution.py:28
  70.6 0.1 pad_maximum_fusion.1.column_ref.stat_column
  70.7 3.8 %all-to-all-done.1.row_ref.stat_row = f32[16,128,128]{2,1,0:T(8,128)S(1)} async-done(((f32[16,128,128]{2,1,0:T(8,128)}), f32[16,128,128]{2,1,0:T(8,128)S(1)}, u32[]{:S(2)}, u32[]{:S(2)}) %all-to-all-start.1) | async-done | bytes 1048608 | tf_op jit(solution)/shard_map/all_to_all | solution.py:36
  74.5 1.6 %shard_map.42 = (f32[16,128,128]{2,1,0:T(8,128)}, f32[136,128]{1,0:T(8,128)S(1)}) custom-call(f32[16,128,128]{2,1,0:T(8,128)S(1)} %all-to-all-done.1.row_ref.stat_row, f32[16,128,128]{2,1,0:T(8,128)S(1)} %pad_maximum_fusion.1.column_ref.stat_column), custom_call_target="tpu_custom_call" | custom-call | tf_op jit(solution)/shard_map/pallas_call | solution.py:170
  76.1 3.6 %collective-permute-start.20 = (f32[136,128]{1,0:T(8,128)S(1)}, f32[136,128]{1,0:T(8,128)S(1)}, u32[]{:S(2)}, u32[]{:S(2)}) collective-permute-start(f32[136,128]{1,0:T(8,128)S(1)} %get-tuple-element.11), channel_id=1, source_target_pairs={{0,192},{32,224},{64,0},{96,32},{128,64},{160,96},{192,128},{224,1... | collective-permute-start | bytes 208904 | tf_op jit(solution)/shard_map/ppermute | solution.py:24
  79.7 2.7 %collective-permute-start.22 = (f32[136,128]{1,0:T(8,128)S(1)}, f32[136,128]{1,0:T(8,128)S(1)}, u32[]{:S(2)}, u32[]{:S(2)}) collective-permute-start(f32[136,128]{1,0:T(8,128)S(1)} %get-tuple-element.11), channel_id=1, source_target_pairs={{0,224},{32,0},{64,32},{96,64},{128,96},{160,128},{192,160},{224,1... | collective-permute-start | bytes 208904 | tf_op jit(solution)/shard_map/ppermute | solution.py:24
  82.3 4.9 %all-to-all-start.2 = ((f32[16,128,128]{2,1,0:T(8,128)}), f32[16,128,128]{2,1,0:T(8,128)}, u32[]{:S(2)}, u32[]{:S(2)}) async-start(f32[16,128,128]{2,1,0:T(8,128)} %get-tuple-element.10), calls=%async_computation.2 | async-start | bytes 2097152 | tf_op jit(solution)/shard_map/all_to_all | solution.py:36
  87.3 0.1 collective-permute-start.23
  87.4 1.3 %collective-permute-start.25 = (f32[136,128]{1,0:T(8,128)S(1)}, f32[136,128]{1,0:T(8,128)S(1)}, u32[]{:S(2)}, u32[]{:S(2)}) collective-permute-start(f32[136,128]{1,0:T(8,128)S(1)} %collective-permute-done.19), channel_id=1, source_target_pairs={{0,64},{32,96},{64,128},{96,160},{128,192},{160,224},{192,0},{224,... | collective-permute-start | bytes 208904 | tf_op jit(solution)/shard_map/ppermute | solution.py:24
  88.8 1.4 %collective-permute-start.24 = (f32[136,128]{1,0:T(8,128)S(1)}, f32[136,128]{1,0:T(8,128)S(1)}, u32[]{:S(2)}, u32[]{:S(2)}) collective-permute-start(f32[136,128]{1,0:T(8,128)S(1)} %collective-permute-done.20), channel_id=1, source_target_pairs={{0,224},{32,0},{64,32},{96,64},{128,96},{160,128},{192,160},{224,1... | collective-permute-start | bytes 208904 | tf_op jit(solution)/shard_map/ppermute | solution.py:24
  90.3 1.5 %collective-permute-done.23 = f32[136,128]{1,0:T(8,128)S(1)} collective-permute-done((f32[136,128]{1,0:T(8,128)S(1)}, f32[136,128]{1,0:T(8,128)S(1)}, u32[]{:S(2)}, u32[]{:S(2)}) %collective-permute-start.23) | collective-permute-done | bytes 69664 | tf_op jit(solution)/shard_map/ppermute | solution.py:24
  91.8 1.4 %collective-permute-done.24 = f32[136,128]{1,0:T(8,128)S(1)} collective-permute-done((f32[136,128]{1,0:T(8,128)S(1)}, f32[136,128]{1,0:T(8,128)S(1)}, u32[]{:S(2)}, u32[]{:S(2)}) %collective-permute-start.24) | collective-permute-done | bytes 69664 | tf_op jit(solution)/shard_map/ppermute | solution.py:24
  93.3 5.4 %collective-permute-start.26 = (f32[8,136,128]{2,1,0:T(8,128)S(1)}, f32[8,136,128]{2,1,0:T(8,128)S(1)}, u32[]{:S(2)}, u32[]{:S(2)}) collective-permute-start(f32[8,136,128]{2,1,0:T(8,128)S(1)} %bitcast_dynamic-update-slice_fusion), channel_id=1, source_target_pairs={{0,1},{1,0},{2,3},{3,2},{4,5},{5,4},{6,7},{7,6},{8,9},{9,8},{10,11... | collective-permute-start | bytes 1671176 | tf_op jit(solution)/shard_map/ppermute | solution.py:28
  98.6 3.3 %collective-permute-start.27 = (f32[128,128]{1,0:T(8,128)S(1)}, f32[128,128]{1,0:T(8,128)S(1)}, u32[]{:S(2)}, u32[]{:S(2)}) collective-permute-start(f32[128,128]{1,0:T(8,128)S(1)} %get-tuple-element.9.stat), channel_id=1, source_target_pairs={{0,0},{1,16},{16,1},{17,17},{2,2},{3,18},{18,3},{19,19},{4,4},{5,2... | collective-permute-start | bytes 196616 | tf_op jit(solution)/shard_map/ppermute | solution.py:32
  101.9 0.1 pad_maximum_fusion.square_column
  102.0 2.6 %collective-permute-done.27.home = f32[128,128]{1,0:T(8,128)S(1)} collective-permute-done((f32[128,128]{1,0:T(8,128)S(1)}, f32[128,128]{1,0:T(8,128)S(1)}, u32[]{:S(2)}, u32[]{:S(2)}) %collective-permute-start.27) | collective-permute-done | bytes 65568 | tf_op jit(solution)/shard_map/ppermute | solution.py:32
  104.6 2.7 %shard_map.43 = (f32[128,128]{1,0:T(8,128)S(1)}, f32[128,128]{1,0:T(8,128)}) custom-call(f32[16,128,128]{2,1,0:T(8,128)} %all-to-all-done.2.square_row, f32[16,128,128]{2,1,0:T(8,128)S(1)} %all-to-all-done.1.row_ref.stat_row, f32[16,136,128]{2,1,0:T(8,128)S(1)} %pad_maximum_fusion.square_column, ...), custom_call_target="tpu_custom_call" | custom-call | tf_op jit(solution)/shard_map/pallas_call | solution.py:170
  107.3 3.5 %collective-permute-start.28 = (f32[128,128]{1,0:T(8,128)S(1)}, f32[128,128]{1,0:T(8,128)S(1)}, u32[]{:S(2)}, u32[]{:S(2)}) collective-permute-start(f32[128,128]{1,0:T(8,128)S(1)} %get-tuple-element.13), channel_id=1, source_target_pairs={{0,0},{1,16},{16,1},{17,17},{2,2},{3,18},{18,3},{19,19},{4,4},{5,2... | collective-permute-start | bytes 196616 | tf_op jit(solution)/shard_map/ppermute | solution.py:32
  110.8 2.1 %collective-permute-done.28 = f32[128,128]{1,0:T(8,128)S(1)} collective-permute-done((f32[128,128]{1,0:T(8,128)S(1)}, f32[128,128]{1,0:T(8,128)S(1)}, u32[]{:S(2)}, u32[]{:S(2)}) %collective-permute-start.28) | collective-permute-done | bytes 65568 | tf_op jit(solution)/shard_map/ppermute | solution.py:32
  112.9 0.6 copy.30
  (54 shorter events, 0.4 us)
Async XLA Ops:
  0.6 32.4 %collective-permute-start = (f32[32,128]{1,0:T(8,128)}, f32[32,128]{1,0:T(8,128)S(1)}, u32[]{:S(2)}, u32[]{:S(2)}) collective-permute-start(f32[32,128]{1,0:T(8,128)} %bitcast.66), channel_id=1, source_target_pairs={{0,16},{16,0},{1,17},{17,1},{2,18},{18,2},{3,19},{19,3},{4,20},{20... | collective-permute-start | bytes 49160 | tf_op jit(solution)/shard_map/ppermute | solution.py:28
  2.7 10.6 %collective-permute-start.1 = (f32[32,128]{1,0:T(8,128)}, f32[32,128]{1,0:T(8,128)S(1)}, u32[]{:S(2)}, u32[]{:S(2)}) collective-permute-start(f32[32,128]{1,0:T(8,128)} %bitcast.67), channel_id=1, source_target_pairs={{10,0},{11,1},{44,2},{45,3},{76,4},{77,5},{98,6},{99,7},{136,8},{1... | collective-permute-start | bytes 49160 | tf_op jit(solution)/shard_map/ppermute | solution.py:73
  9.7 29.7 %collective-permute-start.10 = (f32[128,128]{1,0:T(8,128)}, f32[128,128]{1,0:T(8,128)S(1)}, u32[]{:S(2)}, u32[]{:S(2)}) collective-permute-start(f32[128,128]{1,0:T(8,128)} %param.3), channel_id=1, source_target_pairs={{0,0},{1,16},{16,1},{17,17},{2,2},{3,18},{18,3},{19,19},{4,4},{5,2... | collective-permute-start | bytes 196616 | tf_op jit(solution)/shard_map/ppermute | solution.py:32
  13.3 4.8 %collective-permute-start.2 = (f32[32,128]{1,0:T(8,128)S(1)}, f32[32,128]{1,0:T(8,128)S(1)}, u32[]{:S(2)}, u32[]{:S(2)}) collective-permute-start(f32[32,128]{1,0:T(8,128)S(1)} %collective-permute-done.1), channel_id=1, source_target_pairs={{0,64},{32,96},{64,128},{96,160},{128,192},{160,224},{192,0},{224,... | collective-permute-start | bytes 49160 | tf_op jit(solution)/shard_map/ppermute | solution.py:24
  15.1 5.2 %collective-permute-start.3 = (f32[32,128]{1,0:T(8,128)S(1)}, f32[32,128]{1,0:T(8,128)S(1)}, u32[]{:S(2)}, u32[]{:S(2)}) collective-permute-start(f32[32,128]{1,0:T(8,128)S(1)} %collective-permute-done.1), channel_id=1, source_target_pairs={{0,192},{32,224},{64,0},{96,32},{128,64},{160,96},{192,128},{224,1... | collective-permute-start | bytes 49160 | tf_op jit(solution)/shard_map/ppermute | solution.py:24
  17.0 3.8 %collective-permute-start.4 = (f32[32,128]{1,0:T(8,128)S(1)}, f32[32,128]{1,0:T(8,128)S(1)}, u32[]{:S(2)}, u32[]{:S(2)}) collective-permute-start(f32[32,128]{1,0:T(8,128)S(1)} %collective-permute-done.1), channel_id=1, source_target_pairs={{0,32},{32,64},{64,96},{96,128},{128,160},{160,192},{192,224},{224... | collective-permute-start | bytes 49160 | tf_op jit(solution)/shard_map/ppermute | solution.py:24
  18.1 4.9 %collective-permute-start.5 = (f32[32,128]{1,0:T(8,128)S(1)}, f32[32,128]{1,0:T(8,128)S(1)}, u32[]{:S(2)}, u32[]{:S(2)}) collective-permute-start(f32[32,128]{1,0:T(8,128)S(1)} %collective-permute-done.1), channel_id=1, source_target_pairs={{0,224},{32,0},{64,32},{96,64},{128,96},{160,128},{192,160},{224,1... | collective-permute-start | bytes 49160 | tf_op jit(solution)/shard_map/ppermute | solution.py:24
  20.3 3.8 %collective-permute-start.6 = (f32[32,128]{1,0:T(8,128)S(1)}, f32[32,128]{1,0:T(8,128)S(1)}, u32[]{:S(2)}, u32[]{:S(2)}) collective-permute-start(f32[32,128]{1,0:T(8,128)S(1)} %collective-permute-done.2), channel_id=1, source_target_pairs={{0,32},{32,64},{64,96},{96,128},{128,160},{160,192},{192,224},{224... | collective-permute-start | bytes 49160 | tf_op jit(solution)/shard_map/ppermute | solution.py:24
  20.8 3.4 %collective-permute-start.7 = (f32[32,128]{1,0:T(8,128)S(1)}, f32[32,128]{1,0:T(8,128)S(1)}, u32[]{:S(2)}, u32[]{:S(2)}) collective-permute-start(f32[32,128]{1,0:T(8,128)S(1)} %collective-permute-done.3), channel_id=1, source_target_pairs={{0,224},{32,0},{64,32},{96,64},{128,96},{160,128},{192,160},{224,1... | collective-permute-start | bytes 49160 | tf_op jit(solution)/shard_map/ppermute | solution.py:24
  23.0 4.9 %collective-permute-start.8 = (f32[32,128]{1,0:T(8,128)S(1)}, f32[32,128]{1,0:T(8,128)S(1)}, u32[]{:S(2)}, u32[]{:S(2)}) collective-permute-start(f32[32,128]{1,0:T(8,128)S(1)} %collective-permute-done.2), channel_id=1, source_target_pairs={{0,64},{32,96},{64,128},{96,160},{128,192},{160,224},{192,0},{224,... | collective-permute-start | bytes 49160 | tf_op jit(solution)/shard_map/ppermute | solution.py:24
  27.9 11.4 %collective-permute-start.9 = (f32[8,32,128]{2,1,0:T(8,128)S(1)}, f32[8,32,128]{2,1,0:T(8,128)S(1)}, u32[]{:S(2)}, u32[]{:S(2)}) collective-permute-start(f32[8,32,128]{2,1,0:T(8,128)S(1)} %bitcast_dynamic-update-slice_fusion.16), channel_id=1, source_target_pairs={{0,1},{1,0},{2,3},{3,2},{4,5},{5,4},{6,7},{7,6},{8,9},{9,8},{10,11... | collective-permute-start | bytes 393224 | tf_op jit(solution)/shard_map/ppermute | solution.py:28
  34.5 13.5 %all-to-all-start = ((f32[16,32,128]{2,1,0:T(8,128)}), f32[16,32,128]{2,1,0:T(8,128)S(1)}, u32[]{:S(2)}, u32[]{:S(2)}) async-start(f32[16,32,128]{2,1,0:T(8,128)} %bitcast.3), calls=%async_computation | async-start | bytes 524288 | tf_op jit(solution)/shard_map/all_to_all | solution.py:82
  49.5 10.0 %collective-permute-start.11 = (f32[128,128]{1,0:T(8,128)S(1)}, f32[128,128]{1,0:T(8,128)S(1)}, u32[]{:S(2)}, u32[]{:S(2)}) collective-permute-start(f32[128,128]{1,0:T(8,128)S(1)} %get-tuple-element.9.stat), channel_id=1, source_target_pairs={{0,64},{32,96},{64,128},{96,160},{128,192},{160,224},{192,0},{224,... | collective-permute-start | bytes 196616 | tf_op jit(solution)/shard_map/ppermute | solution.py:24
  49.5 11.6 %collective-permute-start.12 = (f32[128,128]{1,0:T(8,128)S(1)}, f32[128,128]{1,0:T(8,128)S(1)}, u32[]{:S(2)}, u32[]{:S(2)}) collective-permute-start(f32[128,128]{1,0:T(8,128)S(1)} %get-tuple-element.9.stat), channel_id=1, source_target_pairs={{0,192},{32,224},{64,0},{96,32},{128,64},{160,96},{192,128},{224,1... | collective-permute-start | bytes 196616 | tf_op jit(solution)/shard_map/ppermute | solution.py:24
  53.1 9.4 %collective-permute-start.13 = (f32[128,128]{1,0:T(8,128)S(1)}, f32[128,128]{1,0:T(8,128)S(1)}, u32[]{:S(2)}, u32[]{:S(2)}) collective-permute-start(f32[128,128]{1,0:T(8,128)S(1)} %get-tuple-element.9.stat), channel_id=1, source_target_pairs={{0,32},{32,64},{64,96},{96,128},{128,160},{160,192},{192,224},{224... | collective-permute-start | bytes 196616 | tf_op jit(solution)/shard_map/ppermute | solution.py:24
  53.1 9.4 %collective-permute-start.14 = (f32[128,128]{1,0:T(8,128)S(1)}, f32[128,128]{1,0:T(8,128)S(1)}, u32[]{:S(2)}, u32[]{:S(2)}) collective-permute-start(f32[128,128]{1,0:T(8,128)S(1)} %get-tuple-element.9.stat), channel_id=1, source_target_pairs={{0,224},{32,0},{64,32},{96,64},{128,96},{160,128},{192,160},{224,1... | collective-permute-start | bytes 196616 | tf_op jit(solution)/shard_map/ppermute | solution.py:24
  55.7 18.7 %all-to-all-start.1 = ((f32[16,128,128]{2,1,0:T(8,128)}), f32[16,128,128]{2,1,0:T(8,128)S(1)}, u32[]{:S(2)}, u32[]{:S(2)}) async-start(f32[16,128,128]{2,1,0:T(8,128)} %get-tuple-element.8), calls=%async_computation.1 | async-start | bytes 2097152 | tf_op jit(solution)/shard_map/all_to_all | solution.py:36
  59.5 4.6 %collective-permute-start.15 = (f32[128,128]{1,0:T(8,128)S(1)}, f32[128,128]{1,0:T(8,128)S(1)}, u32[]{:S(2)}, u32[]{:S(2)}) collective-permute-start(f32[128,128]{1,0:T(8,128)S(1)} %collective-permute-done.11), channel_id=1, source_target_pairs={{0,32},{32,64},{64,96},{96,128},{128,160},{160,192},{192,224},{224... | collective-permute-start | bytes 196616 | tf_op jit(solution)/shard_map/ppermute | solution.py:24
  59.8 5.8 %collective-permute-start.17 = (f32[128,128]{1,0:T(8,128)S(1)}, f32[128,128]{1,0:T(8,128)S(1)}, u32[]{:S(2)}, u32[]{:S(2)}) collective-permute-start(f32[128,128]{1,0:T(8,128)S(1)} %collective-permute-done.11), channel_id=1, source_target_pairs={{0,64},{32,96},{64,128},{96,160},{128,192},{160,224},{192,0},{224,... | collective-permute-start | bytes 196616 | tf_op jit(solution)/shard_map/ppermute | solution.py:24
  61.1 4.3 %collective-permute-start.16 = (f32[128,128]{1,0:T(8,128)S(1)}, f32[128,128]{1,0:T(8,128)S(1)}, u32[]{:S(2)}, u32[]{:S(2)}) collective-permute-start(f32[128,128]{1,0:T(8,128)S(1)} %collective-permute-done.12), channel_id=1, source_target_pairs={{0,224},{32,0},{64,32},{96,64},{128,96},{160,128},{192,160},{224,1... | collective-permute-start | bytes 196616 | tf_op jit(solution)/shard_map/ppermute | solution.py:24
  65.5 5.1 %collective-permute-start.18 = (f32[8,128,128]{2,1,0:T(8,128)S(1)}, f32[8,128,128]{2,1,0:T(8,128)S(1)}, u32[]{:S(2)}, u32[]{:S(2)}) collective-permute-start(f32[8,128,128]{2,1,0:T(8,128)S(1)} %bitcast_dynamic-update-slice_fusion.8), channel_id=1, source_target_pairs={{0,1},{1,0},{2,3},{3,2},{4,5},{5,4},{6,7},{7,6},{8,9},{9,8},{10,11... | collective-permute-start | bytes 1572872 | tf_op jit(solution)/shard_map/ppermute | solution.py:28
  76.1 11.2 %collective-permute-start.19 = (f32[136,128]{1,0:T(8,128)S(1)}, f32[136,128]{1,0:T(8,128)S(1)}, u32[]{:S(2)}, u32[]{:S(2)}) collective-permute-start(f32[136,128]{1,0:T(8,128)S(1)} %get-tuple-element.11), channel_id=1, source_target_pairs={{0,64},{32,96},{64,128},{96,160},{128,192},{160,224},{192,0},{224,... | collective-permute-start | bytes 208904 | tf_op jit(solution)/shard_map/ppermute | solution.py:24
  76.1 12.7 %collective-permute-start.20 = (f32[136,128]{1,0:T(8,128)S(1)}, f32[136,128]{1,0:T(8,128)S(1)}, u32[]{:S(2)}, u32[]{:S(2)}) collective-permute-start(f32[136,128]{1,0:T(8,128)S(1)} %get-tuple-element.11), channel_id=1, source_target_pairs={{0,192},{32,224},{64,0},{96,32},{128,64},{160,96},{192,128},{224,1... | collective-permute-start | bytes 208904 | tf_op jit(solution)/shard_map/ppermute | solution.py:24
  79.7 10.5 %collective-permute-start.21 = (f32[136,128]{1,0:T(8,128)S(1)}, f32[136,128]{1,0:T(8,128)S(1)}, u32[]{:S(2)}, u32[]{:S(2)}) collective-permute-start(f32[136,128]{1,0:T(8,128)S(1)} %get-tuple-element.11), channel_id=1, source_target_pairs={{0,32},{32,64},{64,96},{96,128},{128,160},{160,192},{192,224},{224... | collective-permute-start | bytes 208904 | tf_op jit(solution)/shard_map/ppermute | solution.py:24
  79.7 10.6 %collective-permute-start.22 = (f32[136,128]{1,0:T(8,128)S(1)}, f32[136,128]{1,0:T(8,128)S(1)}, u32[]{:S(2)}, u32[]{:S(2)}) collective-permute-start(f32[136,128]{1,0:T(8,128)S(1)} %get-tuple-element.11), channel_id=1, source_target_pairs={{0,224},{32,0},{64,32},{96,64},{128,96},{160,128},{192,160},{224,1... | collective-permute-start | bytes 208904 | tf_op jit(solution)/shard_map/ppermute | solution.py:24
  82.3 22.3 %all-to-all-start.2 = ((f32[16,128,128]{2,1,0:T(8,128)}), f32[16,128,128]{2,1,0:T(8,128)}, u32[]{:S(2)}, u32[]{:S(2)}) async-start(f32[16,128,128]{2,1,0:T(8,128)} %get-tuple-element.10), calls=%async_computation.2 | async-start | bytes 2097152 | tf_op jit(solution)/shard_map/all_to_all | solution.py:36
  87.3 4.4 %collective-permute-start.23 = (f32[136,128]{1,0:T(8,128)S(1)}, f32[136,128]{1,0:T(8,128)S(1)}, u32[]{:S(2)}, u32[]{:S(2)}) collective-permute-start(f32[136,128]{1,0:T(8,128)S(1)} %collective-permute-done.19), channel_id=1, source_target_pairs={{0,32},{32,64},{64,96},{96,128},{128,160},{160,192},{192,224},{224... | collective-permute-start | bytes 208904 | tf_op jit(solution)/shard_map/ppermute | solution.py:24
  87.4 5.8 %collective-permute-start.25 = (f32[136,128]{1,0:T(8,128)S(1)}, f32[136,128]{1,0:T(8,128)S(1)}, u32[]{:S(2)}, u32[]{:S(2)}) collective-permute-start(f32[136,128]{1,0:T(8,128)S(1)} %collective-permute-done.19), channel_id=1, source_target_pairs={{0,64},{32,96},{64,128},{96,160},{128,192},{160,224},{192,0},{224,... | collective-permute-start | bytes 208904 | tf_op jit(solution)/shard_map/ppermute | solution.py:24
  88.8 4.5 %collective-permute-start.24 = (f32[136,128]{1,0:T(8,128)S(1)}, f32[136,128]{1,0:T(8,128)S(1)}, u32[]{:S(2)}, u32[]{:S(2)}) collective-permute-start(f32[136,128]{1,0:T(8,128)S(1)} %collective-permute-done.20), channel_id=1, source_target_pairs={{0,224},{32,0},{64,32},{96,64},{128,96},{160,128},{192,160},{224,1... | collective-permute-start | bytes 208904 | tf_op jit(solution)/shard_map/ppermute | solution.py:24
  93.3 8.6 %collective-permute-start.26 = (f32[8,136,128]{2,1,0:T(8,128)S(1)}, f32[8,136,128]{2,1,0:T(8,128)S(1)}, u32[]{:S(2)}, u32[]{:S(2)}) collective-permute-start(f32[8,136,128]{2,1,0:T(8,128)S(1)} %bitcast_dynamic-update-slice_fusion), channel_id=1, source_target_pairs={{0,1},{1,0},{2,3},{3,2},{4,5},{5,4},{6,7},{7,6},{8,9},{9,8},{10,11... | collective-permute-start | bytes 1671176 | tf_op jit(solution)/shard_map/ppermute | solution.py:28
  98.6 6.0 %collective-permute-start.27 = (f32[128,128]{1,0:T(8,128)S(1)}, f32[128,128]{1,0:T(8,128)S(1)}, u32[]{:S(2)}, u32[]{:S(2)}) collective-permute-start(f32[128,128]{1,0:T(8,128)S(1)} %get-tuple-element.9.stat), channel_id=1, source_target_pairs={{0,0},{1,16},{16,1},{17,17},{2,2},{3,18},{18,3},{19,19},{4,4},{5,2... | collective-permute-start | bytes 196616 | tf_op jit(solution)/shard_map/ppermute | solution.py:32
  107.3 5.6 %collective-permute-start.28 = (f32[128,128]{1,0:T(8,128)S(1)}, f32[128,128]{1,0:T(8,128)S(1)}, u32[]{:S(2)}, u32[]{:S(2)}) collective-permute-start(f32[128,128]{1,0:T(8,128)S(1)} %get-tuple-element.13), channel_id=1, source_target_pairs={{0,0},{1,16},{16,1},{17,17},{2,2},{3,18},{18,3},{19,19},{4,4},{5,2... | collective-permute-start | bytes 196616 | tf_op jit(solution)/shard_map/ppermute | solution.py:32
